TPU v7x, 1024 devices: a whole 4x4x32 slice. The times are simulated.
1024 devices in a mesh: dp: 32 (over z_hi, y, core), expert: 32 (over z_lo, x).
Axes of the slice: x: 4, y: 4, z: 32 (z_hi: 4, z_lo: 8; z = z_hi * 8 + z_lo), core: 2. Of those that a mesh axis runs over, the one named last changes fastest.
Arguments:
- hidden: bfloat16 [262144, 768], P(('dp', 'expert')), may hold values from -6 to 6
- w_down: bfloat16 [32, 768, 2048], P('expert', 'dp'), may hold values from -0.21875 to 0.21875
- expert_ids: int32 [32768, 4], P(('dp', 'expert')), may hold values from 0 to 31, all different within a row; in each aligned block of 32 rows (0 to 31, 32 to 63, ...) at most 8 rows name the same one
- gates: float32 [32768, 4], P(('dp', 'expert')), may hold values from 0.05 to 1
- cotangent: bfloat16 [32768, 2048], P(('dp', 'expert')), may hold values from -6 to 6
Outputs:
- mixed: bfloat16 [32768, 2048], P(('dp', 'expert'))
- gate_grads: float32 [32768, 4], P(('dp', 'expert'))
- hidden_grads: bfloat16 [262144, 768], P(('dp', 'expert'))
- weight_grads: bfloat16 [32, 768, 2048], P('expert', 'dp')
Inputs may be any that keep to these rules, and one draw needn't show every extreme that they name: `expert_ids`: each row names 4 different experts. Among the rows of one device no expert is named more than 8 times, a bound that some block reaches.
All inputs are finite; a program needn't handle non-finite values.
Results may differ from a plain program's by a relative error of at most 0.015.
Values may be sent and summed in bfloat16 or wider, within the bound.
No kernel may reach another device: no remote copies, remote signals or barrier semaphores. Data moves between devices by JAX's collectives and lax.ppermute only.
A program may use at most 32 MiB of HBM per device.

v0:
```python
import jax
import jax.numpy as jnp
from jax import lax
from jax.sharding import Mesh
from jax.sharding import PartitionSpec as P

DP = ("dp_0", "dp_1", "dp_2")
DP_EXPERT = ("dp_0", "dp_1", "dp_2", "expert")


def split_up(shard, dim, count):
    shape = shard.shape
    blocks = shard.reshape(*shape[:dim], count, shape[dim] // count, *shape[dim + 1 :])
    return jnp.moveaxis(blocks, dim, 0)


def scatter_pairs(shard, chips, core, dim):
    sizes = (lax.axis_size(chips), lax.axis_size(core))
    blocks = split_up(shard, dim, sizes[0] * sizes[1])
    inside = blocks.shape[1:]
    blocks = blocks.reshape(*sizes, *inside).swapaxes(0, 1).reshape(-1, *inside)
    blocks = lax.psum_scatter(blocks, core, scatter_dimension=0, tiled=True)
    return lax.psum_scatter(blocks, chips, scatter_dimension=0, tiled=True)[0]


def slot_table(expert_ids, experts, capacity):
    flat_ids = expert_ids.reshape(-1)
    choose = (flat_ids[:, None] == jnp.arange(experts, dtype=jnp.int32)[None, :]).astype(jnp.int32)
    earlier = jnp.cumsum(choose, axis=0) - choose
    position = jnp.sum(earlier * choose, axis=1)
    target = flat_ids * capacity + position
    return (target[None, :] == jnp.arange(experts * capacity, dtype=jnp.int32)[:, None]).astype(
        jnp.bfloat16
    )


def send_grads(placer, gates, cotangent, experts, capacity):
    width = cotangent.shape[1]
    scaled = gates[:, :, None] * cotangent.astype(jnp.float32)[:, None, :]
    routed = scaled.astype(jnp.bfloat16).reshape(-1, width)
    packed = jnp.dot(placer, routed, preferred_element_type=jnp.float32).astype(jnp.bfloat16)
    packed = packed.reshape(experts, capacity, width)
    arrived = lax.all_to_all(packed, "expert", split_axis=0, concat_axis=0, tiled=True)
    return arrived.reshape(experts * capacity, width)


def per_device(hidden, w_down, expert_ids, gates, cotangent):
    experts = lax.axis_size("expert")
    capacity = hidden.shape[0] // experts
    width = cotangent.shape[1]
    tok_count = expert_ids.shape[0]
    top_count = expert_ids.shape[1]
    weight_rows = w_down.reshape(w_down.shape[1], width)
    placer = slot_table(expert_ids, experts, capacity)
    full_weight = lax.all_gather(weight_rows, DP, axis=0, tiled=True)
    outputs = jnp.dot(hidden, full_weight, preferred_element_type=jnp.float32)
    packed_out = outputs.astype(jnp.bfloat16).reshape(experts, capacity, width)
    returned = lax.all_to_all(packed_out, "expert", split_axis=0, concat_axis=0, tiled=True)
    picked = lax.dot_general(
        placer,
        returned.reshape(experts * capacity, width),
        (((0,), (0,)), ((), ())),
        preferred_element_type=jnp.float32,
    )
    picked = picked.reshape(tok_count, top_count, width)
    mixed = jnp.sum(gates[:, :, None] * picked, axis=1).astype(jnp.bfloat16)
    gate_grads = jnp.sum(picked * cotangent.astype(jnp.float32)[:, None, :], axis=2)
    grads_in = send_grads(placer, gates, cotangent, experts, capacity)
    hidden_grads = lax.dot_general(
        grads_in, full_weight, (((1,), (1,)), ((), ())), preferred_element_type=jnp.float32
    ).astype(jnp.bfloat16)
    partial_sum = lax.dot_general(
        hidden, grads_in, (((0,), (0,)), ((), ())), preferred_element_type=jnp.float32
    )
    rounded = lax.optimization_barrier(partial_sum.astype(jnp.bfloat16))
    weight_sums = scatter_pairs(
        rounded.astype(jnp.float32).astype(jnp.bfloat16), ("dp_0", "dp_1"), "dp_2", 0
    ).astype(jnp.float32)
    weight_grads = weight_sums.astype(jnp.bfloat16).reshape(1, weight_rows.shape[0], width)
    return (mixed, gate_grads, hidden_grads, weight_grads)


def solution(mesh):
    torus = Mesh(
        mesh.devices.reshape(4, 4, 2, mesh.shape["expert"]), ("dp_0", "dp_1", "dp_2", "expert")
    )
    return jax.shard_map(
        per_device,
        mesh=torus,
        in_specs=(
            P(DP_EXPERT, None),
            P("expert", DP, None),
            P(DP_EXPERT, None),
            P(DP_EXPERT, None),
            P(DP_EXPERT, None),
        ),
        out_specs=(
            P(DP_EXPERT, None),
            P(DP_EXPERT, None),
            P(DP_EXPERT, None),
            P("expert", DP, None),
        ),
        check_vma=False,
    )
```

profile of v0, /device:TPU:1, one launch (start us, length us, event | category | flops | bytes accessed | tf_op | source)
XLA Modules:
  0.0 400.1 jit_solution(4007200619533505715)
XLA Ops:
  8.0 0.0 copy-start
  8.0 0.8 copy.30
  8.8 0.1 reshape.64
  8.9 0.8 copy.32
  9.7 0.1 mul.59
  9.8 0.1 fusion.24
  9.9 0.2 reduce_window_sum.11
  10.1 0.2 select_reduce_fusion
  10.3 1.1 mul.55.clone
  11.4 0.4 mul.61
  11.8 1.5 fusion.11
  13.3 16.0 %all-to-all-start.1 = ((bf16[32,8,2048]{2,1,0:T(8,128)(2,1)}), bf16[32,8,2048]{2,1,0:T(8,128)(2,1)}, u32[]{:S(2)}, u32[]{:S(2)}) async-start(bf16[32,8,2048]{2,1,0:T(8,128)(2,1)} %fusion.11), calls=%async_computation.1 | async-start | bytes 2097152 | tf_op jit(solution)/shard_map/all_to_all | solution.py:43
  29.3 0.0 all-gather.3.cloned.1.call-start
  29.4 0.7 all-gather.3.cloned.1.call-update
  30.0 0.0 reduce-scatter.3.cloned.1.call-start
  30.1 53.0 %all-to-all-done.1 = bf16[32,8,2048]{2,1,0:T(8,128)(2,1)} async-done(((bf16[32,8,2048]{2,1,0:T(8,128)(2,1)}), bf16[32,8,2048]{2,1,0:T(8,128)(2,1)}, u32[]{:S(2)}, u32[]{:S(2)}) %all-to-all-start.1) | async-done | bytes 1048608 | tf_op jit(solution)/shard_map/all_to_all | solution.py:43
  83.1 2.3 fusion.4
  85.3 3.0 copy.34
  88.3 4.0 %copy.35 = bf16[2,16,24,2048]{3,2,1,0:T(8,128)(2,1)} copy(bf16[2,16,24,2048]{3,2,0,1:T(8,128)(2,1)} %bitcast.41) | data formatting | bytes 6291456 | tf_op jit(solution)/shard_map/transpose | solution.py:21
  92.3 0.0 reduce-scatter.3.cloned.1.call-update
  92.4 103.0 %all-gather.3.cloned.1.call-done = bf16[1,768,2048]{2,1,0:T(8,128)(2,1)} async-done(((bf16[1,24,2048]{2,1,0:T(8,128)(2,1)}), bf16[1,768,2048]{2,1,0:T(8,128)(2,1)}) %all-gather.3.cloned.1.call-update) | async-done | bytes 3145744 | tf_op jit(solution)/shard_map/all_gather | solution.py:55
  195.4 3.9 fusion.8
  199.3 5.1 %all-to-all-start = ((bf16[32,8,2048]{2,1,0:T(8,128)(2,1)}), bf16[32,8,2048]{2,1,0:T(8,128)(2,1)S(1)}, u32[]{:S(2)}, u32[]{:S(2)}) async-start(bf16[32,8,2048]{2,1,0:T(8,128)(2,1)} %fusion.8), calls=%async_computation | async-start | bytes 2097152 | tf_op jit(solution)/shard_map/all_to_all | solution.py:58
  204.4 0.0 reduce-scatter.5.cloned.1.call-start
  204.4 0.0 reduce-scatter.3.cloned.1.call-done
  204.5 0.5 reduce-scatter.5.cloned.1.call-update
  205.0 0.1 reduce_sum.30
  205.1 0.1 copy.31
  205.2 4.0 fusion.12
  209.2 61.8 %all-to-all-done = bf16[32,8,2048]{2,1,0:T(8,128)(2,1)S(1)} async-done(((bf16[32,8,2048]{2,1,0:T(8,128)(2,1)}), bf16[32,8,2048]{2,1,0:T(8,128)(2,1)S(1)}, u32[]{:S(2)}, u32[]{:S(2)}) %all-to-all-start) | async-done | bytes 1048608 | tf_op jit(solution)/shard_map/all_to_all | solution.py:58
  271.0 1.1 multiply_reduce_fusion
  272.1 120.6 %reduce-scatter.5.cloned.1.call-done = bf16[1,24,2048]{2,1,0:T(8,128)(2,1)} async-done(((bf16[16,24,2048]{2,1,0:T(8,128)(2,1)}), bf16[1,24,2048]{2,1,0:T(8,128)(2,1)}) %reduce-scatter.5.cloned.1.call-update) | async-done | bytes 98320 | tf_op jit(solution)/shard_map/reduce_scatter | solution.py:23
  (10 shorter events, 0.0 us)
Async XLA Ops:
  8.0 75.1 %copy-start = (bf16[256,768]{1,0:T(8,128)(2,1)S(1)}, bf16[256,768]{1,0:T(8,128)(2,1)}, u32[]{:S(2)}) copy-start(bf16[256,768]{1,0:T(8,128)(2,1)} %param.5) | copy-start | bytes 1179652
  13.3 69.8 %all-to-all-start.1 = ((bf16[32,8,2048]{2,1,0:T(8,128)(2,1)}), bf16[32,8,2048]{2,1,0:T(8,128)(2,1)}, u32[]{:S(2)}, u32[]{:S(2)}) async-start(bf16[32,8,2048]{2,1,0:T(8,128)(2,1)} %fusion.11), calls=%async_computation.1 | async-start | bytes 2097152 | tf_op jit(solution)/shard_map/all_to_all | solution.py:43
  29.3 166.0 %all-gather.3.cloned.1.call-start = ((), (), s32[]{:S(2)}) async-start(), calls=%async_computation.6 | async-start | bytes 3244032 | tf_op jit(solution)/shard_map/all_gather | solution.py:55
  30.0 174.4 %reduce-scatter.3.cloned.1.call-start = ((), (), s32[]{:S(2)}) async-start(), calls=%async_computation.4 | async-start | bytes 4718592 | tf_op jit(solution)/shard_map/reduce_scatter | solution.py:22
  92.4 112.7 %copy-start.1 = (bf16[32,2048]{1,0:T(8,128)(2,1)S(1)}, bf16[32,2048]{1,0:T(8,128)(2,1)}, u32[]{:S(2)}) copy-start(bf16[32,2048]{1,0:T(8,128)(2,1)} %param.9) | copy-start | bytes 393220
  199.3 5.9 %copy-start.2 = (s32[32,4]{0,1:T(4,128)S(1)}, s32[32,4]{0,1:T(4,128)}, u32[]{:S(2)}) copy-start(s32[32,4]{0,1:T(4,128)} %param.7) | copy-start | bytes 1540
  199.3 71.7 %all-to-all-start = ((bf16[32,8,2048]{2,1,0:T(8,128)(2,1)}), bf16[32,8,2048]{2,1,0:T(8,128)(2,1)S(1)}, u32[]{:S(2)}, u32[]{:S(2)}) async-start(bf16[32,8,2048]{2,1,0:T(8,128)(2,1)} %fusion.8), calls=%async_computation | async-start | bytes 2097152 | tf_op jit(solution)/shard_map/all_to_all | solution.py:58
  204.4 188.3 %reduce-scatter.5.cloned.1.call-start = ((), (), s32[]{:S(2)}) async-start(), calls=%async_computation.5 | async-start | bytes 1671168 | tf_op jit(solution)/shard_map/reduce_scatter | solution.py:23
  205.0 66.0 %copy-start.3 = (f32[32,4]{0,1:T(4,128)S(1)}, f32[32,4]{0,1:T(4,128)}, u32[]{:S(2)}) copy-start(f32[32,4]{0,1:T(4,128)} %param.8) | copy-start | bytes 1540
Sparse Core Ops, SparseCore 0:
  34.4 160.8 all-gather.2
Sparse Core Ops, SparseCore 1:
  92.4 43.3 reduce-scatter.2
  210.7 181.9 reduce-scatter.4
where the time goes:
time: 401 us; the launch traced here: 400 us
  waiting for transfers between devices  340 us (85%)
  starting transfers between devices  21.3 us (5%)
  between operations  15.6 us (4%)
  matrix products  12.8 us (3%)
  local copies, waits for them, and re-layouts  10.5 us (3%)
    reduce_scatter x1, waiting for transfers between devices, scatter_pairs(): return lax.psum_scatter(blocks, chips, scatter_dimension=0, tiled=True)[0]  121 us
    all_gather x1, waiting for transfers between devices, per_device(): full_weight = lax.all_gather(weight_rows, DP, axis=0, tiled=True)  103 us
    all_to_all x1, waiting for transfers between devices, per_device(): lax.all_to_all(packed_out, 'expert', split_axis=0, concat_axis=0, tiled=T...  61.8 us
    all_to_all x1, waiting for transfers between devices, send_grads(): lax.all_to_all(packed, 'expert', split_axis=0, concat_axis=0, tiled=True)  53 us
    all_to_all x1, starting transfers between devices, send_grads(): lax.all_to_all(packed, 'expert', split_axis=0, concat_axis=0, tiled=True)  16 us
  transfers between devices with their start and end apart: 5, of which 4 were waited for; matrix products, arithmetic and copies ran while one was open for 5% of the time, Pallas kernels for 0%

commit v1 on v0

v1 whole, which is shorter than its diff:
```python
import jax
import jax.numpy as jnp
from jax import lax
from jax.sharding import Mesh
from jax.sharding import PartitionSpec as P


ZH, Y, CORE, HALF, GRP = "zh", "y", "core", "half", "grp"
DP = (ZH, Y, CORE)
ALL = (ZH, Y, CORE, HALF, GRP)
N_ZH, N_Y, N_CORE, N_HALF = 4, 4, 2, 2
RING = 4
RIGHT = [(i, (i + 1) % RING) for i in range(RING)]
LEFT = [(i, (i - 1) % RING) for i in range(RING)]
SWAP = [(0, 1), (1, 0)]
F32, BF16 = jnp.float32, jnp.bfloat16


def dot(a, b, dims):
    return lax.dot_general(a, b, (dims, ((), ())), preferred_element_type=F32)


def exchange(rows, axis):
    return lax.all_to_all(rows, axis, split_axis=0, concat_axis=0, tiled=True)


def slots_of(ids, gates, cotangent, first_expert, experts, capacity):
    tokens, top = ids.shape
    line = jnp.arange(experts * capacity, dtype=jnp.int32)[:, None]
    expert = first_expert + line // capacity
    same = [expert == ids[:, k][None, :] for k in range(top)]
    named = same[0]
    gate = jnp.where(same[0], gates[:, 0][None, :], 0.0)
    for k in range(1, top):
        named = named | same[k]
        gate = jnp.where(same[k], gates[:, k][None, :], gate)
    order = jnp.arange(tokens, dtype=jnp.int32)
    before = (order[:, None] < order[None, :]).astype(BF16)
    earlier = dot(named.astype(BF16), before, ((1,), (0,)))
    fills = named & (earlier == (line % capacity).astype(F32))
    slot_gate = jnp.sum(jnp.where(fills, gate, 0.0), axis=1, keepdims=True)
    rows = dot(fills.astype(BF16), cotangent, ((1,), (0,)))
    return fills, same, slot_gate, rows


def combine(returned, fills, same, slot_gate, rows):
    weight = jnp.where(fills, slot_gate, 0.0)
    high = lax.reduce_precision(weight, 8, 7)
    low = (weight - high).astype(BF16)
    mixed = dot(high.astype(BF16), returned, ((0,), (0,))) + dot(low, returned, ((0,), (0,)))
    inner = jnp.sum(returned.astype(F32) * rows.astype(F32), axis=1, keepdims=True)
    spread = jnp.where(fills, inner, 0.0)
    grads = jnp.stack([jnp.sum(jnp.where(s, spread, 0.0), axis=0) for s in same], axis=0)
    return mixed, grads


def gather_ring(own, axis):
    here = lax.axis_index(axis)
    half = own.shape[-1] // 2
    below = lax.ppermute(own, axis, RIGHT)
    above = lax.ppermute(own, axis, LEFT)
    far_a = lax.ppermute(below[..., :half], axis, RIGHT)
    far_b = lax.ppermute(above[..., half:], axis, LEFT)
    blocks = jnp.zeros((RING, *own.shape), own.dtype)
    zeros = (0,) * (own.ndim - 1)
    for step, block, column in (
        (0, own, 0),
        (3, below, 0),
        (1, above, 0),
        (2, far_a, 0),
        (2, far_b, half),
    ):
        blocks = lax.dynamic_update_slice(blocks, block[None], ((here + step) & 3, *zeros, column))
    return blocks


def scatter_ring(blocks, axis):
    here = lax.axis_index(axis)
    half = blocks.shape[-1] // 2

    def block(step):
        return lax.dynamic_index_in_dim(blocks, (here + step) & 3, 0, keepdims=False)

    far = block(2).astype(BF16)
    got_a = lax.ppermute(far[..., :half], axis, RIGHT)
    got_b = lax.ppermute(far[..., half:], axis, LEFT)
    up, down = block(1).astype(F32), block(3).astype(F32)
    up = jnp.concatenate([up[..., :half] + got_a.astype(F32), up[..., half:]], axis=-1)
    down = jnp.concatenate([down[..., :half], down[..., half:] + got_b.astype(F32)], axis=-1)
    from_below = lax.ppermute(up.astype(BF16), axis, RIGHT)
    from_above = lax.ppermute(down.astype(BF16), axis, LEFT)
    return block(0).astype(F32) + from_below.astype(F32) + from_above.astype(F32)


def per_device(hidden, w_down, ids, gates, cotangent):
    groups = lax.axis_size(GRP)
    slots, inner = hidden.shape
    capacity = slots // (N_HALF * groups)
    half_slots = slots // 2
    rows, width = w_down.shape[1:]
    core, half = lax.axis_index(CORE), lax.axis_index(HALF)
    part = inner // 2

    pair = jnp.concatenate([ids.astype(F32), gates], axis=1)
    pair_p = lax.ppermute(pair, HALF, SWAP)
    cot_p = lax.ppermute(cotangent, HALF, SWAP)
    top = ids.shape[1]
    ids_p, gates_p = pair_p[:, :top].astype(jnp.int32), pair_p[:, top:]

    wz = gather_ring(w_down.reshape(rows, width), ZH)

    first = half * groups
    fills, same, slot_gate, mine = slots_of(ids, gates, cotangent, first, groups, capacity)
    sent = (slot_gate * mine).astype(BF16).reshape(groups, capacity, width)
    grads_own = exchange(sent, GRP)

    wy = gather_ring(wz.reshape(N_ZH * rows, width), Y).reshape(part, width)
    w_other = lax.ppermute(wy, CORE, SWAP)

    fills_p, same_p, slot_gate_p, mine_p = slots_of(ids_p, gates_p, cot_p, first, groups, capacity)
    sent_p = (slot_gate_p * mine_p).astype(BF16).reshape(groups, capacity, width)
    sent_p, grads_own = lax.optimization_barrier((sent_p, grads_own))
    grads_par = exchange(sent_p, GRP)

    hid_own = lax.dynamic_slice_in_dim(hidden, half * half_slots, half_slots, 0)
    hid_par = lax.dynamic_slice_in_dim(hidden, (1 - half) * half_slots, half_slots, 0)
    hid_t = jnp.concatenate([hid_own, hid_par], axis=0).T
    hid_t = hid_t.reshape(N_ZH, N_Y, N_CORE, rows, slots).transpose(2, 1, 0, 3, 4)
    hid_t = hid_t.reshape(N_CORE, part, slots)
    hid_self = lax.dynamic_index_in_dim(hid_t, core, 0, keepdims=False)
    hid_other = lax.dynamic_index_in_dim(hid_t, 1 - core, 0, keepdims=False)
    hid_self, hid_other = lax.optimization_barrier((hid_self, hid_other))

    def project(lo, hi):
        out = dot(hid_self[:, lo:hi], wy, ((0,), (0,))) + dot(hid_other[:, lo:hi], w_other, ((0,), (0,)))
        return out.astype(BF16).reshape(groups, capacity, width)

    out_par, grads_par = lax.optimization_barrier((project(half_slots, slots), grads_par))
    back_par = exchange(out_par, GRP)
    out_own, back_par = lax.optimization_barrier((project(0, half_slots), back_par))
    back_own = exchange(out_own, GRP).reshape(half_slots, width)
    back_par = back_par.reshape(half_slots, width)
    mixed_p, gg_p = combine(back_par, fills_p, same_p, slot_gate_p, mine_p)
    mixed_r = lax.ppermute(mixed_p.astype(BF16), HALF, SWAP)
    gg_r = lax.ppermute(gg_p, HALF, SWAP)
    mixed_o, gg_o = combine(back_own, fills, same, slot_gate, mine)
    mixed = (mixed_o + mixed_r.astype(F32)).astype(BF16)
    gate_grads = (gg_o + gg_r).T

    grads = jnp.concatenate(
        [grads_own.reshape(half_slots, width), grads_par.reshape(half_slots, width)], axis=0
    )
    for_other = dot(hid_other, grads, ((1,), (0,))).astype(BF16)
    got = lax.ppermute(for_other, CORE, SWAP)
    kept = dot(hid_self, grads, ((1,), (0,))) + got.astype(F32)
    by_y = scatter_ring(kept.reshape(RING, N_ZH * rows, width), Y)
    sums = scatter_ring(by_y.reshape(RING, rows, width), ZH)
    weight_grads = sums.astype(BF16).reshape(1, rows, width)

    hg_self = dot(wy, grads, ((1,), (1,))).astype(BF16)
    hg_other = dot(w_other, grads, ((1,), (1,))).astype(BF16)
    low = jnp.where(core == 0, hg_self, hg_other)
    high = jnp.where(core == 0, hg_other, hg_self)
    hg = jnp.stack([low, high]).reshape(N_CORE, N_Y, N_ZH, rows, slots)
    hg = hg.transpose(2, 1, 0, 3, 4).reshape(inner, slots).T
    hidden_grads = jnp.where(half == 0, hg, jnp.roll(hg, half_slots, axis=0))
    return mixed, gate_grads, hidden_grads, weight_grads


def solution(mesh):
    groups = mesh.shape["expert"] // N_HALF
    torus = Mesh(mesh.devices.reshape(N_ZH, N_Y, N_CORE, N_HALF, groups), ALL)
    spread = P(ALL, None)
    weights = P((HALF, GRP), DP, None)

    return jax.shard_map(
        per_device,
        mesh=torus,
        in_specs=(spread, weights, spread, spread, spread),
        out_specs=(spread, spread, spread, weights),
        check_vma=False,
    )
```

time: 401 us -> 259 us (0.65)
  the two profiles are of different devices: /device:TPU:1 before, /device:TPU:4 now
where the time goes in v1:
time: 259 us; the launch traced here: 257 us
  starting transfers between devices  163 us (63%)
  waiting for transfers between devices  46.5 us (18%)
  matrix products  21.5 us (8%)
  local copies, waits for them, and re-layouts  13 us (5%)
  other arithmetic  11.4 us (4%)
    all_to_all x4, starting transfers between devices, exchange(): return lax.all_to_all(rows, axis, split_axis=0, concat_axis=0, tiled=True)  49.3 us
    dot_general x16, matrix products, dot(): return lax.dot_general(a, b, (dims, ((), ())), preferred_element_type=F32)  21.5 us
    ppermute x2, waiting for transfers between devices, gather_ring(): below = lax.ppermute(own, axis, RIGHT)  15.4 us
    ppermute x2, starting transfers between devices, gather_ring(): far_b = lax.ppermute(above[..., half:], axis, LEFT)  15.3 us
    ppermute x2, starting transfers between devices, gather_ring(): below = lax.ppermute(own, axis, RIGHT)  13.1 us
    ppermute x2, starting transfers between devices, scatter_ring(): from_above = lax.ppermute(down.astype(BF16), axis, LEFT)  11.7 us
    ppermute x2, starting transfers between devices, scatter_ring(): got_b = lax.ppermute(far[..., half:], axis, LEFT)  11.5 us
    ppermute x2, starting transfers between devices, scatter_ring(): got_a = lax.ppermute(far[..., :half], axis, RIGHT)  10.6 us
  transfers between devices with their start and end apart: 26, of which 11 were waited for; matrix products, arithmetic and copies ran while one was open for 15% of the time, Pallas kernels for 0%

profile of v1, /device:TPU:4, one launch (start us, length us, event | category | flops | bytes accessed | tf_op | source)
XLA Modules:
  0.0 257.0 jit_solution(7290998246430351817)
XLA Ops:
  2.0 9.1 %collective-permute-start.9 = (f32[32,8]{0,1:T(8,128)S(1)}, f32[32,8]{0,1:T(8,128)S(1)}, u32[]{:S(2)}, u32[]{:S(2)}) collective-permute-start(f32[32,8]{0,1:T(8,128)S(1)} %pad_maximum_fusion.7), channel_id=1, source_target_pairs={{0,16},{16,0},{1,17},{17,1},{2,18},{18,2},{3,19},{19,3},{4,20},{20... | collective-permute-start | bytes 3080 | tf_op jit(solution)/shard_map/ppermute | solution.py:105
  15.7 15.0 %all-to-all-start = ((bf16[16,8,2048]{2,1,0:T(8,128)(2,1)}), bf16[16,8,2048]{2,1,0:T(8,128)(2,1)S(1)}, u32[]{:S(2)}, u32[]{:S(2)}) async-start(bf16[16,8,2048]{2,1,0:T(8,128)(2,1)} %fusion.9), calls=%async_computation | async-start | bytes 1048576 | tf_op jit(solution)/shard_map/all_to_all | solution.py:24
  30.7 9.6 %collective-permute-start = (bf16[24,2048]{1,0:T(8,128)(2,1)S(1)}, bf16[24,2048]{1,0:T(8,128)(2,1)S(1)}, u32[]{:S(2)}, u32[]{:S(2)}) collective-permute-start(bf16[24,2048]{1,0:T(8,128)(2,1)S(1)} %bitcast.172), channel_id=1, source_target_pairs={{0,256},{256,512},{512,768},{768,0},{1,257},{257,513},{513,769},{7... | collective-permute-start | bytes 294920 | tf_op jit(solution)/shard_map/ppermute | solution.py:60
  40.3 5.0 %collective-permute-start.1 = (bf16[24,2048]{1,0:T(8,128)(2,1)S(1)}, bf16[24,2048]{1,0:T(8,128)(2,1)S(1)}, u32[]{:S(2)}, u32[]{:S(2)}) collective-permute-start(bf16[24,2048]{1,0:T(8,128)(2,1)S(1)} %bitcast.173), channel_id=1, source_target_pairs={{0,768},{256,0},{512,256},{768,512},{1,769},{257,1},{513,257},{769... | collective-permute-start | bytes 294920 | tf_op jit(solution)/shard_map/ppermute | solution.py:61
  45.4 4.5 %collective-permute-start.10 = (bf16[32,2048]{1,0:T(8,128)(2,1)S(1)}, bf16[32,2048]{1,0:T(8,128)(2,1)S(1)}, u32[]{:S(2)}, u32[]{:S(2)}) collective-permute-start(bf16[32,2048]{1,0:T(8,128)(2,1)S(1)} %copy-done.8), channel_id=1, source_target_pairs={{0,16},{16,0},{1,17},{17,1},{2,18},{18,2},{3,19},{19,3},{4,20},{20... | collective-permute-start | bytes 393224 | tf_op jit(solution)/shard_map/ppermute | solution.py:106
  50.0 9.6 %collective-permute-done = bf16[24,2048]{1,0:T(8,128)(2,1)S(1)} collective-permute-done((bf16[24,2048]{1,0:T(8,128)(2,1)S(1)}, bf16[24,2048]{1,0:T(8,128)(2,1)S(1)}, u32[]{:S(2)}, u32[]{:S(2)}) %collective-permute-start) | collective-permute-done | bytes 98336 | tf_op jit(solution)/shard_map/ppermute | solution.py:60
  59.6 3.0 %collective-permute-start.2 = (bf16[24,1024]{1,0:T(8,128)(2,1)S(1)}, bf16[24,1024]{1,0:T(8,128)(2,1)S(1)}, u32[]{:S(2)}, u32[]{:S(2)}) collective-permute-start(bf16[24,1024]{1,0:T(8,128)(2,1)S(1)} %slice.167), channel_id=1, source_target_pairs={{0,256},{256,512},{512,768},{768,0},{1,257},{257,513},{513,769},{7... | collective-permute-start | bytes 147464 | tf_op jit(solution)/shard_map/ppermute | solution.py:62
  63.7 10.5 %collective-permute-start.3 = (bf16[24,1024]{1,0:T(8,128)(2,1)S(1)}, bf16[24,1024]{1,0:T(8,128)(2,1)S(1)}, u32[]{:S(2)}, u32[]{:S(2)}) collective-permute-start(bf16[24,1024]{1,0:T(8,128)(2,1)S(1)} %slice.168), channel_id=1, source_target_pairs={{0,768},{256,0},{512,256},{768,512},{1,769},{257,1},{513,257},{769... | collective-permute-start | bytes 147464 | tf_op jit(solution)/shard_map/ppermute | solution.py:63
  74.2 2.9 %collective-permute-done.10 = bf16[32,2048]{1,0:T(8,128)(2,1)S(1)} collective-permute-done((bf16[32,2048]{1,0:T(8,128)(2,1)S(1)}, bf16[32,2048]{1,0:T(8,128)(2,1)S(1)}, u32[]{:S(2)}, u32[]{:S(2)}) %collective-permute-start.10) | collective-permute-done | bytes 131104 | tf_op jit(solution)/shard_map/ppermute | solution.py:106
  79.4 19.2 %all-to-all-start.1 = ((bf16[16,8,2048]{2,1,0:T(8,128)(2,1)}), bf16[16,8,2048]{2,1,0:T(8,128)(2,1)S(1)}, u32[]{:S(2)}, u32[]{:S(2)}) async-start(bf16[16,8,2048]{2,1,0:T(8,128)(2,1)} %fusion.8), calls=%async_computation.1 | async-start | bytes 1048576 | tf_op jit(solution)/shard_map/all_to_all | solution.py:24
  98.7 3.5 %collective-permute-start.4 = (bf16[96,2048]{1,0:T(8,128)(2,1)S(1)}, bf16[96,2048]{1,0:T(8,128)(2,1)}, u32[]{:S(2)}, u32[]{:S(2)}) collective-permute-start(bf16[96,2048]{1,0:T(8,128)(2,1)S(1)} %bitcast.167), channel_id=1, source_target_pairs={{0,64},{64,128},{128,192},{192,0},{1,65},{65,129},{129,193},{193,1... | collective-permute-start | bytes 1179656 | tf_op jit(solution)/shard_map/ppermute | solution.py:60
  102.2 3.6 %collective-permute-start.5 = (bf16[96,2048]{1,0:T(8,128)(2,1)S(1)}, bf16[96,2048]{1,0:T(8,128)(2,1)}, u32[]{:S(2)}, u32[]{:S(2)}) collective-permute-start(bf16[96,2048]{1,0:T(8,128)(2,1)S(1)} %bitcast.168), channel_id=1, source_target_pairs={{0,192},{64,0},{128,64},{192,128},{1,193},{65,1},{129,65},{193,129... | collective-permute-start | bytes 1179656 | tf_op jit(solution)/shard_map/ppermute | solution.py:61
  106.0 5.8 %collective-permute-done.4 = bf16[96,2048]{1,0:T(8,128)(2,1)} collective-permute-done((bf16[96,2048]{1,0:T(8,128)(2,1)S(1)}, bf16[96,2048]{1,0:T(8,128)(2,1)}, u32[]{:S(2)}, u32[]{:S(2)}) %collective-permute-start.4) | collective-permute-done | bytes 393248 | tf_op jit(solution)/shard_map/ppermute | solution.py:60
  112.7 2.3 collective-permute-start.6
  116.0 4.8 %collective-permute-start.7 = (bf16[96,1024]{1,0:T(8,128)(2,1)S(1)}, bf16[96,1024]{1,0:T(8,128)(2,1)S(1)}, u32[]{:S(2)}, u32[]{:S(2)}) collective-permute-start(bf16[96,1024]{1,0:T(8,128)(2,1)S(1)} %slice.170), channel_id=1, source_target_pairs={{0,192},{64,0},{128,64},{192,128},{1,193},{65,1},{129,65},{193,129... | collective-permute-start | bytes 589832 | tf_op jit(solution)/shard_map/ppermute | solution.py:63
  134.7 7.5 %all-to-all-start.2 = ((bf16[16,8,2048]{2,1,0:T(8,128)(2,1)}), bf16[16,8,2048]{2,1,0:T(8,128)(2,1)S(1)}, u32[]{:S(2)}, u32[]{:S(2)}) async-start(bf16[16,8,2048]{2,1,0:T(8,128)(2,1)} %fusion.2), calls=%async_computation.2 | async-start | bytes 1048576 | tf_op jit(solution)/shard_map/all_to_all | solution.py:24
  142.2 2.9 %convolution_convert_fusion = bf16[384,2048]{1,0:T(8,128)(2,1)} fusion(bf16[384,256]{1,0:T(8,128)(2,1)S(1)} %get-tuple-element.13, bf16[128,2048]{1,0:T(8,128)(2,1)} %bitcast.157, bf16[128,2048]{1,0:T(8,128)(2,1)} %bitcast.153), kind=kOutput, calls=%fused_computation.1 | convolution fusion | flops 405536768 | bytes 2818048 | tf_op jit(solution)/shard_map/dot_general | solution.py:20
  150.3 2.8 %convolution_convert_fusion.1 = bf16[384,256]{1,0:T(8,128)(2,1)} fusion(bf16[384,2048]{1,0:T(8,128)(2,1)} %collective-permute-done.8, bf16[128,2048]{1,0:T(8,128)(2,1)S(1)} %bitcast.159, bf16[128,2048]{1,0:T(8,128)(2,1)S(1)} %bitcast.155), kind=kOutput, calls=%fused_computation.11 | convolution fusion | flops 404848640 | bytes 2818048 | tf_op jit(solution)/shard_map/dot_general | solution.py:20
  155.2 5.6 %collective-permute-start.16 = (bf16[96,1024]{1,0:T(8,128)(2,1)S(1)}, bf16[96,1024]{1,0:T(8,128)(2,1)S(1)}, u32[]{:S(2)}, u32[]{:S(2)}) collective-permute-start(bf16[96,1024]{1,0:T(8,128)(2,1)S(1)} %get-tuple-element.43), channel_id=1, source_target_pairs={{0,192},{64,0},{128,64},{192,128},{1,193},{65,1},{129,65},{193,129... | collective-permute-start | bytes 589832 | tf_op jit(solution)/shard_map/ppermute | solution.py:86
  162.9 2.7 %collective-permute-done.16 = bf16[96,1024]{1,0:T(8,128)(2,1)S(1)} collective-permute-done((bf16[96,1024]{1,0:T(8,128)(2,1)S(1)}, bf16[96,1024]{1,0:T(8,128)(2,1)S(1)}, u32[]{:S(2)}, u32[]{:S(2)}) %collective-permute-start.16) | collective-permute-done | bytes 196640 | tf_op jit(solution)/shard_map/ppermute | solution.py:86
  166.4 5.6 %collective-permute-start.17 = (bf16[96,2048]{1,0:T(8,128)(2,1)}, bf16[96,2048]{1,0:T(8,128)(2,1)S(1)}, u32[]{:S(2)}, u32[]{:S(2)}) collective-permute-start(bf16[96,2048]{1,0:T(8,128)(2,1)} %pad_maximum_fusion.4), channel_id=1, source_target_pairs={{0,192},{64,0},{128,64},{192,128},{1,193},{65,1},{129,65},{193,129... | collective-permute-start | bytes 1179656 | tf_op jit(solution)/shard_map/ppermute | solution.py:91
  174.8 7.5 %all-to-all-start.3 = ((bf16[16,8,2048]{2,1,0:T(8,128)(2,1)}), bf16[16,8,2048]{2,1,0:T(8,128)(2,1)}, u32[]{:S(2)}, u32[]{:S(2)}) async-start(bf16[16,8,2048]{2,1,0:T(8,128)(2,1)} %fusion.3), calls=%async_computation.3 | async-start | bytes 1048576 | tf_op jit(solution)/shard_map/all_to_all | solution.py:24
  184.3 2.4 collective-permute-done.15
  188.1 5.8 %collective-permute-start.20 = (bf16[24,1024]{1,0:T(8,128)(2,1)S(1)}, bf16[24,1024]{1,0:T(8,128)(2,1)S(1)}, u32[]{:S(2)}, u32[]{:S(2)}) collective-permute-start(bf16[24,1024]{1,0:T(8,128)(2,1)S(1)} %get-tuple-element.53), channel_id=1, source_target_pairs={{0,768},{256,0},{512,256},{768,512},{1,769},{257,1},{513,257},{769... | collective-permute-start | bytes 147464 | tf_op jit(solution)/shard_map/ppermute | solution.py:86
  194.0 8.7 %collective-permute-start.18 = (bf16[24,1024]{1,0:T(8,128)(2,1)S(1)}, bf16[24,1024]{1,0:T(8,128)(2,1)S(1)}, u32[]{:S(2)}, u32[]{:S(2)}) collective-permute-start(bf16[24,1024]{1,0:T(8,128)(2,1)S(1)} %get-tuple-element.52), channel_id=1, source_target_pairs={{0,256},{256,512},{512,768},{768,0},{1,257},{257,513},{513,769},{7... | collective-permute-start | bytes 147464 | tf_op jit(solution)/shard_map/ppermute | solution.py:85
  202.7 3.3 %collective-permute-done.20 = bf16[24,1024]{1,0:T(8,128)(2,1)S(1)} collective-permute-done((bf16[24,1024]{1,0:T(8,128)(2,1)S(1)}, bf16[24,1024]{1,0:T(8,128)(2,1)S(1)}, u32[]{:S(2)}, u32[]{:S(2)}) %collective-permute-start.20) | collective-permute-done | bytes 49184 | tf_op jit(solution)/shard_map/ppermute | solution.py:86
  206.0 6.1 %collective-permute-start.21 = (bf16[24,2048]{1,0:T(8,128)(2,1)S(1)}, bf16[24,2048]{1,0:T(8,128)(2,1)S(1)}, u32[]{:S(2)}, u32[]{:S(2)}) collective-permute-start(bf16[24,2048]{1,0:T(8,128)(2,1)S(1)} %pad_maximum_fusion.6), channel_id=1, source_target_pairs={{0,768},{256,0},{512,256},{768,512},{1,769},{257,1},{513,257},{769... | collective-permute-start | bytes 294920 | tf_op jit(solution)/shard_map/ppermute | solution.py:91
  212.2 8.5 %collective-permute-start.19 = (bf16[24,2048]{1,0:T(8,128)(2,1)S(1)}, bf16[24,2048]{1,0:T(8,128)(2,1)S(1)}, u32[]{:S(2)}, u32[]{:S(2)}) collective-permute-start(bf16[24,2048]{1,0:T(8,128)(2,1)S(1)} %pad_maximum_fusion.5), channel_id=1, source_target_pairs={{0,256},{256,512},{512,768},{768,0},{1,257},{257,513},{513,769},{7... | collective-permute-start | bytes 294920 | tf_op jit(solution)/shard_map/ppermute | solution.py:90
  221.7 6.4 %collective-permute-done.21 = bf16[24,2048]{1,0:T(8,128)(2,1)S(1)} collective-permute-done((bf16[24,2048]{1,0:T(8,128)(2,1)S(1)}, bf16[24,2048]{1,0:T(8,128)(2,1)S(1)}, u32[]{:S(2)}, u32[]{:S(2)}) %collective-permute-start.21) | collective-permute-done | bytes 98336 | tf_op jit(solution)/shard_map/ppermute | solution.py:91
  228.1 4.9 %collective-permute-done.19 = bf16[24,2048]{1,0:T(8,128)(2,1)S(1)} collective-permute-done((bf16[24,2048]{1,0:T(8,128)(2,1)S(1)}, bf16[24,2048]{1,0:T(8,128)(2,1)S(1)}, u32[]{:S(2)}, u32[]{:S(2)}) %collective-permute-start.19) | collective-permute-done | bytes 98336 | tf_op jit(solution)/shard_map/ppermute | solution.py:90
  239.0 7.8 %collective-permute-start.12 = (f32[4,32]{1,0:T(4,128)S(1)}, f32[4,32]{1,0:T(4,128)S(1)}, u32[]{:S(2)}, u32[]{:S(2)}) collective-permute-start(f32[4,32]{1,0:T(4,128)S(1)} %pad_maximum_fusion.8), channel_id=1, source_target_pairs={{0,16},{16,0},{1,17},{17,1},{2,18},{18,2},{3,19},{19,3},{4,20},{20... | collective-permute-start | bytes 1544 | tf_op jit(solution)/shard_map/ppermute | solution.py:145
  248.0 6.5 %collective-permute-done.11 = bf16[32,2048]{1,0:T(8,128)(2,1)S(1)} collective-permute-done((bf16[32,2048]{1,0:T(8,128)(2,1)S(1)}, bf16[32,2048]{1,0:T(8,128)(2,1)S(1)}, u32[]{:S(2)}, u32[]{:S(2)}) %collective-permute-start.11) | collective-permute-done | bytes 131104 | tf_op jit(solution)/shard_map/ppermute | solution.py:144
  (155 shorter events, 51.9 us)
Async XLA Ops:
  2.0 10.8 %collective-permute-start.9 = (f32[32,8]{0,1:T(8,128)S(1)}, f32[32,8]{0,1:T(8,128)S(1)}, u32[]{:S(2)}, u32[]{:S(2)}) collective-permute-start(f32[32,8]{0,1:T(8,128)S(1)} %pad_maximum_fusion.7), channel_id=1, source_target_pairs={{0,16},{16,0},{1,17},{17,1},{2,18},{18,2},{3,19},{19,3},{4,20},{20... | collective-permute-start | bytes 3080 | tf_op jit(solution)/shard_map/ppermute | solution.py:105
  14.7 16.0 %copy-start.9 = (bf16[1,24,2048]{2,1,0:T(8,128)(2,1)S(1)}, bf16[1,24,2048]{2,1,0:T(8,128)(2,1)}, u32[]{:S(2)}) copy-start(bf16[1,24,2048]{2,1,0:T(8,128)(2,1)} %param.6) | copy-start | bytes 294916
  14.7 30.6 %copy-start.8 = (bf16[32,2048]{1,0:T(8,128)(2,1)S(1)}, bf16[32,2048]{1,0:T(8,128)(2,1)}, u32[]{:S(2)}) copy-start(bf16[32,2048]{1,0:T(8,128)(2,1)} %param.9) | copy-start | bytes 393220
  15.7 63.7 %all-to-all-start = ((bf16[16,8,2048]{2,1,0:T(8,128)(2,1)}), bf16[16,8,2048]{2,1,0:T(8,128)(2,1)S(1)}, u32[]{:S(2)}, u32[]{:S(2)}) async-start(bf16[16,8,2048]{2,1,0:T(8,128)(2,1)} %fusion.9), calls=%async_computation | async-start | bytes 1048576 | tf_op jit(solution)/shard_map/all_to_all | solution.py:24
  30.7 28.9 %collective-permute-start = (bf16[24,2048]{1,0:T(8,128)(2,1)S(1)}, bf16[24,2048]{1,0:T(8,128)(2,1)S(1)}, u32[]{:S(2)}, u32[]{:S(2)}) collective-permute-start(bf16[24,2048]{1,0:T(8,128)(2,1)S(1)} %bitcast.172), channel_id=1, source_target_pairs={{0,256},{256,512},{512,768},{768,0},{1,257},{257,513},{513,769},{7... | collective-permute-start | bytes 294920 | tf_op jit(solution)/shard_map/ppermute | solution.py:60
  40.3 23.3 %collective-permute-start.1 = (bf16[24,2048]{1,0:T(8,128)(2,1)S(1)}, bf16[24,2048]{1,0:T(8,128)(2,1)S(1)}, u32[]{:S(2)}, u32[]{:S(2)}) collective-permute-start(bf16[24,2048]{1,0:T(8,128)(2,1)S(1)} %bitcast.173), channel_id=1, source_target_pairs={{0,768},{256,0},{512,256},{768,512},{1,769},{257,1},{513,257},{769... | collective-permute-start | bytes 294920 | tf_op jit(solution)/shard_map/ppermute | solution.py:61
  45.4 31.7 %collective-permute-start.10 = (bf16[32,2048]{1,0:T(8,128)(2,1)S(1)}, bf16[32,2048]{1,0:T(8,128)(2,1)S(1)}, u32[]{:S(2)}, u32[]{:S(2)}) collective-permute-start(bf16[32,2048]{1,0:T(8,128)(2,1)S(1)} %copy-done.8), channel_id=1, source_target_pairs={{0,16},{16,0},{1,17},{17,1},{2,18},{18,2},{3,19},{19,3},{4,20},{20... | collective-permute-start | bytes 393224 | tf_op jit(solution)/shard_map/ppermute | solution.py:106
  59.6 19.8 %collective-permute-start.2 = (bf16[24,1024]{1,0:T(8,128)(2,1)S(1)}, bf16[24,1024]{1,0:T(8,128)(2,1)S(1)}, u32[]{:S(2)}, u32[]{:S(2)}) collective-permute-start(bf16[24,1024]{1,0:T(8,128)(2,1)S(1)} %slice.167), channel_id=1, source_target_pairs={{0,256},{256,512},{512,768},{768,0},{1,257},{257,513},{513,769},{7... | collective-permute-start | bytes 147464 | tf_op jit(solution)/shard_map/ppermute | solution.py:62
  63.7 35.0 %collective-permute-start.3 = (bf16[24,1024]{1,0:T(8,128)(2,1)S(1)}, bf16[24,1024]{1,0:T(8,128)(2,1)S(1)}, u32[]{:S(2)}, u32[]{:S(2)}) collective-permute-start(bf16[24,1024]{1,0:T(8,128)(2,1)S(1)} %slice.168), channel_id=1, source_target_pairs={{0,768},{256,0},{512,256},{768,512},{1,769},{257,1},{513,257},{769... | collective-permute-start | bytes 147464 | tf_op jit(solution)/shard_map/ppermute | solution.py:63
  79.4 26.4 %copy-start.3 = (bf16[16,8,2048]{2,1,0:T(8,128)(2,1)}, bf16[16,8,2048]{2,1,0:T(8,128)(2,1)S(1)}, u32[]{:S(2)}) copy-start(bf16[16,8,2048]{2,1,0:T(8,128)(2,1)S(1)} %all-to-all-done) | copy-start | bytes 1572868
  79.4 54.5 %all-to-all-start.1 = ((bf16[16,8,2048]{2,1,0:T(8,128)(2,1)}), bf16[16,8,2048]{2,1,0:T(8,128)(2,1)S(1)}, u32[]{:S(2)}, u32[]{:S(2)}) async-start(bf16[16,8,2048]{2,1,0:T(8,128)(2,1)} %fusion.8), calls=%async_computation.1 | async-start | bytes 1048576 | tf_op jit(solution)/shard_map/all_to_all | solution.py:24
  98.7 13.1 %collective-permute-start.4 = (bf16[96,2048]{1,0:T(8,128)(2,1)S(1)}, bf16[96,2048]{1,0:T(8,128)(2,1)}, u32[]{:S(2)}, u32[]{:S(2)}) collective-permute-start(bf16[96,2048]{1,0:T(8,128)(2,1)S(1)} %bitcast.167), channel_id=1, source_target_pairs={{0,64},{64,128},{128,192},{192,0},{1,65},{65,129},{129,193},{193,1... | collective-permute-start | bytes 1179656 | tf_op jit(solution)/shard_map/ppermute | solution.py:60
  102.2 12.8 %collective-permute-start.5 = (bf16[96,2048]{1,0:T(8,128)(2,1)S(1)}, bf16[96,2048]{1,0:T(8,128)(2,1)}, u32[]{:S(2)}, u32[]{:S(2)}) collective-permute-start(bf16[96,2048]{1,0:T(8,128)(2,1)S(1)} %bitcast.168), channel_id=1, source_target_pairs={{0,192},{64,0},{128,64},{192,128},{1,193},{65,1},{129,65},{193,129... | collective-permute-start | bytes 1179656 | tf_op jit(solution)/shard_map/ppermute | solution.py:61
  112.7 10.1 %collective-permute-start.6 = (bf16[96,1024]{1,0:T(8,128)(2,1)S(1)}, bf16[96,1024]{1,0:T(8,128)(2,1)S(1)}, u32[]{:S(2)}, u32[]{:S(2)}) collective-permute-start(bf16[96,1024]{1,0:T(8,128)(2,1)S(1)} %slice.169), channel_id=1, source_target_pairs={{0,64},{64,128},{128,192},{192,0},{1,65},{65,129},{129,193},{193,1... | collective-permute-start | bytes 589832 | tf_op jit(solution)/shard_map/ppermute | solution.py:62
  116.0 7.9 %collective-permute-start.7 = (bf16[96,1024]{1,0:T(8,128)(2,1)S(1)}, bf16[96,1024]{1,0:T(8,128)(2,1)S(1)}, u32[]{:S(2)}, u32[]{:S(2)}) collective-permute-start(bf16[96,1024]{1,0:T(8,128)(2,1)S(1)} %slice.170), channel_id=1, source_target_pairs={{0,192},{64,0},{128,64},{192,128},{1,193},{65,1},{129,65},{193,129... | collective-permute-start | bytes 589832 | tf_op jit(solution)/shard_map/ppermute | solution.py:63
  123.9 6.8 %collective-permute-start.8 = (bf16[384,2048]{1,0:T(8,128)(2,1)S(1)}, bf16[384,2048]{1,0:T(8,128)(2,1)}, u32[]{:S(2)}, u32[]{:S(2)}) collective-permute-start(bf16[384,2048]{1,0:T(8,128)(2,1)S(1)} %bitcast.146), channel_id=1, source_target_pairs={{0,32},{32,0},{1,33},{33,1},{2,34},{34,2},{3,35},{35,3},{4,36},{36... | collective-permute-start | bytes 4718600 | tf_op jit(solution)/shard_map/ppermute | solution.py:118
  134.7 40.1 %all-to-all-start.2 = ((bf16[16,8,2048]{2,1,0:T(8,128)(2,1)}), bf16[16,8,2048]{2,1,0:T(8,128)(2,1)S(1)}, u32[]{:S(2)}, u32[]{:S(2)}) async-start(bf16[16,8,2048]{2,1,0:T(8,128)(2,1)} %fusion.2), calls=%async_computation.2 | async-start | bytes 1048576 | tf_op jit(solution)/shard_map/all_to_all | solution.py:24
  145.1 7.9 %collective-permute-start.13 = (bf16[384,2048]{1,0:T(8,128)(2,1)}, bf16[384,2048]{1,0:T(8,128)(2,1)}, u32[]{:S(2)}, u32[]{:S(2)}) collective-permute-start(bf16[384,2048]{1,0:T(8,128)(2,1)} %convolution_convert_fusion), channel_id=1, source_target_pairs={{0,32},{32,0},{1,33},{33,1},{2,34},{34,2},{3,35},{35,3},{4,36},{36... | collective-permute-start | bytes 4718600 | tf_op jit(solution)/shard_map/ppermute | solution.py:154
  155.0 5.8 %copy-start = (f32[384,2048]{1,0:T(8,128)}, f32[384,2048]{1,0:T(8,128)S(1)}, u32[]{:S(2)}) copy-start(f32[384,2048]{1,0:T(8,128)S(1)} %convert_add_fusion) | copy-start | bytes 9437188
  155.2 10.4 %collective-permute-start.16 = (bf16[96,1024]{1,0:T(8,128)(2,1)S(1)}, bf16[96,1024]{1,0:T(8,128)(2,1)S(1)}, u32[]{:S(2)}, u32[]{:S(2)}) collective-permute-start(bf16[96,1024]{1,0:T(8,128)(2,1)S(1)} %get-tuple-element.43), channel_id=1, source_target_pairs={{0,192},{64,0},{128,64},{192,128},{1,193},{65,1},{129,65},{193,129... | collective-permute-start | bytes 589832 | tf_op jit(solution)/shard_map/ppermute | solution.py:86
  161.0 11.0 %collective-permute-start.14 = (bf16[96,1024]{1,0:T(8,128)(2,1)S(1)}, bf16[96,1024]{1,0:T(8,128)(2,1)S(1)}, u32[]{:S(2)}, u32[]{:S(2)}) collective-permute-start(bf16[96,1024]{1,0:T(8,128)(2,1)S(1)} %get-tuple-element.42), channel_id=1, source_target_pairs={{0,64},{64,128},{128,192},{192,0},{1,65},{65,129},{129,193},{193,1... | collective-permute-start | bytes 589832 | tf_op jit(solution)/shard_map/ppermute | solution.py:85
  166.4 17.9 %collective-permute-start.17 = (bf16[96,2048]{1,0:T(8,128)(2,1)}, bf16[96,2048]{1,0:T(8,128)(2,1)S(1)}, u32[]{:S(2)}, u32[]{:S(2)}) collective-permute-start(bf16[96,2048]{1,0:T(8,128)(2,1)} %pad_maximum_fusion.4), channel_id=1, source_target_pairs={{0,192},{64,0},{128,64},{192,128},{1,193},{65,1},{129,65},{193,129... | collective-permute-start | bytes 1179656 | tf_op jit(solution)/shard_map/ppermute | solution.py:91
  172.9 13.8 %collective-permute-start.15 = (bf16[96,2048]{1,0:T(8,128)(2,1)}, bf16[96,2048]{1,0:T(8,128)(2,1)}, u32[]{:S(2)}, u32[]{:S(2)}) collective-permute-start(bf16[96,2048]{1,0:T(8,128)(2,1)} %pad_maximum_fusion.3), channel_id=1, source_target_pairs={{0,64},{64,128},{128,192},{192,0},{1,65},{65,129},{129,193},{193,1... | collective-permute-start | bytes 1179656 | tf_op jit(solution)/shard_map/ppermute | solution.py:90
  174.8 62.5 %all-to-all-start.3 = ((bf16[16,8,2048]{2,1,0:T(8,128)(2,1)}), bf16[16,8,2048]{2,1,0:T(8,128)(2,1)}, u32[]{:S(2)}, u32[]{:S(2)}) async-start(bf16[16,8,2048]{2,1,0:T(8,128)(2,1)} %fusion.3), calls=%async_computation.3 | async-start | bytes 1048576 | tf_op jit(solution)/shard_map/all_to_all | solution.py:24
  188.0 32.6 %copy-start.7 = (f32[96,2048]{1,0:T(8,128)}, f32[96,2048]{1,0:T(8,128)S(1)}, u32[]{:S(2)}) copy-start(f32[96,2048]{1,0:T(8,128)S(1)} %fusion.7) | copy-start | bytes 2359300
  188.1 17.9 %collective-permute-start.20 = (bf16[24,1024]{1,0:T(8,128)(2,1)S(1)}, bf16[24,1024]{1,0:T(8,128)(2,1)S(1)}, u32[]{:S(2)}, u32[]{:S(2)}) collective-permute-start(bf16[24,1024]{1,0:T(8,128)(2,1)S(1)} %get-tuple-element.53), channel_id=1, source_target_pairs={{0,768},{256,0},{512,256},{768,512},{1,769},{257,1},{513,257},{769... | collective-permute-start | bytes 147464 | tf_op jit(solution)/shard_map/ppermute | solution.py:86
  194.0 18.1 %collective-permute-start.18 = (bf16[24,1024]{1,0:T(8,128)(2,1)S(1)}, bf16[24,1024]{1,0:T(8,128)(2,1)S(1)}, u32[]{:S(2)}, u32[]{:S(2)}) collective-permute-start(bf16[24,1024]{1,0:T(8,128)(2,1)S(1)} %get-tuple-element.52), channel_id=1, source_target_pairs={{0,256},{256,512},{512,768},{768,0},{1,257},{257,513},{513,769},{7... | collective-permute-start | bytes 147464 | tf_op jit(solution)/shard_map/ppermute | solution.py:85
  206.0 22.1 %collective-permute-start.21 = (bf16[24,2048]{1,0:T(8,128)(2,1)S(1)}, bf16[24,2048]{1,0:T(8,128)(2,1)S(1)}, u32[]{:S(2)}, u32[]{:S(2)}) collective-permute-start(bf16[24,2048]{1,0:T(8,128)(2,1)S(1)} %pad_maximum_fusion.6), channel_id=1, source_target_pairs={{0,768},{256,0},{512,256},{768,512},{1,769},{257,1},{513,257},{769... | collective-permute-start | bytes 294920 | tf_op jit(solution)/shard_map/ppermute | solution.py:91
  212.2 20.9 %collective-permute-start.19 = (bf16[24,2048]{1,0:T(8,128)(2,1)S(1)}, bf16[24,2048]{1,0:T(8,128)(2,1)S(1)}, u32[]{:S(2)}, u32[]{:S(2)}) collective-permute-start(bf16[24,2048]{1,0:T(8,128)(2,1)S(1)} %pad_maximum_fusion.5), channel_id=1, source_target_pairs={{0,256},{256,512},{512,768},{768,0},{1,257},{257,513},{513,769},{7... | collective-permute-start | bytes 294920 | tf_op jit(solution)/shard_map/ppermute | solution.py:90
  220.8 16.3 %copy-start.2 = (f32[128,2048]{1,0:T(8,128)S(1)}, f32[128,2048]{1,0:T(8,128)}, u32[]{:S(2)}) copy-start(f32[128,2048]{1,0:T(8,128)} %copy-done.1) | copy-start | bytes 3145732
  235.2 19.3 %collective-permute-start.11 = (bf16[32,2048]{1,0:T(8,128)(2,1)S(1)}, bf16[32,2048]{1,0:T(8,128)(2,1)S(1)}, u32[]{:S(2)}, u32[]{:S(2)}) collective-permute-start(bf16[32,2048]{1,0:T(8,128)(2,1)S(1)} %fusion.4), channel_id=1, source_target_pairs={{0,16},{16,0},{1,17},{17,1},{2,18},{18,2},{3,19},{19,3},{4,20},{20... | collective-permute-start | bytes 393224 | tf_op jit(solution)/shard_map/ppermute | solution.py:144
  239.0 17.5 %collective-permute-start.12 = (f32[4,32]{1,0:T(4,128)S(1)}, f32[4,32]{1,0:T(4,128)S(1)}, u32[]{:S(2)}, u32[]{:S(2)}) collective-permute-start(f32[4,32]{1,0:T(4,128)S(1)} %pad_maximum_fusion.8), channel_id=1, source_target_pairs={{0,16},{16,0},{1,17},{17,1},{2,18},{18,2},{3,19},{19,3},{4,20},{20... | collective-permute-start | bytes 1544 | tf_op jit(solution)/shard_map/ppermute | solution.py:145
  (22 other events, 40.9 us)

commit v2 on v1

v2 whole, which is shorter than its diff:
```python
import jax
import jax.numpy as jnp
from jax import lax
from jax.sharding import Mesh
from jax.sharding import PartitionSpec as P


ZH, Y, CORE, HALF, GRP = "zh", "y", "core", "half", "grp"
DP = (ZH, Y, CORE)
ALL = (ZH, Y, CORE, HALF, GRP)
N_ZH, N_Y, N_CORE, N_HALF = 4, 4, 2, 2
RING = 4
LANES = 128
RIGHT = [(i, (i + 1) % RING) for i in range(RING)]
LEFT = [(i, (i - 1) % RING) for i in range(RING)]
SWAP = [(0, 1), (1, 0)]
F32, BF16 = jnp.float32, jnp.bfloat16


def dot(a, b, dims):
    return lax.dot_general(a, b, (dims, ((), ())), preferred_element_type=F32)


def exchange(rows, axis):
    return lax.all_to_all(rows, axis, split_axis=0, concat_axis=0, tiled=True)


def slots_of(ids, gates, cotangent, first_expert, experts, capacity):
    top, tokens = ids.shape
    line = jnp.arange(N_HALF * experts * capacity, dtype=jnp.int32)[:, None]
    expert = first_expert + line // (N_HALF * capacity)
    order = jnp.arange(tokens, dtype=jnp.int32)
    source = order // (tokens // N_HALF)
    from_source = (line // capacity) % N_HALF == source[None, :]
    same = [(expert == ids[k][None, :]) & from_source for k in range(top)]
    named = same[0]
    gate = jnp.where(same[0], gates[0][None, :], 0.0)
    for k in range(1, top):
        named = named | same[k]
        gate = jnp.where(same[k], gates[k][None, :], gate)
    before = (order[:, None] < order[None, :]).astype(BF16)
    earlier = dot(named.astype(BF16), before, ((1,), (0,)))
    fills = named & (earlier == (line % capacity).astype(F32))
    slot_gate = jnp.sum(jnp.where(fills, gate, 0.0), axis=1, keepdims=True)
    rows = dot(fills.astype(BF16), cotangent, ((1,), (0,)))
    return fills, same, slot_gate, rows


def combine(returned, fills, same, slot_gate, rows):
    weight = jnp.where(fills, slot_gate, 0.0)
    high = lax.reduce_precision(weight, 8, 7)
    low = (weight - high).astype(BF16)
    mixed = dot(high.astype(BF16), returned, ((0,), (0,))) + dot(low, returned, ((0,), (0,)))
    inner = jnp.sum(returned.astype(F32) * rows.astype(F32), axis=1, keepdims=True)
    spread = jnp.where(fills, inner, 0.0)
    grads = jnp.stack([jnp.sum(jnp.where(s, spread, 0.0), axis=0) for s in same], axis=0)
    return mixed, grads


def pieces_of(value, count):
    found = []
    for _ in range(count):
        piece = lax.reduce_precision(value, 8, 7)
        found.append(piece.astype(BF16))
        value = value - piece
    return found


def beside(rows, columns):
    extra = jnp.concatenate(columns, axis=0).T
    extra = jnp.pad(extra, ((0, 0), (0, LANES - extra.shape[1])))
    return jnp.concatenate([rows, extra], axis=1)


def scatter_ring(blocks, dim, axis):
    here = lax.axis_index(axis)

    def block(step):
        return lax.dynamic_index_in_dim(blocks, (here + step) & 3, dim, keepdims=False)

    far = block(2).astype(BF16)
    cut = 0 if far.ndim == 3 else 1
    half = far.shape[cut] // 2
    low, high = (lambda v: lax.slice_in_dim(v, 0, half, axis=cut)), (
        lambda v: lax.slice_in_dim(v, half, 2 * half, axis=cut)
    )
    got_a = lax.ppermute(low(far), axis, RIGHT)
    got_b = lax.ppermute(high(far), axis, LEFT)
    up, down = block(1).astype(F32), block(3).astype(F32)
    up = jnp.concatenate([low(up) + got_a.astype(F32), high(up)], axis=cut)
    down = jnp.concatenate([low(down), high(down) + got_b.astype(F32)], axis=cut)
    from_below = lax.ppermute(up.astype(BF16), axis, RIGHT)
    from_above = lax.ppermute(down.astype(BF16), axis, LEFT)
    return block(0).astype(F32) + from_below.astype(F32) + from_above.astype(F32)


def gather(value, axis):
    return lax.all_gather(value, axis, axis=0, tiled=True)


def per_device(hidden, w_down, ids, gates, cotangent):
    groups = lax.axis_size(GRP)
    slots, inner = hidden.shape
    capacity = slots // (N_HALF * groups)
    tokens, top = ids.shape
    rows, width = w_down.shape[1:]
    core, half = lax.axis_index(CORE), lax.axis_index(HALF)
    piece = RING // 2 * RING * rows
    part = 2 * piece

    columns = [ids.T.astype(BF16), *pieces_of(gates.T, 3)]
    sent_on = lax.ppermute(beside(cotangent, columns), HALF, SWAP)

    wz = gather(w_down.reshape(rows, width), ZH).reshape(2, piece // RING, width)
    w_self = [gather(wz[i], Y) for i in range(2)]
    w_other = [lax.ppermute(w_self[i], CORE, SWAP) for i in range(2)]

    extra = sent_on[:, width : width + 4 * top].astype(F32).T
    ids_both = jnp.concatenate([ids.T, extra[:top].astype(jnp.int32)], axis=1)
    gates_p = extra[top : 2 * top] + extra[2 * top : 3 * top] + extra[3 * top : 4 * top]
    gates_both = jnp.concatenate([gates.T, gates_p], axis=1)
    cot_both = jnp.concatenate([cotangent, sent_on[:, :width]], axis=0)
    fills, same, slot_gate, picked = slots_of(
        ids_both, gates_both, cot_both, half * groups, groups, capacity
    )
    picked = picked.astype(BF16)
    sent = (slot_gate * picked.astype(F32)).astype(BF16).reshape(groups, N_HALF * capacity, width)
    grads = exchange(sent, GRP).reshape(slots, width)

    hid = hidden.reshape(N_HALF, groups, capacity, inner)
    hid = jnp.where(half == 0, hid, hid[::-1]).transpose(1, 0, 2, 3).reshape(slots, inner)
    hid_t = hid.T.reshape(2, 2, RING, N_CORE, rows, slots).transpose(3, 0, 2, 1, 4, 5)
    hid_t = hid_t.reshape(N_CORE, part, slots)
    hid_self = lax.dynamic_index_in_dim(hid_t, core, 0, keepdims=False)
    hid_other = lax.dynamic_index_in_dim(hid_t, 1 - core, 0, keepdims=False)
    hid_self, hid_other, sent_on = lax.optimization_barrier((hid_self, hid_other, sent_on))

    for_other = dot(hid_other, grads, ((1,), (0,))).astype(BF16)
    got = lax.ppermute(for_other, CORE, SWAP)
    kept = dot(hid_self, grads, ((1,), (0,))) + got.astype(F32)
    kept = kept.reshape(2, RING, piece // RING, width)
    by_y = scatter_ring(kept, 1, Y)
    sums = scatter_ring(by_y.reshape(RING, rows, width), 0, ZH)
    weight_grads = sums.astype(BF16).reshape(1, rows, width)

    out = sum(
        dot(h[i * piece : (i + 1) * piece], w[i], ((0,), (0,)))
        for h, w in ((hid_self, w_self), (hid_other, w_other))
        for i in range(2)
    )
    out = out.astype(BF16).reshape(groups, N_HALF * capacity, width)
    out, grads = lax.optimization_barrier((out, grads))
    back = exchange(out, GRP).reshape(slots, width)
    mixed, gate_grads = combine(back, fills, same, slot_gate, picked)
    passed = beside(mixed[tokens:].astype(BF16), pieces_of(gate_grads[:, tokens:], 2))
    passed = lax.ppermute(passed, HALF, SWAP)
    mixed = (mixed[:tokens] + passed[:, :width].astype(F32)).astype(BF16)
    extra = passed[:, width : width + 2 * top].astype(F32)
    gate_grads = gate_grads[:, :tokens].T + extra[:, :top] + extra[:, top:]

    hg_self, hg_other = (
        jnp.concatenate([dot(w[i], grads, ((1,), (1,))).astype(BF16) for i in range(2)], axis=0)
        for w in (w_self, w_other)
    )
    low = jnp.where(core == 0, hg_self, hg_other)
    high = jnp.where(core == 0, hg_other, hg_self)
    hg = jnp.stack([low, high]).reshape(N_CORE, 2, RING, 2, rows, slots)
    hg = hg.transpose(1, 3, 2, 0, 4, 5).reshape(inner, slots).T
    hg = hg.reshape(groups, N_HALF, capacity, inner).transpose(1, 0, 2, 3)
    hidden_grads = jnp.where(half == 0, hg, hg[::-1]).reshape(slots, inner)
    return mixed, gate_grads, hidden_grads, weight_grads


def solution(mesh):
    groups = mesh.shape["expert"] // N_HALF
    torus = Mesh(mesh.devices.reshape(N_ZH, N_Y, N_CORE, N_HALF, groups), ALL)
    spread = P(ALL, None)
    weights = P((HALF, GRP), DP, None)

    return jax.shard_map(
        per_device,
        mesh=torus,
        in_specs=(spread, weights, spread, spread, spread),
        out_specs=(spread, spread, spread, weights),
        check_vma=False,
    )
```

time: 259 us -> 260 us (level)
  the two profiles are of different devices: /device:TPU:4 before, /device:TPU:99 now
where the time goes in v2:
time: 260 us; the launch traced here: 259 us
  starting transfers between devices  105 us (40%)
  blocking collectives  76.8 us (30%)
  waiting for transfers between devices  43.2 us (17%)
  matrix products  17.8 us (7%)
  other arithmetic  10 us (4%)
  local copies, waits for them, and re-layouts  5.3 us (2%)
    all_gather x3, blocking collectives, gather(): return lax.all_gather(value, axis, axis=0, tiled=True)  76.8 us
    all_to_all x2, starting transfers between devices, exchange(): return lax.all_to_all(rows, axis, split_axis=0, concat_axis=0, tiled=True)  24.9 us
    dot_general x14, matrix products, dot(): return lax.dot_general(a, b, (dims, ((), ())), preferred_element_type=F32)  17.8 us
    ppermute x1, waiting for transfers between devices, per_device(): passed = lax.ppermute(passed, HALF, SWAP)  17.5 us
    ppermute x2, starting transfers between devices, per_device(): w_other = [lax.ppermute(w_self[i], CORE, SWAP) for i in range(2)]  13.8 us
    ppermute x1, starting transfers between devices, per_device(): passed = lax.ppermute(passed, HALF, SWAP)  13.4 us
    ppermute x2, starting transfers between devices, scatter_ring(): from_above = lax.ppermute(down.astype(BF16), axis, LEFT)  12.7 us
    ppermute x2, starting transfers between devices, scatter_ring(): got_b = lax.ppermute(high(far), axis, LEFT)  11.4 us
  transfers between devices with their start and end apart: 15, of which 7 were waited for; matrix products, arithmetic and copies ran while one was open for 10% of the time, Pallas kernels for 0%

profile of v2, /device:TPU:99, one launch (start us, length us, event | category | flops | bytes accessed | tf_op | source)
XLA Modules:
  0.0 259.0 jit_solution(7826552173419235741)
XLA Ops:
  3.0 8.8 %collective-permute-start = (bf16[32,2176]{1,0:T(8,128)(2,1)S(1)}, bf16[32,2176]{1,0:T(8,128)(2,1)S(1)}, u32[]{:S(2)}, u32[]{:S(2)}) collective-permute-start(bf16[32,2176]{1,0:T(8,128)(2,1)S(1)} %fusion.25), channel_id=1, source_target_pairs={{0,16},{16,0},{1,17},{17,1},{2,18},{18,2},{3,19},{19,3},{4,20},{20... | collective-permute-start | bytes 417800 | tf_op jit(solution)/shard_map/ppermute | solution.py:112
  11.9 10.9 %collective-permute-done = bf16[32,2176]{1,0:T(8,128)(2,1)S(1)} collective-permute-done((bf16[32,2176]{1,0:T(8,128)(2,1)S(1)}, bf16[32,2176]{1,0:T(8,128)(2,1)S(1)}, u32[]{:S(2)}, u32[]{:S(2)}) %collective-permute-start) | collective-permute-done | bytes 139296 | tf_op jit(solution)/shard_map/ppermute | solution.py:112
  24.8 2.7 %fusion.2 = (bf16[256,2048]{1,0:T(8,128)(2,1)}, bf16[256,2048]{1,0:T(8,128)(2,1)}) fusion(f32[256]{0:T(256)S(1)} %get-tuple-element.72, pred[256,64]{0,1:T(32,128)(4,1)S(1)} %get-tuple-element.73, bf16[32,2048]{1,0:T(8,128)(2,1)S(1)} %slice.200, bf16[32,2048]{1,0:T(8,128)(2,1)} %param.9), kind=kOutput, calls=%fused_computation.10 | convolution fusion | flops 69730304 | bytes 2376704 | tf_op jit(solution)/shard_map/dot_general | solution.py:21
  27.5 7.0 %all-to-all-start = ((bf16[16,16,2048]{2,1,0:T(8,128)(2,1)}), bf16[16,16,2048]{2,1,0:T(8,128)(2,1)S(1)}, u32[]{:S(2)}, u32[]{:S(2)}) async-start(bf16[16,16,2048]{2,1,0:T(8,128)(2,1)} %bitcast.24), calls=%async_computation | async-start | bytes 2097152 | tf_op jit(solution)/shard_map/all_to_all | solution.py:25
  34.5 53.4 %all-gather = bf16[1,96,2048]{2,1,0:T(8,128)(2,1)S(1)} all-gather(bf16[1,24,2048]{2,1,0:T(8,128)(2,1)S(1)} %copy-done.4), channel_id=2, replica_groups=mesh['zh'=4,'y'=4,'core'=2,'half'=2,'grp'=16] {'zh'}, dimensions={1}, use_global_device_ids=true | all-gather | bytes 491520 | tf_op jit(solution)/shard_map/all_gather | solution.py:98
  87.9 11.4 %all-gather.2 = bf16[1,192,2048]{2,1,0:T(8,128)(2,1)S(1)} all-gather(bf16[1,48,2048]{2,1,0:T(8,128)(2,1)S(1)} %get-tuple-element.51), channel_id=4, replica_groups=mesh['zh'=4,'y'=4,'core'=2,'half'=2,'grp'=16] {'y'}, dimensions={1}, use_global_device_ids=true | all-gather | bytes 983040 | tf_op jit(solution)/shard_map/all_gather | solution.py:98
  99.3 10.0 %collective-permute-start.2 = (bf16[192,2048]{1,0:T(8,128)(2,1)S(1)}, bf16[192,2048]{1,0:T(8,128)(2,1)}, u32[]{:S(2)}, u32[]{:S(2)}) collective-permute-start(bf16[192,2048]{1,0:T(8,128)(2,1)S(1)} %bitcast.160), channel_id=1, source_target_pairs={{0,32},{32,0},{1,33},{33,1},{2,34},{34,2},{3,35},{35,3},{4,36},{36... | collective-permute-start | bytes 2359304 | tf_op jit(solution)/shard_map/ppermute | solution.py:116
  109.4 12.0 %all-gather.1 = bf16[1,192,2048]{2,1,0:T(8,128)(2,1)S(1)} all-gather(bf16[1,48,2048]{2,1,0:T(8,128)(2,1)S(1)} %get-tuple-element.50), channel_id=3, replica_groups=mesh['zh'=4,'y'=4,'core'=2,'half'=2,'grp'=16] {'y'}, dimensions={1}, use_global_device_ids=true | all-gather | bytes 983040 | tf_op jit(solution)/shard_map/all_gather | solution.py:98
  121.4 3.8 %collective-permute-start.1 = (bf16[192,2048]{1,0:T(8,128)(2,1)S(1)}, bf16[192,2048]{1,0:T(8,128)(2,1)}, u32[]{:S(2)}, u32[]{:S(2)}) collective-permute-start(bf16[192,2048]{1,0:T(8,128)(2,1)S(1)} %bitcast.159), channel_id=1, source_target_pairs={{0,32},{32,0},{1,33},{33,1},{2,34},{34,2},{3,35},{35,3},{4,36},{36... | collective-permute-start | bytes 2359304 | tf_op jit(solution)/shard_map/ppermute | solution.py:116
  126.2 1.8 copy.74
  131.6 2.6 fusion.1
  134.2 17.9 %all-to-all-start.1 = ((bf16[16,16,2048]{2,1,0:T(8,128)(2,1)}), bf16[16,16,2048]{2,1,0:T(8,128)(2,1)S(1)}, u32[]{:S(2)}, u32[]{:S(2)}) async-start(bf16[16,16,2048]{2,1,0:T(8,128)(2,1)} %bitcast.161), calls=%async_computation.1 | async-start | bytes 2097152 | tf_op jit(solution)/shard_map/all_to_all | solution.py:25
  152.1 1.7 convolution_convert_fusion
  153.8 2.5 collective-permute-start.4
  156.3 1.6 fusion.5
  158.5 1.6 fusion.7
  160.1 1.6 fusion.6
  161.8 2.0 convert_add_fusion
  163.9 3.2 %collective-permute-start.5 = (bf16[1,48,2048]{2,1,0:T(8,128)(2,1)S(1)}, bf16[1,48,2048]{2,1,0:T(8,128)(2,1)S(1)}, u32[]{:S(2)}, u32[]{:S(2)}) collective-permute-start(bf16[1,48,2048]{2,1,0:T(8,128)(2,1)S(1)} %get-tuple-element.46), channel_id=1, source_target_pairs={{0,64},{64,128},{128,192},{192,0},{1,65},{65,129},{129,193},{193,1... | collective-permute-start | bytes 589832 | tf_op jit(solution)/shard_map/ppermute | solution.py:87
  167.1 3.3 %collective-permute-start.7 = (bf16[1,48,2048]{2,1,0:T(8,128)(2,1)S(1)}, bf16[1,48,2048]{2,1,0:T(8,128)(2,1)S(1)}, u32[]{:S(2)}, u32[]{:S(2)}) collective-permute-start(bf16[1,48,2048]{2,1,0:T(8,128)(2,1)S(1)} %get-tuple-element.47), channel_id=1, source_target_pairs={{0,192},{64,0},{128,64},{192,128},{1,193},{65,1},{129,65},{193,129... | collective-permute-start | bytes 589832 | tf_op jit(solution)/shard_map/ppermute | solution.py:88
  170.4 3.0 %collective-permute-done.5 = bf16[1,48,2048]{2,1,0:T(8,128)(2,1)S(1)} collective-permute-done((bf16[1,48,2048]{2,1,0:T(8,128)(2,1)S(1)}, bf16[1,48,2048]{2,1,0:T(8,128)(2,1)S(1)}, u32[]{:S(2)}, u32[]{:S(2)}) %collective-permute-start.5) | collective-permute-done | bytes 196640 | tf_op jit(solution)/shard_map/ppermute | solution.py:87
  173.4 1.7 collective-permute-done.7
  175.3 4.5 %collective-permute-start.8 = (bf16[2,48,2048]{2,1,0:T(8,128)(2,1)S(1)}, bf16[2,48,2048]{2,1,0:T(8,128)(2,1)S(1)}, u32[]{:S(2)}, u32[]{:S(2)}) collective-permute-start(bf16[2,48,2048]{2,1,0:T(8,128)(2,1)S(1)} %pad_maximum_fusion.2), channel_id=1, source_target_pairs={{0,192},{64,0},{128,64},{192,128},{1,193},{65,1},{129,65},{193,129... | collective-permute-start | bytes 1179656 | tf_op jit(solution)/shard_map/ppermute | solution.py:93
  179.8 1.9 collective-permute-start.6
  183.0 4.1 %collective-permute-done.8 = bf16[2,48,2048]{2,1,0:T(8,128)(2,1)S(1)} collective-permute-done((bf16[2,48,2048]{2,1,0:T(8,128)(2,1)S(1)}, bf16[2,48,2048]{2,1,0:T(8,128)(2,1)S(1)}, u32[]{:S(2)}, u32[]{:S(2)}) %collective-permute-start.8) | collective-permute-done | bytes 393248 | tf_op jit(solution)/shard_map/ppermute | solution.py:93
  187.1 5.1 %collective-permute-done.6 = bf16[2,48,2048]{2,1,0:T(8,128)(2,1)S(1)} collective-permute-done((bf16[2,48,2048]{2,1,0:T(8,128)(2,1)S(1)}, bf16[2,48,2048]{2,1,0:T(8,128)(2,1)S(1)}, u32[]{:S(2)}, u32[]{:S(2)}) %collective-permute-start.6) | collective-permute-done | bytes 393248 | tf_op jit(solution)/shard_map/ppermute | solution.py:92
  193.5 8.1 %collective-permute-start.11 = (bf16[24,1024]{1,0:T(8,128)(2,1)S(1)}, bf16[24,1024]{1,0:T(8,128)(2,1)S(1)}, u32[]{:S(2)}, u32[]{:S(2)}) collective-permute-start(bf16[24,1024]{1,0:T(8,128)(2,1)S(1)} %get-tuple-element.55), channel_id=1, source_target_pairs={{0,768},{256,0},{512,256},{768,512},{1,769},{257,1},{513,257},{769... | collective-permute-start | bytes 147464 | tf_op jit(solution)/shard_map/ppermute | solution.py:88
  201.7 5.9 %collective-permute-start.9 = (bf16[24,1024]{1,0:T(8,128)(2,1)S(1)}, bf16[24,1024]{1,0:T(8,128)(2,1)S(1)}, u32[]{:S(2)}, u32[]{:S(2)}) collective-permute-start(bf16[24,1024]{1,0:T(8,128)(2,1)S(1)} %get-tuple-element.54), channel_id=1, source_target_pairs={{0,256},{256,512},{512,768},{768,0},{1,257},{257,513},{513,769},{7... | collective-permute-start | bytes 147464 | tf_op jit(solution)/shard_map/ppermute | solution.py:87
  207.6 8.2 %collective-permute-start.12 = (bf16[24,2048]{1,0:T(8,128)(2,1)S(1)}, bf16[24,2048]{1,0:T(8,128)(2,1)}, u32[]{:S(2)}, u32[]{:S(2)}) collective-permute-start(bf16[24,2048]{1,0:T(8,128)(2,1)S(1)} %pad_maximum_fusion.6), channel_id=1, source_target_pairs={{0,768},{256,0},{512,256},{768,512},{1,769},{257,1},{513,257},{769... | collective-permute-start | bytes 294920 | tf_op jit(solution)/shard_map/ppermute | solution.py:93
  217.4 6.0 %collective-permute-start.10 = (bf16[24,2048]{1,0:T(8,128)(2,1)}, bf16[24,2048]{1,0:T(8,128)(2,1)}, u32[]{:S(2)}, u32[]{:S(2)}) collective-permute-start(bf16[24,2048]{1,0:T(8,128)(2,1)} %pad_maximum_fusion.5), channel_id=1, source_target_pairs={{0,256},{256,512},{512,768},{768,0},{1,257},{257,513},{513,769},{7... | collective-permute-start | bytes 294920 | tf_op jit(solution)/shard_map/ppermute | solution.py:92
  225.0 13.4 %collective-permute-start.3 = (bf16[32,2176]{1,0:T(8,128)(2,1)S(1)}, bf16[32,2176]{1,0:T(8,128)(2,1)S(1)}, u32[]{:S(2)}, u32[]{:S(2)}) collective-permute-start(bf16[32,2176]{1,0:T(8,128)(2,1)S(1)} %fusion.26), channel_id=1, source_target_pairs={{0,16},{16,0},{1,17},{17,1},{2,18},{18,2},{3,19},{19,3},{4,20},{20... | collective-permute-start | bytes 417800 | tf_op jit(solution)/shard_map/ppermute | solution.py:156
  240.1 17.5 %collective-permute-done.3 = bf16[32,2176]{1,0:T(8,128)(2,1)S(1)} collective-permute-done((bf16[32,2176]{1,0:T(8,128)(2,1)S(1)}, bf16[32,2176]{1,0:T(8,128)(2,1)S(1)}, u32[]{:S(2)}, u32[]{:S(2)}) %collective-permute-start.3) | collective-permute-done | bytes 139296 | tf_op jit(solution)/shard_map/ppermute | solution.py:156
  (84 shorter events, 18.4 us)
Async XLA Ops:
  3.0 19.8 %collective-permute-start = (bf16[32,2176]{1,0:T(8,128)(2,1)S(1)}, bf16[32,2176]{1,0:T(8,128)(2,1)S(1)}, u32[]{:S(2)}, u32[]{:S(2)}) collective-permute-start(bf16[32,2176]{1,0:T(8,128)(2,1)S(1)} %fusion.25), channel_id=1, source_target_pairs={{0,16},{16,0},{1,17},{17,1},{2,18},{18,2},{3,19},{19,3},{4,20},{20... | collective-permute-start | bytes 417800 | tf_op jit(solution)/shard_map/ppermute | solution.py:112
  24.7 9.7 %copy-start.4 = (bf16[1,24,2048]{2,1,0:T(8,128)(2,1)S(1)}, bf16[1,24,2048]{2,1,0:T(8,128)(2,1)}, u32[]{:S(2)}) copy-start(bf16[1,24,2048]{2,1,0:T(8,128)(2,1)} %param.6) | copy-start | bytes 294916
  27.5 106.7 %all-to-all-start = ((bf16[16,16,2048]{2,1,0:T(8,128)(2,1)}), bf16[16,16,2048]{2,1,0:T(8,128)(2,1)S(1)}, u32[]{:S(2)}, u32[]{:S(2)}) async-start(bf16[16,16,2048]{2,1,0:T(8,128)(2,1)} %bitcast.24), calls=%async_computation | async-start | bytes 2097152 | tf_op jit(solution)/shard_map/all_to_all | solution.py:25
  34.5 90.7 %copy-start.3 = (bf16[256,768]{1,0:T(8,128)(2,1)S(1)}, bf16[256,768]{1,0:T(8,128)(2,1)}, u32[]{:S(2)}) copy-start(bf16[256,768]{1,0:T(8,128)(2,1)} %param.5) | copy-start | bytes 1179652
  99.3 29.7 %copy-start.1 = (bf16[1,192,2048]{2,1,0:T(8,128)(2,1)}, bf16[1,192,2048]{2,1,0:T(8,128)(2,1)S(1)}, u32[]{:S(2)}) copy-start(bf16[1,192,2048]{2,1,0:T(8,128)(2,1)S(1)} %all-gather.2) | copy-start | bytes 2359300
  99.3 30.7 %collective-permute-start.2 = (bf16[192,2048]{1,0:T(8,128)(2,1)S(1)}, bf16[192,2048]{1,0:T(8,128)(2,1)}, u32[]{:S(2)}, u32[]{:S(2)}) collective-permute-start(bf16[192,2048]{1,0:T(8,128)(2,1)S(1)} %bitcast.160), channel_id=1, source_target_pairs={{0,32},{32,0},{1,33},{33,1},{2,34},{34,2},{3,35},{35,3},{4,36},{36... | collective-permute-start | bytes 2359304 | tf_op jit(solution)/shard_map/ppermute | solution.py:116
  121.4 10.2 %collective-permute-start.1 = (bf16[192,2048]{1,0:T(8,128)(2,1)S(1)}, bf16[192,2048]{1,0:T(8,128)(2,1)}, u32[]{:S(2)}, u32[]{:S(2)}) collective-permute-start(bf16[192,2048]{1,0:T(8,128)(2,1)S(1)} %bitcast.159), channel_id=1, source_target_pairs={{0,32},{32,0},{1,33},{33,1},{2,34},{34,2},{3,35},{35,3},{4,36},{36... | collective-permute-start | bytes 2359304 | tf_op jit(solution)/shard_map/ppermute | solution.py:116
  134.2 89.3 %all-to-all-start.1 = ((bf16[16,16,2048]{2,1,0:T(8,128)(2,1)}), bf16[16,16,2048]{2,1,0:T(8,128)(2,1)S(1)}, u32[]{:S(2)}, u32[]{:S(2)}) async-start(bf16[16,16,2048]{2,1,0:T(8,128)(2,1)} %bitcast.161), calls=%async_computation.1 | async-start | bytes 2097152 | tf_op jit(solution)/shard_map/all_to_all | solution.py:25
  153.8 7.9 %collective-permute-start.4 = (bf16[384,2048]{1,0:T(8,128)(2,1)}, bf16[384,2048]{1,0:T(8,128)(2,1)}, u32[]{:S(2)}, u32[]{:S(2)}) collective-permute-start(bf16[384,2048]{1,0:T(8,128)(2,1)} %convolution_convert_fusion), channel_id=1, source_target_pairs={{0,32},{32,0},{1,33},{33,1},{2,34},{34,2},{3,35},{35,3},{4,36},{36... | collective-permute-start | bytes 4718600 | tf_op jit(solution)/shard_map/ppermute | solution.py:139
  163.8 11.5 %copy-start = (f32[384,2048]{1,0:T(8,128)}, f32[384,2048]{1,0:T(8,128)S(1)}, u32[]{:S(2)}) copy-start(f32[384,2048]{1,0:T(8,128)S(1)} %convert_add_fusion) | copy-start | bytes 9437188
  163.9 9.6 %collective-permute-start.5 = (bf16[1,48,2048]{2,1,0:T(8,128)(2,1)S(1)}, bf16[1,48,2048]{2,1,0:T(8,128)(2,1)S(1)}, u32[]{:S(2)}, u32[]{:S(2)}) collective-permute-start(bf16[1,48,2048]{2,1,0:T(8,128)(2,1)S(1)} %get-tuple-element.46), channel_id=1, source_target_pairs={{0,64},{64,128},{128,192},{192,0},{1,65},{65,129},{129,193},{193,1... | collective-permute-start | bytes 589832 | tf_op jit(solution)/shard_map/ppermute | solution.py:87
  167.1 8.1 %collective-permute-start.7 = (bf16[1,48,2048]{2,1,0:T(8,128)(2,1)S(1)}, bf16[1,48,2048]{2,1,0:T(8,128)(2,1)S(1)}, u32[]{:S(2)}, u32[]{:S(2)}) collective-permute-start(bf16[1,48,2048]{2,1,0:T(8,128)(2,1)S(1)} %get-tuple-element.47), channel_id=1, source_target_pairs={{0,192},{64,0},{128,64},{192,128},{1,193},{65,1},{129,65},{193,129... | collective-permute-start | bytes 589832 | tf_op jit(solution)/shard_map/ppermute | solution.py:88
  175.3 11.8 %collective-permute-start.8 = (bf16[2,48,2048]{2,1,0:T(8,128)(2,1)S(1)}, bf16[2,48,2048]{2,1,0:T(8,128)(2,1)S(1)}, u32[]{:S(2)}, u32[]{:S(2)}) collective-permute-start(bf16[2,48,2048]{2,1,0:T(8,128)(2,1)S(1)} %pad_maximum_fusion.2), channel_id=1, source_target_pairs={{0,192},{64,0},{128,64},{192,128},{1,193},{65,1},{129,65},{193,129... | collective-permute-start | bytes 1179656 | tf_op jit(solution)/shard_map/ppermute | solution.py:93
  179.8 12.4 %collective-permute-start.6 = (bf16[2,48,2048]{2,1,0:T(8,128)(2,1)S(1)}, bf16[2,48,2048]{2,1,0:T(8,128)(2,1)S(1)}, u32[]{:S(2)}, u32[]{:S(2)}) collective-permute-start(bf16[2,48,2048]{2,1,0:T(8,128)(2,1)S(1)} %pad_maximum_fusion.1), channel_id=1, source_target_pairs={{0,64},{64,128},{128,192},{192,0},{1,65},{65,129},{129,193},{193,1... | collective-permute-start | bytes 1179656 | tf_op jit(solution)/shard_map/ppermute | solution.py:92
  193.5 14.1 %collective-permute-start.11 = (bf16[24,1024]{1,0:T(8,128)(2,1)S(1)}, bf16[24,1024]{1,0:T(8,128)(2,1)S(1)}, u32[]{:S(2)}, u32[]{:S(2)}) collective-permute-start(bf16[24,1024]{1,0:T(8,128)(2,1)S(1)} %get-tuple-element.55), channel_id=1, source_target_pairs={{0,768},{256,0},{512,256},{768,512},{1,769},{257,1},{513,257},{769... | collective-permute-start | bytes 147464 | tf_op jit(solution)/shard_map/ppermute | solution.py:88
  201.7 15.1 %collective-permute-start.9 = (bf16[24,1024]{1,0:T(8,128)(2,1)S(1)}, bf16[24,1024]{1,0:T(8,128)(2,1)S(1)}, u32[]{:S(2)}, u32[]{:S(2)}) collective-permute-start(bf16[24,1024]{1,0:T(8,128)(2,1)S(1)} %get-tuple-element.54), channel_id=1, source_target_pairs={{0,256},{256,512},{512,768},{768,0},{1,257},{257,513},{513,769},{7... | collective-permute-start | bytes 147464 | tf_op jit(solution)/shard_map/ppermute | solution.py:87
  207.6 16.5 %copy-start.2 = (bf16[256,2048]{1,0:T(8,128)(2,1)S(1)}, bf16[256,2048]{1,0:T(8,128)(2,1)}, u32[]{:S(2)}) copy-start(bf16[256,2048]{1,0:T(8,128)(2,1)} %get-tuple-element.75) | copy-start | bytes 3145732
  207.6 30.7 %collective-permute-start.12 = (bf16[24,2048]{1,0:T(8,128)(2,1)S(1)}, bf16[24,2048]{1,0:T(8,128)(2,1)}, u32[]{:S(2)}, u32[]{:S(2)}) collective-permute-start(bf16[24,2048]{1,0:T(8,128)(2,1)S(1)} %pad_maximum_fusion.6), channel_id=1, source_target_pairs={{0,768},{256,0},{512,256},{768,512},{1,769},{257,1},{513,257},{769... | collective-permute-start | bytes 294920 | tf_op jit(solution)/shard_map/ppermute | solution.py:93
  217.4 20.9 %collective-permute-start.10 = (bf16[24,2048]{1,0:T(8,128)(2,1)}, bf16[24,2048]{1,0:T(8,128)(2,1)}, u32[]{:S(2)}, u32[]{:S(2)}) collective-permute-start(bf16[24,2048]{1,0:T(8,128)(2,1)} %pad_maximum_fusion.5), channel_id=1, source_target_pairs={{0,256},{256,512},{512,768},{768,0},{1,257},{257,513},{513,769},{7... | collective-permute-start | bytes 294920 | tf_op jit(solution)/shard_map/ppermute | solution.py:92
  225.0 32.6 %collective-permute-start.3 = (bf16[32,2176]{1,0:T(8,128)(2,1)S(1)}, bf16[32,2176]{1,0:T(8,128)(2,1)S(1)}, u32[]{:S(2)}, u32[]{:S(2)}) collective-permute-start(bf16[32,2176]{1,0:T(8,128)(2,1)S(1)} %fusion.26), channel_id=1, source_target_pairs={{0,16},{16,0},{1,17},{17,1},{2,18},{18,2},{3,19},{19,3},{4,20},{20... | collective-permute-start | bytes 417800 | tf_op jit(solution)/shard_map/ppermute | solution.py:156

commit v3 on v2

--- a/solution.py
+++ b/solution.py
@@ -11,8 +11,6 @@
 N_ZH, N_Y, N_CORE, N_HALF = 4, 4, 2, 2
 RING = 4
 LANES = 128
-RIGHT = [(i, (i + 1) % RING) for i in range(RING)]
-LEFT = [(i, (i - 1) % RING) for i in range(RING)]
 SWAP = [(0, 1), (1, 0)]
 F32, BF16 = jnp.float32, jnp.bfloat16
 
@@ -72,26 +70,17 @@
     return jnp.concatenate([rows, extra], axis=1)
 
 
-def scatter_ring(blocks, dim, axis):
+def scatter(blocks, axis):
     here = lax.axis_index(axis)
 
     def block(step):
-        return lax.dynamic_index_in_dim(blocks, (here + step) & 3, dim, keepdims=False)
+        return lax.dynamic_index_in_dim(blocks, (here + step) & 3, 0, keepdims=False)
 
-    far = block(2).astype(BF16)
-    cut = 0 if far.ndim == 3 else 1
-    half = far.shape[cut] // 2
-    low, high = (lambda v: lax.slice_in_dim(v, 0, half, axis=cut)), (
-        lambda v: lax.slice_in_dim(v, half, 2 * half, axis=cut)
-    )
-    got_a = lax.ppermute(low(far), axis, RIGHT)
-    got_b = lax.ppermute(high(far), axis, LEFT)
-    up, down = block(1).astype(F32), block(3).astype(F32)
-    up = jnp.concatenate([low(up) + got_a.astype(F32), high(up)], axis=cut)
-    down = jnp.concatenate([low(down), high(down) + got_b.astype(F32)], axis=cut)
-    from_below = lax.ppermute(up.astype(BF16), axis, RIGHT)
-    from_above = lax.ppermute(down.astype(BF16), axis, LEFT)
-    return block(0).astype(F32) + from_below.astype(F32) + from_above.astype(F32)
+    total = block(0).astype(F32)
+    for step in (2, 1, 3):
+        perm = [(i, (i + step) % RING) for i in range(RING)]
+        total = total + lax.ppermute(block(step).astype(BF16), axis, perm).astype(F32)
+    return total
 
 
 def gather(value, axis):
@@ -105,15 +94,17 @@
     tokens, top = ids.shape
     rows, width = w_down.shape[1:]
     core, half = lax.axis_index(CORE), lax.axis_index(HALF)
-    piece = RING // 2 * RING * rows
-    part = 2 * piece
+    part = RING * RING * rows
 
     columns = [ids.T.astype(BF16), *pieces_of(gates.T, 3)]
-    sent_on = lax.ppermute(beside(cotangent, columns), HALF, SWAP)
+    to_send, weight_rows = lax.optimization_barrier(
+        (beside(cotangent, columns), w_down.reshape(rows, width))
+    )
 
-    wz = gather(w_down.reshape(rows, width), ZH).reshape(2, piece // RING, width)
-    w_self = [gather(wz[i], Y) for i in range(2)]
-    w_other = [lax.ppermute(w_self[i], CORE, SWAP) for i in range(2)]
+    wz = gather(weight_rows, ZH)
+    sent_on = lax.ppermute(to_send, HALF, SWAP)
+    w_self = exchange(jnp.broadcast_to(wz[None], (RING, *wz.shape)), Y).reshape(part, width)
+    w_other = lax.ppermute(w_self, CORE, SWAP)
 
     extra = sent_on[:, width : width + 4 * top].astype(F32).T
     ids_both = jnp.concatenate([ids.T, extra[:top].astype(jnp.int32)], axis=1)
@@ -125,31 +116,28 @@
     )
     picked = picked.astype(BF16)
     sent = (slot_gate * picked.astype(F32)).astype(BF16).reshape(groups, N_HALF * capacity, width)
+    sent, w_self = lax.optimization_barrier((sent, w_self))
     grads = exchange(sent, GRP).reshape(slots, width)
 
     hid = hidden.reshape(N_HALF, groups, capacity, inner)
     hid = jnp.where(half == 0, hid, hid[::-1]).transpose(1, 0, 2, 3).reshape(slots, inner)
-    hid_t = hid.T.reshape(2, 2, RING, N_CORE, rows, slots).transpose(3, 0, 2, 1, 4, 5)
+    hid_t = hid.T.reshape(RING, RING, N_CORE, rows, slots).transpose(2, 1, 0, 3, 4)
     hid_t = hid_t.reshape(N_CORE, part, slots)
     hid_self = lax.dynamic_index_in_dim(hid_t, core, 0, keepdims=False)
     hid_other = lax.dynamic_index_in_dim(hid_t, 1 - core, 0, keepdims=False)
-    hid_self, hid_other, sent_on = lax.optimization_barrier((hid_self, hid_other, sent_on))
+    hid_self, hid_other = lax.optimization_barrier((hid_self, hid_other))
+
+    out = dot(hid_self, w_self, ((0,), (0,))) + dot(hid_other, w_other, ((0,), (0,)))
+    out = out.astype(BF16).reshape(groups, N_HALF * capacity, width)
+    out, grads = lax.optimization_barrier((out, grads))
 
     for_other = dot(hid_other, grads, ((1,), (0,))).astype(BF16)
     got = lax.ppermute(for_other, CORE, SWAP)
     kept = dot(hid_self, grads, ((1,), (0,))) + got.astype(F32)
-    kept = kept.reshape(2, RING, piece // RING, width)
-    by_y = scatter_ring(kept, 1, Y)
-    sums = scatter_ring(by_y.reshape(RING, rows, width), 0, ZH)
-    weight_grads = sums.astype(BF16).reshape(1, rows, width)
+    by_y = scatter(kept.reshape(RING, RING * rows, width), Y)
+    weight_grads = scatter(by_y.reshape(RING, rows, width), ZH)
+    weight_grads = weight_grads.astype(BF16).reshape(1, rows, width)
 
-    out = sum(
-        dot(h[i * piece : (i + 1) * piece], w[i], ((0,), (0,)))
-        for h, w in ((hid_self, w_self), (hid_other, w_other))
-        for i in range(2)
-    )
-    out = out.astype(BF16).reshape(groups, N_HALF * capacity, width)
-    out, grads = lax.optimization_barrier((out, grads))
     back = exchange(out, GRP).reshape(slots, width)
     mixed, gate_grads = combine(back, fills, same, slot_gate, picked)
     passed = beside(mixed[tokens:].astype(BF16), pieces_of(gate_grads[:, tokens:], 2))
@@ -158,14 +146,12 @@
     extra = passed[:, width : width + 2 * top].astype(F32)
     gate_grads = gate_grads[:, :tokens].T + extra[:, :top] + extra[:, top:]
 
-    hg_self, hg_other = (
-        jnp.concatenate([dot(w[i], grads, ((1,), (1,))).astype(BF16) for i in range(2)], axis=0)
-        for w in (w_self, w_other)
-    )
+    hg_self = dot(w_self, grads, ((1,), (1,))).astype(BF16)
+    hg_other = dot(w_other, grads, ((1,), (1,))).astype(BF16)
     low = jnp.where(core == 0, hg_self, hg_other)
     high = jnp.where(core == 0, hg_other, hg_self)
-    hg = jnp.stack([low, high]).reshape(N_CORE, 2, RING, 2, rows, slots)
-    hg = hg.transpose(1, 3, 2, 0, 4, 5).reshape(inner, slots).T
+    hg = jnp.stack([low, high]).reshape(N_CORE, RING, RING, rows, slots)
+    hg = hg.transpose(2, 1, 0, 3, 4).reshape(inner, slots).T
     hg = hg.reshape(groups, N_HALF, capacity, inner).transpose(1, 0, 2, 3)
     hidden_grads = jnp.where(half == 0, hg, hg[::-1]).reshape(slots, inner)
     return mixed, gate_grads, hidden_grads, weight_grads

time: 260 us -> 232 us (0.89)
  the two profiles are of different devices: /device:TPU:99 before, /device:TPU:1 now
where the time goes in v3:
time: 232 us; the launch traced here: 230 us
  starting transfers between devices  94.5 us (41%)
  waiting for transfers between devices  64.9 us (28%)
  blocking collectives  41.6 us (18%)
  matrix products  14.3 us (6%)
  other arithmetic  8.24 us (4%)
  local copies, waits for them, and re-layouts  5.55 us (2%)
    all_gather x1, blocking collectives, gather(): return lax.all_gather(value, axis, axis=0, tiled=True)  41.6 us
    all_to_all x3, starting transfers between devices, exchange(): return lax.all_to_all(rows, axis, split_axis=0, concat_axis=0, tiled=True)  41.2 us
    ppermute x6, starting transfers between devices, scatter(): lax.ppermute(block(step).astype(BF16), axis, perm).astype(F32)  33.9 us
    all_to_all x3, waiting for transfers between devices, exchange(): return lax.all_to_all(rows, axis, split_axis=0, concat_axis=0, tiled=True)  23.6 us
    ppermute x6, waiting for transfers between devices, scatter(): lax.ppermute(block(step).astype(BF16), axis, perm).astype(F32)  23 us
    ppermute x1, waiting for transfers between devices, per_device(): passed = lax.ppermute(passed, HALF, SWAP)  16.7 us
    dot_general x10, matrix products, dot(): return lax.dot_general(a, b, (dims, ((), ())), preferred_element_type=F32)  14.3 us
    ppermute x1, starting transfers between devices, per_device(): sent_on = lax.ppermute(to_send, HALF, SWAP)  9.64 us
  transfers between devices with their start and end apart: 13, of which 8 were waited for; matrix products, arithmetic and copies ran while one was open for 11% of the time, Pallas kernels for 0%

profile of v3, /device:TPU:1, one launch (start us, length us, event | category | flops | bytes accessed | tf_op | source)
XLA Modules:
  0.0 230.1 jit_solution(12447866771992721907)
XLA Ops:
  3.0 9.6 %collective-permute-start = (bf16[32,2176]{1,0:T(8,128)(2,1)S(1)}, bf16[32,2176]{1,0:T(8,128)(2,1)S(1)}, u32[]{:S(2)}, u32[]{:S(2)}) collective-permute-start(bf16[32,2176]{1,0:T(8,128)(2,1)S(1)} %fusion.19), channel_id=1, source_target_pairs={{0,16},{16,0},{1,17},{17,1},{2,18},{18,2},{3,19},{19,3},{4,20},{20... | collective-permute-start | bytes 417800 | tf_op jit(solution)/shard_map/ppermute | solution.py:105
  12.7 41.6 %all_gather.3 = bf16[96,2048]{1,0:T(8,128)(2,1)S(1)} all-gather(bf16[24,2048]{1,0:T(8,128)(2,1)} %bitcast.137), channel_id=1, replica_groups=mesh['zh'=4,'y'=4,'core'=2,'half'=2,'grp'=16] {'zh'}, dimensions={0}, use_global_device_ids=true | all-gather | bytes 491520 | tf_op jit(solution)/shard_map/all_gather | solution.py:87
  54.3 1.4 broadcast_in_dim.82
  55.6 4.3 %all-to-all-start = ((bf16[4,96,2048]{2,1,0:T(8,128)(2,1)}), bf16[4,96,2048]{2,1,0:T(8,128)(2,1)S(1)}, u32[]{:S(2)}, u32[]{:S(2)}) async-start(bf16[4,96,2048]{2,1,0:T(8,128)(2,1)} %broadcast_in_dim.82), calls=%async_computation | async-start | bytes 3145728 | tf_op jit(solution)/shard_map/all_to_all | solution.py:23
  60.6 1.8 fusion.1
  62.4 11.8 %all-to-all-done = bf16[4,96,2048]{2,1,0:T(8,128)(2,1)S(1)} async-done(((bf16[4,96,2048]{2,1,0:T(8,128)(2,1)}), bf16[4,96,2048]{2,1,0:T(8,128)(2,1)S(1)}, u32[]{:S(2)}, u32[]{:S(2)}) %all-to-all-start) | async-done | bytes 1572896 | tf_op jit(solution)/shard_map/all_to_all | solution.py:23
  74.2 29.1 %all-to-all-start.1 = ((bf16[16,16,2048]{2,1,0:T(8,128)(2,1)}), bf16[16,16,2048]{2,1,0:T(8,128)(2,1)S(1)}, u32[]{:S(2)}, u32[]{:S(2)}) async-start(bf16[16,16,2048]{2,1,0:T(8,128)(2,1)} %bitcast.124), calls=%async_computation.1 | async-start | bytes 2097152 | tf_op jit(solution)/shard_map/all_to_all | solution.py:23
  103.3 4.1 %collective-permute-start.1 = (bf16[384,2048]{1,0:T(8,128)(2,1)S(1)}, bf16[384,2048]{1,0:T(8,128)(2,1)}, u32[]{:S(2)}, u32[]{:S(2)}) collective-permute-start(bf16[384,2048]{1,0:T(8,128)(2,1)S(1)} %bitcast.121), channel_id=1, source_target_pairs={{0,32},{32,0},{1,33},{33,1},{2,34},{34,2},{3,35},{35,3},{4,36},{36... | collective-permute-start | bytes 4718600 | tf_op jit(solution)/shard_map/ppermute | solution.py:107
  107.5 0.9 copy.73
  108.4 1.0 copy.74
  110.5 3.2 %fusion = bf16[256,2048]{1,0:T(8,128)(2,1)} fusion(f32[256,2048]{1,0:T(8,128)S(1)} %fusion.59, bf16[384,256]{1,0:T(8,128)(2,1)S(1)} %get-tuple-element.16, bf16[384,2048]{1,0:T(8,128)(2,1)} %collective-permute-done.1), kind=kOutput, calls=%fused_computation.5 | convolution fusion | flops 403701760 | bytes 4915200 | tf_op jit(solution)/shard_map/dot_general | solution.py:19
  113.7 11.8 %all-to-all-done.1 = bf16[16,16,2048]{2,1,0:T(8,128)(2,1)S(1)} async-done(((bf16[16,16,2048]{2,1,0:T(8,128)(2,1)}), bf16[16,16,2048]{2,1,0:T(8,128)(2,1)S(1)}, u32[]{:S(2)}, u32[]{:S(2)}) %all-to-all-start.1) | async-done | bytes 1048608 | tf_op jit(solution)/shard_map/all_to_all | solution.py:23
  125.5 7.8 %all-to-all-start.2 = ((bf16[16,16,2048]{2,1,0:T(8,128)(2,1)}), bf16[16,16,2048]{2,1,0:T(8,128)(2,1)S(1)}, u32[]{:S(2)}, u32[]{:S(2)}) async-start(bf16[16,16,2048]{2,1,0:T(8,128)(2,1)} %bitcast.24), calls=%async_computation.2 | async-start | bytes 2097152 | tf_op jit(solution)/shard_map/all_to_all | solution.py:23
  133.3 1.7 convolution_convert_fusion
  135.0 3.8 %collective-permute-start.3 = (bf16[384,2048]{1,0:T(8,128)(2,1)}, bf16[384,2048]{1,0:T(8,128)(2,1)}, u32[]{:S(2)}, u32[]{:S(2)}) collective-permute-start(bf16[384,2048]{1,0:T(8,128)(2,1)} %convolution_convert_fusion), channel_id=1, source_target_pairs={{0,32},{32,0},{1,33},{33,1},{2,34},{34,2},{3,35},{35,3},{4,36},{36... | collective-permute-start | bytes 4718600 | tf_op jit(solution)/shard_map/ppermute | solution.py:135
  138.8 2.0 convolution_convert_fusion.3
  140.8 1.3 collective-permute-done.3
  142.1 2.0 convert_add_fusion
  144.3 2.8 %collective-permute-start.6 = (bf16[96,2048]{1,0:T(8,128)(2,1)S(1)}, bf16[96,2048]{1,0:T(8,128)(2,1)}, u32[]{:S(2)}, u32[]{:S(2)}) collective-permute-start(bf16[96,2048]{1,0:T(8,128)(2,1)S(1)} %get-tuple-element.49), channel_id=1, source_target_pairs={{0,192},{64,0},{128,64},{192,128},{1,193},{65,1},{129,65},{193,129... | collective-permute-start | bytes 1179656 | tf_op jit(solution)/shard_map/ppermute | solution.py:82
  147.1 2.5 %collective-permute-start.5 = (bf16[96,2048]{1,0:T(8,128)(2,1)S(1)}, bf16[96,2048]{1,0:T(8,128)(2,1)}, u32[]{:S(2)}, u32[]{:S(2)}) collective-permute-start(bf16[96,2048]{1,0:T(8,128)(2,1)S(1)} %get-tuple-element.50), channel_id=1, source_target_pairs={{0,64},{64,128},{128,192},{192,0},{1,65},{65,129},{129,193},{193,1... | collective-permute-start | bytes 1179656 | tf_op jit(solution)/shard_map/ppermute | solution.py:82
  149.6 2.5 %collective-permute-start.4 = (bf16[96,2048]{1,0:T(8,128)(2,1)S(1)}, bf16[96,2048]{1,0:T(8,128)(2,1)}, u32[]{:S(2)}, u32[]{:S(2)}) collective-permute-start(bf16[96,2048]{1,0:T(8,128)(2,1)S(1)} %get-tuple-element.48), channel_id=1, source_target_pairs={{0,128},{64,192},{128,0},{192,64},{1,129},{65,193},{129,1},{193,65... | collective-permute-start | bytes 1179656 | tf_op jit(solution)/shard_map/ppermute | solution.py:82
  152.1 2.0 broadcast_select_fusion.1
  155.3 1.3 collective-permute-done.6
  156.6 12.2 %collective-permute-done.5 = bf16[96,2048]{1,0:T(8,128)(2,1)} collective-permute-done((bf16[96,2048]{1,0:T(8,128)(2,1)S(1)}, bf16[96,2048]{1,0:T(8,128)(2,1)}, u32[]{:S(2)}, u32[]{:S(2)}) %collective-permute-start.5) | collective-permute-done | bytes 393248 | tf_op jit(solution)/shard_map/ppermute | solution.py:82
  168.8 1.7 fusion.5
  171.2 1.9 collective-permute-start.9
  173.1 12.1 %collective-permute-start.8 = (bf16[24,2048]{1,0:T(8,128)(2,1)}, bf16[24,2048]{1,0:T(8,128)(2,1)}, u32[]{:S(2)}, u32[]{:S(2)}) collective-permute-start(bf16[24,2048]{1,0:T(8,128)(2,1)} %get-tuple-element.53), channel_id=1, source_target_pairs={{0,256},{256,512},{512,768},{768,0},{1,257},{257,513},{513,769},{7... | collective-permute-start | bytes 294920 | tf_op jit(solution)/shard_map/ppermute | solution.py:82
  185.2 12.1 %collective-permute-start.7 = (bf16[24,2048]{1,0:T(8,128)(2,1)S(1)}, bf16[24,2048]{1,0:T(8,128)(2,1)}, u32[]{:S(2)}, u32[]{:S(2)}) collective-permute-start(bf16[24,2048]{1,0:T(8,128)(2,1)S(1)} %get-tuple-element.51), channel_id=1, source_target_pairs={{0,512},{256,768},{512,0},{768,256},{1,513},{257,769},{513,1},{769... | collective-permute-start | bytes 294920 | tf_op jit(solution)/shard_map/ppermute | solution.py:82
  198.8 1.9 collective-permute-start.2
  200.7 9.5 %collective-permute-done.7 = bf16[24,2048]{1,0:T(8,128)(2,1)} collective-permute-done((bf16[24,2048]{1,0:T(8,128)(2,1)S(1)}, bf16[24,2048]{1,0:T(8,128)(2,1)}, u32[]{:S(2)}, u32[]{:S(2)}) %collective-permute-start.7) | collective-permute-done | bytes 98336 | tf_op jit(solution)/shard_map/ppermute | solution.py:82
  210.2 1.7 fusion.24
  212.0 16.7 %collective-permute-done.2 = bf16[32,2176]{1,0:T(8,128)(2,1)S(1)} collective-permute-done((bf16[32,2176]{1,0:T(8,128)(2,1)S(1)}, bf16[32,2176]{1,0:T(8,128)(2,1)S(1)}, u32[]{:S(2)}, u32[]{:S(2)}) %collective-permute-start.2) | collective-permute-done | bytes 139296 | tf_op jit(solution)/shard_map/ppermute | solution.py:144
  (64 shorter events, 9.1 us)
Async XLA Ops:
  3.0 56.9 %collective-permute-start = (bf16[32,2176]{1,0:T(8,128)(2,1)S(1)}, bf16[32,2176]{1,0:T(8,128)(2,1)S(1)}, u32[]{:S(2)}, u32[]{:S(2)}) collective-permute-start(bf16[32,2176]{1,0:T(8,128)(2,1)S(1)} %fusion.19), channel_id=1, source_target_pairs={{0,16},{16,0},{1,17},{17,1},{2,18},{18,2},{3,19},{19,3},{4,20},{20... | collective-permute-start | bytes 417800 | tf_op jit(solution)/shard_map/ppermute | solution.py:105
  55.6 4.5 %copy-start.5 = (f32[32,4]{0,1:T(4,128)S(1)}, f32[32,4]{0,1:T(4,128)}, u32[]{:S(2)}) copy-start(f32[32,4]{0,1:T(4,128)} %param.8) | copy-start | bytes 1540
  55.6 4.6 %copy-start.6 = (s32[32,4]{0,1:T(4,128)S(1)}, s32[32,4]{0,1:T(4,128)}, u32[]{:S(2)}) copy-start(s32[32,4]{0,1:T(4,128)} %param.7) | copy-start | bytes 1540
  55.6 4.9 %copy-start.3 = (bf16[32,2048]{1,0:T(8,128)(2,1)S(1)}, bf16[32,2048]{1,0:T(8,128)(2,1)}, u32[]{:S(2)}) copy-start(bf16[32,2048]{1,0:T(8,128)(2,1)} %param.9) | copy-start | bytes 393220
  55.6 18.6 %all-to-all-start = ((bf16[4,96,2048]{2,1,0:T(8,128)(2,1)}), bf16[4,96,2048]{2,1,0:T(8,128)(2,1)S(1)}, u32[]{:S(2)}, u32[]{:S(2)}) async-start(bf16[4,96,2048]{2,1,0:T(8,128)(2,1)} %broadcast_in_dim.82), calls=%async_computation | async-start | bytes 3145728 | tf_op jit(solution)/shard_map/all_to_all | solution.py:23
  60.6 46.8 %copy-start.4 = (bf16[256,768]{1,0:T(8,128)(2,1)S(1)}, bf16[256,768]{1,0:T(8,128)(2,1)}, u32[]{:S(2)}) copy-start(bf16[256,768]{1,0:T(8,128)(2,1)} %param.5) | copy-start | bytes 1179652
  74.2 35.3 %copy-start.1 = (bf16[4,96,2048]{2,1,0:T(8,128)(2,1)}, bf16[4,96,2048]{2,1,0:T(8,128)(2,1)S(1)}, u32[]{:S(2)}) copy-start(bf16[4,96,2048]{2,1,0:T(8,128)(2,1)S(1)} %all-to-all-done) | copy-start | bytes 4718596
  74.2 51.3 %all-to-all-start.1 = ((bf16[16,16,2048]{2,1,0:T(8,128)(2,1)}), bf16[16,16,2048]{2,1,0:T(8,128)(2,1)S(1)}, u32[]{:S(2)}, u32[]{:S(2)}) async-start(bf16[16,16,2048]{2,1,0:T(8,128)(2,1)} %bitcast.124), calls=%async_computation.1 | async-start | bytes 2097152 | tf_op jit(solution)/shard_map/all_to_all | solution.py:23
  103.3 7.2 %collective-permute-start.1 = (bf16[384,2048]{1,0:T(8,128)(2,1)S(1)}, bf16[384,2048]{1,0:T(8,128)(2,1)}, u32[]{:S(2)}, u32[]{:S(2)}) collective-permute-start(bf16[384,2048]{1,0:T(8,128)(2,1)S(1)} %bitcast.121), channel_id=1, source_target_pairs={{0,32},{32,0},{1,33},{33,1},{2,34},{34,2},{3,35},{35,3},{4,36},{36... | collective-permute-start | bytes 4718600 | tf_op jit(solution)/shard_map/ppermute | solution.py:107
  125.5 71.8 %all-to-all-start.2 = ((bf16[16,16,2048]{2,1,0:T(8,128)(2,1)}), bf16[16,16,2048]{2,1,0:T(8,128)(2,1)S(1)}, u32[]{:S(2)}, u32[]{:S(2)}) async-start(bf16[16,16,2048]{2,1,0:T(8,128)(2,1)} %bitcast.24), calls=%async_computation.2 | async-start | bytes 2097152 | tf_op jit(solution)/shard_map/all_to_all | solution.py:23
  135.0 7.1 %collective-permute-start.3 = (bf16[384,2048]{1,0:T(8,128)(2,1)}, bf16[384,2048]{1,0:T(8,128)(2,1)}, u32[]{:S(2)}, u32[]{:S(2)}) collective-permute-start(bf16[384,2048]{1,0:T(8,128)(2,1)} %convolution_convert_fusion), channel_id=1, source_target_pairs={{0,32},{32,0},{1,33},{33,1},{2,34},{34,2},{3,35},{35,3},{4,36},{36... | collective-permute-start | bytes 4718600 | tf_op jit(solution)/shard_map/ppermute | solution.py:135
  144.1 10.1 %copy-start = (f32[384,2048]{1,0:T(8,128)}, f32[384,2048]{1,0:T(8,128)S(1)}, u32[]{:S(2)}) copy-start(f32[384,2048]{1,0:T(8,128)S(1)} %convert_add_fusion) | copy-start | bytes 9437188
  144.3 12.3 %collective-permute-start.6 = (bf16[96,2048]{1,0:T(8,128)(2,1)S(1)}, bf16[96,2048]{1,0:T(8,128)(2,1)}, u32[]{:S(2)}, u32[]{:S(2)}) collective-permute-start(bf16[96,2048]{1,0:T(8,128)(2,1)S(1)} %get-tuple-element.49), channel_id=1, source_target_pairs={{0,192},{64,0},{128,64},{192,128},{1,193},{65,1},{129,65},{193,129... | collective-permute-start | bytes 1179656 | tf_op jit(solution)/shard_map/ppermute | solution.py:82
  147.1 21.7 %collective-permute-start.5 = (bf16[96,2048]{1,0:T(8,128)(2,1)S(1)}, bf16[96,2048]{1,0:T(8,128)(2,1)}, u32[]{:S(2)}, u32[]{:S(2)}) collective-permute-start(bf16[96,2048]{1,0:T(8,128)(2,1)S(1)} %get-tuple-element.50), channel_id=1, source_target_pairs={{0,64},{64,128},{128,192},{192,0},{1,65},{65,129},{129,193},{193,1... | collective-permute-start | bytes 1179656 | tf_op jit(solution)/shard_map/ppermute | solution.py:82
  149.6 19.2 %collective-permute-start.4 = (bf16[96,2048]{1,0:T(8,128)(2,1)S(1)}, bf16[96,2048]{1,0:T(8,128)(2,1)}, u32[]{:S(2)}, u32[]{:S(2)}) collective-permute-start(bf16[96,2048]{1,0:T(8,128)(2,1)S(1)} %get-tuple-element.48), channel_id=1, source_target_pairs={{0,128},{64,192},{128,0},{192,64},{1,129},{65,193},{129,1},{193,65... | collective-permute-start | bytes 1179656 | tf_op jit(solution)/shard_map/ppermute | solution.py:82
  170.4 27.5 %copy-start.2 = (bf16[256,2048]{1,0:T(8,128)(2,1)S(1)}, bf16[256,2048]{1,0:T(8,128)(2,1)}, u32[]{:S(2)}) copy-start(bf16[256,2048]{1,0:T(8,128)(2,1)} %get-tuple-element.77) | copy-start | bytes 3145732
  171.2 29.5 %collective-permute-start.9 = (bf16[24,2048]{1,0:T(8,128)(2,1)}, bf16[24,2048]{1,0:T(8,128)(2,1)}, u32[]{:S(2)}, u32[]{:S(2)}) collective-permute-start(bf16[24,2048]{1,0:T(8,128)(2,1)} %get-tuple-element.52), channel_id=1, source_target_pairs={{0,768},{256,0},{512,256},{768,512},{1,769},{257,1},{513,257},{769... | collective-permute-start | bytes 294920 | tf_op jit(solution)/shard_map/ppermute | solution.py:82
  173.1 27.6 %collective-permute-start.8 = (bf16[24,2048]{1,0:T(8,128)(2,1)}, bf16[24,2048]{1,0:T(8,128)(2,1)}, u32[]{:S(2)}, u32[]{:S(2)}) collective-permute-start(bf16[24,2048]{1,0:T(8,128)(2,1)} %get-tuple-element.53), channel_id=1, source_target_pairs={{0,256},{256,512},{512,768},{768,0},{1,257},{257,513},{513,769},{7... | collective-permute-start | bytes 294920 | tf_op jit(solution)/shard_map/ppermute | solution.py:82
  185.2 25.1 %collective-permute-start.7 = (bf16[24,2048]{1,0:T(8,128)(2,1)S(1)}, bf16[24,2048]{1,0:T(8,128)(2,1)}, u32[]{:S(2)}, u32[]{:S(2)}) collective-permute-start(bf16[24,2048]{1,0:T(8,128)(2,1)S(1)} %get-tuple-element.51), channel_id=1, source_target_pairs={{0,512},{256,768},{512,0},{768,256},{1,513},{257,769},{513,1},{769... | collective-permute-start | bytes 294920 | tf_op jit(solution)/shard_map/ppermute | solution.py:82
  198.8 29.9 %collective-permute-start.2 = (bf16[32,2176]{1,0:T(8,128)(2,1)S(1)}, bf16[32,2176]{1,0:T(8,128)(2,1)S(1)}, u32[]{:S(2)}, u32[]{:S(2)}) collective-permute-start(bf16[32,2176]{1,0:T(8,128)(2,1)S(1)} %fusion.20), channel_id=1, source_target_pairs={{0,16},{16,0},{1,17},{17,1},{2,18},{18,2},{3,19},{19,3},{4,20},{20... | collective-permute-start | bytes 417800 | tf_op jit(solution)/shard_map/ppermute | solution.py:144

commit v4 on v3

--- a/solution.py
+++ b/solution.py
@@ -70,21 +70,26 @@
     return jnp.concatenate([rows, extra], axis=1)
 
 
+def forward(step):
+    return [(i, (i + step) % RING) for i in range(RING)]
+
+
+def gather(own, axis):
+    got = {4 - step: lax.ppermute(own, axis, forward(step)) for step in (2, 1, 3)}
+    return jnp.concatenate([own, got[1], got[2], got[3]], axis=0)
+
+
 def scatter(blocks, axis):
-    here = lax.axis_index(axis)
-
-    def block(step):
-        return lax.dynamic_index_in_dim(blocks, (here + step) & 3, 0, keepdims=False)
-
-    total = block(0).astype(F32)
+    total = blocks[0].astype(F32)
     for step in (2, 1, 3):
-        perm = [(i, (i + step) % RING) for i in range(RING)]
-        total = total + lax.ppermute(block(step).astype(BF16), axis, perm).astype(F32)
+        got = lax.ppermute(blocks[step].astype(BF16), axis, forward(step))
+        total = total + got.astype(F32)
     return total
 
 
-def gather(value, axis):
-    return lax.all_gather(value, axis, axis=0, tiled=True)
+def turned(blocks, dim, start):
+    twice = jnp.concatenate([blocks, blocks], axis=dim)
+    return lax.dynamic_slice_in_dim(twice, start, RING, dim)
 
 
 def per_device(hidden, w_down, ids, gates, cotangent):
@@ -94,16 +99,13 @@
     tokens, top = ids.shape
     rows, width = w_down.shape[1:]
     core, half = lax.axis_index(CORE), lax.axis_index(HALF)
+    zh, y = lax.axis_index(ZH), lax.axis_index(Y)
     part = RING * RING * rows
 
     columns = [ids.T.astype(BF16), *pieces_of(gates.T, 3)]
-    to_send, weight_rows = lax.optimization_barrier(
-        (beside(cotangent, columns), w_down.reshape(rows, width))
-    )
+    sent_on = lax.ppermute(beside(cotangent, columns), HALF, SWAP)
 
-    wz = gather(weight_rows, ZH)
-    sent_on = lax.ppermute(to_send, HALF, SWAP)
-    w_self = exchange(jnp.broadcast_to(wz[None], (RING, *wz.shape)), Y).reshape(part, width)
+    w_self = gather(gather(w_down.reshape(rows, width), ZH), Y)
     w_other = lax.ppermute(w_self, CORE, SWAP)
 
     extra = sent_on[:, width : width + 4 * top].astype(F32).T
@@ -116,20 +118,16 @@
     )
     picked = picked.astype(BF16)
     sent = (slot_gate * picked.astype(F32)).astype(BF16).reshape(groups, N_HALF * capacity, width)
-    sent, w_self = lax.optimization_barrier((sent, w_self))
     grads = exchange(sent, GRP).reshape(slots, width)
 
     hid = hidden.reshape(N_HALF, groups, capacity, inner)
     hid = jnp.where(half == 0, hid, hid[::-1]).transpose(1, 0, 2, 3).reshape(slots, inner)
     hid_t = hid.T.reshape(RING, RING, N_CORE, rows, slots).transpose(2, 1, 0, 3, 4)
+    hid_t = turned(turned(hid_t, 2, zh), 1, y)
     hid_t = hid_t.reshape(N_CORE, part, slots)
     hid_self = lax.dynamic_index_in_dim(hid_t, core, 0, keepdims=False)
     hid_other = lax.dynamic_index_in_dim(hid_t, 1 - core, 0, keepdims=False)
     hid_self, hid_other = lax.optimization_barrier((hid_self, hid_other))
-
-    out = dot(hid_self, w_self, ((0,), (0,))) + dot(hid_other, w_other, ((0,), (0,)))
-    out = out.astype(BF16).reshape(groups, N_HALF * capacity, width)
-    out, grads = lax.optimization_barrier((out, grads))
 
     for_other = dot(hid_other, grads, ((1,), (0,))).astype(BF16)
     got = lax.ppermute(for_other, CORE, SWAP)
@@ -138,6 +136,9 @@
     weight_grads = scatter(by_y.reshape(RING, rows, width), ZH)
     weight_grads = weight_grads.astype(BF16).reshape(1, rows, width)
 
+    out = dot(hid_self, w_self, ((0,), (0,))) + dot(hid_other, w_other, ((0,), (0,)))
+    out = out.astype(BF16).reshape(groups, N_HALF * capacity, width)
+    out, grads = lax.optimization_barrier((out, grads))
     back = exchange(out, GRP).reshape(slots, width)
     mixed, gate_grads = combine(back, fills, same, slot_gate, picked)
     passed = beside(mixed[tokens:].astype(BF16), pieces_of(gate_grads[:, tokens:], 2))
@@ -151,6 +152,7 @@
     low = jnp.where(core == 0, hg_self, hg_other)
     high = jnp.where(core == 0, hg_other, hg_self)
     hg = jnp.stack([low, high]).reshape(N_CORE, RING, RING, rows, slots)
+    hg = turned(turned(hg, 2, (RING - zh) % RING), 1, (RING - y) % RING)
     hg = hg.transpose(2, 1, 0, 3, 4).reshape(inner, slots).T
     hg = hg.reshape(groups, N_HALF, capacity, inner).transpose(1, 0, 2, 3)
     hidden_grads = jnp.where(half == 0, hg, hg[::-1]).reshape(slots, inner)

time: 232 us -> 265 us (1.14)
  the two profiles are of different devices: /device:TPU:1 before, /device:TPU:66 now
where the time goes in v4:
time: 265 us; the launch traced here: 264 us
  starting transfers between devices  128 us (48%)
  waiting for transfers between devices  97.2 us (37%)
  matrix products  17 us (6%)
  other arithmetic  11.1 us (4%)
  local copies, waits for them, and re-layouts  9.15 us (3%)
    ppermute x6, starting transfers between devices, gather(): lax.ppermute(own, axis, forward(step))  50.5 us
    ppermute x6, waiting for transfers between devices, scatter(): got = lax.ppermute(blocks[step].astype(BF16), axis, forward(step))  47.4 us
    ppermute x6, waiting for transfers between devices, gather(): lax.ppermute(own, axis, forward(step))  38.9 us
    ppermute x6, starting transfers between devices, scatter(): got = lax.ppermute(blocks[step].astype(BF16), axis, forward(step))  34 us
    all_to_all x2, starting transfers between devices, exchange(): return lax.all_to_all(rows, axis, split_axis=0, concat_axis=0, tiled=True)  19.5 us
    dot_general x10, matrix products, dot(): return lax.dot_general(a, b, (dims, ((), ())), preferred_element_type=F32)  17 us
    ppermute x1, starting transfers between devices, per_device(): passed = lax.ppermute(passed, HALF, SWAP)  11.4 us
    ppermute x1, starting transfers between devices, per_device(): sent_on = lax.ppermute(beside(cotangent, columns), HALF, SWAP)  9.1 us
  transfers between devices with their start and end apart: 18, of which 8 were waited for; matrix products, arithmetic and copies ran while one was open for 11% of the time, Pallas kernels for 0%

profile of v4, /device:TPU:66, one launch (start us, length us, event | category | flops | bytes accessed | tf_op | source)
XLA Modules:
  0.0 263.9 jit_solution(18132070233642864862)
XLA Ops:
  3.1 9.1 %collective-permute-start = (bf16[32,2176]{1,0:T(8,128)(2,1)S(1)}, bf16[32,2176]{1,0:T(8,128)(2,1)S(1)}, u32[]{:S(2)}, u32[]{:S(2)}) collective-permute-start(bf16[32,2176]{1,0:T(8,128)(2,1)S(1)} %fusion.22), channel_id=1, source_target_pairs={{0,16},{16,0},{1,17},{17,1},{2,18},{18,2},{3,19},{19,3},{4,20},{20... | collective-permute-start | bytes 417800 | tf_op jit(solution)/shard_map/ppermute | solution.py:106
  12.3 7.9 %collective-permute-done = bf16[32,2176]{1,0:T(8,128)(2,1)S(1)} collective-permute-done((bf16[32,2176]{1,0:T(8,128)(2,1)S(1)}, bf16[32,2176]{1,0:T(8,128)(2,1)S(1)}, u32[]{:S(2)}, u32[]{:S(2)}) %collective-permute-start) | collective-permute-done | bytes 139296 | tf_op jit(solution)/shard_map/ppermute | solution.py:106
  24.2 10.6 %all-to-all-start = ((bf16[16,16,2048]{2,1,0:T(8,128)(2,1)}), bf16[16,16,2048]{2,1,0:T(8,128)(2,1)S(1)}, u32[]{:S(2)}, u32[]{:S(2)}) async-start(bf16[16,16,2048]{2,1,0:T(8,128)(2,1)} %bitcast.23), calls=%async_computation | async-start | bytes 2097152 | tf_op jit(solution)/shard_map/all_to_all | solution.py:23
  34.8 19.5 %collective-permute-start.1 = (bf16[24,2048]{1,0:T(8,128)(2,1)S(1)}, bf16[24,2048]{1,0:T(8,128)(2,1)S(1)}, u32[]{:S(2)}, u32[]{:S(2)}) collective-permute-start(bf16[24,2048]{1,0:T(8,128)(2,1)S(1)} %bitcast.95), channel_id=1, source_target_pairs={{0,768},{256,0},{512,256},{768,512},{1,769},{257,1},{513,257},{769... | collective-permute-start | bytes 294920 | tf_op jit(solution)/shard_map/ppermute | solution.py:78
  54.4 8.3 %collective-permute-start.2 = (bf16[24,2048]{1,0:T(8,128)(2,1)S(1)}, bf16[24,2048]{1,0:T(8,128)(2,1)S(1)}, u32[]{:S(2)}, u32[]{:S(2)}) collective-permute-start(bf16[24,2048]{1,0:T(8,128)(2,1)S(1)} %bitcast.96), channel_id=1, source_target_pairs={{0,512},{256,768},{512,0},{768,256},{1,513},{257,769},{513,1},{769... | collective-permute-start | bytes 294920 | tf_op jit(solution)/shard_map/ppermute | solution.py:78
  62.7 12.2 %collective-permute-start.3 = (bf16[24,2048]{1,0:T(8,128)(2,1)S(1)}, bf16[24,2048]{1,0:T(8,128)(2,1)S(1)}, u32[]{:S(2)}, u32[]{:S(2)}) collective-permute-start(bf16[24,2048]{1,0:T(8,128)(2,1)S(1)} %bitcast.97), channel_id=1, source_target_pairs={{0,256},{256,512},{512,768},{768,0},{1,257},{257,513},{513,769},{7... | collective-permute-start | bytes 294920 | tf_op jit(solution)/shard_map/ppermute | solution.py:78
  75.5 26.5 %collective-permute-done.1 = bf16[24,2048]{1,0:T(8,128)(2,1)S(1)} collective-permute-done((bf16[24,2048]{1,0:T(8,128)(2,1)S(1)}, bf16[24,2048]{1,0:T(8,128)(2,1)S(1)}, u32[]{:S(2)}, u32[]{:S(2)}) %collective-permute-start.1) | collective-permute-done | bytes 98336 | tf_op jit(solution)/shard_map/ppermute | solution.py:78
  102.1 5.1 %collective-permute-start.4 = (bf16[96,2048]{1,0:T(8,128)(2,1)S(1)}, bf16[96,2048]{1,0:T(8,128)(2,1)S(1)}, u32[]{:S(2)}, u32[]{:S(2)}) collective-permute-start(bf16[96,2048]{1,0:T(8,128)(2,1)S(1)} %pad_maximum_fusion), channel_id=1, source_target_pairs={{0,192},{64,0},{128,64},{192,128},{1,193},{65,1},{129,65},{193,129... | collective-permute-start | bytes 1179656 | tf_op jit(solution)/shard_map/ppermute | solution.py:78
  107.2 2.5 collective-permute-start.5
  109.7 2.9 %collective-permute-start.6 = (bf16[96,2048]{1,0:T(8,128)(2,1)S(1)}, bf16[96,2048]{1,0:T(8,128)(2,1)S(1)}, u32[]{:S(2)}, u32[]{:S(2)}) collective-permute-start(bf16[96,2048]{1,0:T(8,128)(2,1)S(1)} %pad_maximum_fusion), channel_id=1, source_target_pairs={{0,64},{64,128},{128,192},{192,0},{1,65},{65,129},{129,193},{193,1... | collective-permute-start | bytes 1179656 | tf_op jit(solution)/shard_map/ppermute | solution.py:78
  114.6 8.4 %collective-permute-done.4 = bf16[96,2048]{1,0:T(8,128)(2,1)S(1)} collective-permute-done((bf16[96,2048]{1,0:T(8,128)(2,1)S(1)}, bf16[96,2048]{1,0:T(8,128)(2,1)S(1)}, u32[]{:S(2)}, u32[]{:S(2)}) %collective-permute-start.4) | collective-permute-done | bytes 393248 | tf_op jit(solution)/shard_map/ppermute | solution.py:78
  124.5 4.1 %collective-permute-done.6 = bf16[96,2048]{1,0:T(8,128)(2,1)S(1)} collective-permute-done((bf16[96,2048]{1,0:T(8,128)(2,1)S(1)}, bf16[96,2048]{1,0:T(8,128)(2,1)S(1)}, u32[]{:S(2)}, u32[]{:S(2)}) %collective-permute-start.6) | collective-permute-done | bytes 393248 | tf_op jit(solution)/shard_map/ppermute | solution.py:78
  129.3 1.9 collective-permute-start.7
  132.0 3.0 %collective-permute-done.7 = bf16[384,2048]{1,0:T(8,128)(2,1)} collective-permute-done((bf16[384,2048]{1,0:T(8,128)(2,1)}, bf16[384,2048]{1,0:T(8,128)(2,1)}, u32[]{:S(2)}, u32[]{:S(2)}) %collective-permute-start.7) | collective-permute-done | bytes 1572896 | tf_op jit(solution)/shard_map/ppermute | solution.py:109
  135.0 2.1 fusion.64
  137.1 3.1 %fusion = bf16[256,2048]{1,0:T(8,128)(2,1)} fusion(f32[256,2048]{1,0:T(8,128)S(1)} %fusion.64, bf16[384,256]{1,0:T(8,128)(2,1)S(1)} %get-tuple-element.8, bf16[384,2048]{1,0:T(8,128)(2,1)} %constant_dynamic-update-slice_fusion), kind=kOutput, calls=%fused_computation.5 | convolution fusion | flops 403701760 | bytes 4915200 | tf_op jit(solution)/shard_map/dot_general | solution.py:19
  140.2 8.9 %all-to-all-start.1 = ((bf16[16,16,2048]{2,1,0:T(8,128)(2,1)}), bf16[16,16,2048]{2,1,0:T(8,128)(2,1)S(1)}, u32[]{:S(2)}, u32[]{:S(2)}) async-start(bf16[16,16,2048]{2,1,0:T(8,128)(2,1)} %bitcast.22), calls=%async_computation.1 | async-start | bytes 2097152 | tf_op jit(solution)/shard_map/all_to_all | solution.py:23
  150.8 1.9 collective-permute-start.9
  152.8 2.0 convolution_convert_fusion.3
  154.8 2.0 broadcast_select_fusion
  156.8 3.6 %fusion.60 = (bf16[384,2048]{1,0:T(8,128)(2,1)S(1)}, f32[384,2048]{1,0:T(8,128)}) fusion(bf16[384,2048]{1,0:T(8,128)(2,1)} %collective-permute-done.9, bf16[384,256]{1,0:T(8,128)(2,1)S(1)} %get-tuple-element.8, bf16[256,2048]{1,0:T(8,128)(2,1)S(1)} %bitcast.88), kind=kOutput, calls=%fused_computation.152 | convolution fusion | flops 405012480 | bytes 7536640 | tf_op jit(solution)/shard_map/dot_general | solution.py:19
  161.5 2.5 collective-permute-start.12
  164.1 3.3 %collective-permute-start.11 = (bf16[96,2048]{1,0:T(8,128)(2,1)}, bf16[96,2048]{1,0:T(8,128)(2,1)}, u32[]{:S(2)}, u32[]{:S(2)}) collective-permute-start(bf16[96,2048]{1,0:T(8,128)(2,1)} %get-tuple-element.46), channel_id=1, source_target_pairs={{0,64},{64,128},{128,192},{192,0},{1,65},{65,129},{129,193},{193,1... | collective-permute-start | bytes 1179656 | tf_op jit(solution)/shard_map/ppermute | solution.py:85
  167.4 2.5 collective-permute-start.10
  171.4 4.2 %collective-permute-done.12 = bf16[96,2048]{1,0:T(8,128)(2,1)S(1)} collective-permute-done((bf16[96,2048]{1,0:T(8,128)(2,1)}, bf16[96,2048]{1,0:T(8,128)(2,1)S(1)}, u32[]{:S(2)}, u32[]{:S(2)}) %collective-permute-start.12) | collective-permute-done | bytes 393248 | tf_op jit(solution)/shard_map/ppermute | solution.py:85
  175.6 11.6 %collective-permute-done.11 = bf16[96,2048]{1,0:T(8,128)(2,1)} collective-permute-done((bf16[96,2048]{1,0:T(8,128)(2,1)}, bf16[96,2048]{1,0:T(8,128)(2,1)}, u32[]{:S(2)}, u32[]{:S(2)}) %collective-permute-start.11) | collective-permute-done | bytes 393248 | tf_op jit(solution)/shard_map/ppermute | solution.py:85
  187.2 2.5 fusion.58
  190.3 3.5 %collective-permute-start.15 = (bf16[24,2048]{1,0:T(8,128)(2,1)}, bf16[24,2048]{1,0:T(8,128)(2,1)S(1)}, u32[]{:S(2)}, u32[]{:S(2)}) collective-permute-start(bf16[24,2048]{1,0:T(8,128)(2,1)} %get-tuple-element.48), channel_id=1, source_target_pairs={{0,768},{256,0},{512,256},{768,512},{1,769},{257,1},{513,257},{769... | collective-permute-start | bytes 294920 | tf_op jit(solution)/shard_map/ppermute | solution.py:85
  193.8 11.0 %collective-permute-start.14 = (bf16[24,2048]{1,0:T(8,128)(2,1)S(1)}, bf16[24,2048]{1,0:T(8,128)(2,1)S(1)}, u32[]{:S(2)}, u32[]{:S(2)}) collective-permute-start(bf16[24,2048]{1,0:T(8,128)(2,1)S(1)} %get-tuple-element.49), channel_id=1, source_target_pairs={{0,256},{256,512},{512,768},{768,0},{1,257},{257,513},{513,769},{7... | collective-permute-start | bytes 294920 | tf_op jit(solution)/shard_map/ppermute | solution.py:85
  204.8 11.1 %collective-permute-start.13 = (bf16[24,2048]{1,0:T(8,128)(2,1)S(1)}, bf16[24,2048]{1,0:T(8,128)(2,1)}, u32[]{:S(2)}, u32[]{:S(2)}) collective-permute-start(bf16[24,2048]{1,0:T(8,128)(2,1)S(1)} %get-tuple-element.47), channel_id=1, source_target_pairs={{0,512},{256,768},{512,0},{768,256},{1,513},{257,769},{513,1},{769... | collective-permute-start | bytes 294920 | tf_op jit(solution)/shard_map/ppermute | solution.py:85
  217.8 11.4 %collective-permute-start.8 = (bf16[32,2176]{1,0:T(8,128)(2,1)S(1)}, bf16[32,2176]{1,0:T(8,128)(2,1)S(1)}, u32[]{:S(2)}, u32[]{:S(2)}) collective-permute-start(bf16[32,2176]{1,0:T(8,128)(2,1)S(1)} %fusion.23), channel_id=1, source_target_pairs={{0,16},{16,0},{1,17},{17,1},{2,18},{18,2},{3,19},{19,3},{4,20},{20... | collective-permute-start | bytes 417800 | tf_op jit(solution)/shard_map/ppermute | solution.py:145
  229.2 31.6 %collective-permute-done.13 = bf16[24,2048]{1,0:T(8,128)(2,1)} collective-permute-done((bf16[24,2048]{1,0:T(8,128)(2,1)S(1)}, bf16[24,2048]{1,0:T(8,128)(2,1)}, u32[]{:S(2)}, u32[]{:S(2)}) %collective-permute-start.13) | collective-permute-done | bytes 98336 | tf_op jit(solution)/shard_map/ppermute | solution.py:85
  (107 shorter events, 21.9 us)
Async XLA Ops:
  0.6 22.1 %copy-start = (bf16[32,2048]{1,0:T(8,128)(2,1)S(1)}, bf16[32,2048]{1,0:T(8,128)(2,1)}, u32[]{:S(2)}) copy-start(bf16[32,2048]{1,0:T(8,128)(2,1)} %param.9) | copy-start | bytes 393220
  3.1 17.1 %collective-permute-start = (bf16[32,2176]{1,0:T(8,128)(2,1)S(1)}, bf16[32,2176]{1,0:T(8,128)(2,1)S(1)}, u32[]{:S(2)}, u32[]{:S(2)}) collective-permute-start(bf16[32,2176]{1,0:T(8,128)(2,1)S(1)} %fusion.22), channel_id=1, source_target_pairs={{0,16},{16,0},{1,17},{17,1},{2,18},{18,2},{3,19},{19,3},{4,20},{20... | collective-permute-start | bytes 417800 | tf_op jit(solution)/shard_map/ppermute | solution.py:106
  12.2 9.7 %copy-start.15 = (s32[256]{0:T(256)}, s32[256]{0:T(256)S(1)}, u32[]{:S(2)}) copy-start(s32[256]{0:T(256)S(1)} %fusion.52) | copy-start | bytes 3076
  12.2 9.6 %copy-start.17 = (s32[64]{0:T(128)}, s32[64]{0:T(128)S(1)}, u32[]{:S(2)}) copy-start(s32[64]{0:T(128)S(1)} %and_select_fusion.1) | copy-start | bytes 772
  12.2 9.6 %copy-start.5 = (s32[256]{0:T(256)}, s32[256]{0:T(256)S(1)}, u32[]{:S(2)}) copy-start(s32[256]{0:T(256)S(1)} %get-tuple-element.74) | copy-start | bytes 3076
  22.7 1.5 copy-start.3
  24.2 10.6 %copy-start.1 = (bf16[1,24,2048]{2,1,0:T(8,128)(2,1)S(1)}, bf16[1,24,2048]{2,1,0:T(8,128)(2,1)}, u32[]{:S(2)}) copy-start(bf16[1,24,2048]{2,1,0:T(8,128)(2,1)} %param.6) | copy-start | bytes 294916
  24.2 116.0 %all-to-all-start = ((bf16[16,16,2048]{2,1,0:T(8,128)(2,1)}), bf16[16,16,2048]{2,1,0:T(8,128)(2,1)S(1)}, u32[]{:S(2)}, u32[]{:S(2)}) async-start(bf16[16,16,2048]{2,1,0:T(8,128)(2,1)} %bitcast.23), calls=%async_computation | async-start | bytes 2097152 | tf_op jit(solution)/shard_map/all_to_all | solution.py:23
  34.8 67.2 %collective-permute-start.1 = (bf16[24,2048]{1,0:T(8,128)(2,1)S(1)}, bf16[24,2048]{1,0:T(8,128)(2,1)S(1)}, u32[]{:S(2)}, u32[]{:S(2)}) collective-permute-start(bf16[24,2048]{1,0:T(8,128)(2,1)S(1)} %bitcast.95), channel_id=1, source_target_pairs={{0,768},{256,0},{512,256},{768,512},{1,769},{257,1},{513,257},{769... | collective-permute-start | bytes 294920 | tf_op jit(solution)/shard_map/ppermute | solution.py:78
  54.4 47.7 %collective-permute-start.2 = (bf16[24,2048]{1,0:T(8,128)(2,1)S(1)}, bf16[24,2048]{1,0:T(8,128)(2,1)S(1)}, u32[]{:S(2)}, u32[]{:S(2)}) collective-permute-start(bf16[24,2048]{1,0:T(8,128)(2,1)S(1)} %bitcast.96), channel_id=1, source_target_pairs={{0,512},{256,768},{512,0},{768,256},{1,513},{257,769},{513,1},{769... | collective-permute-start | bytes 294920 | tf_op jit(solution)/shard_map/ppermute | solution.py:78
  62.7 39.4 %collective-permute-start.3 = (bf16[24,2048]{1,0:T(8,128)(2,1)S(1)}, bf16[24,2048]{1,0:T(8,128)(2,1)S(1)}, u32[]{:S(2)}, u32[]{:S(2)}) collective-permute-start(bf16[24,2048]{1,0:T(8,128)(2,1)S(1)} %bitcast.97), channel_id=1, source_target_pairs={{0,256},{256,512},{512,768},{768,0},{1,257},{257,513},{513,769},{7... | collective-permute-start | bytes 294920 | tf_op jit(solution)/shard_map/ppermute | solution.py:78
  102.1 29.2 %copy-start.2 = (bf16[256,768]{1,0:T(8,128)(2,1)S(1)}, bf16[256,768]{1,0:T(8,128)(2,1)}, u32[]{:S(2)}) copy-start(bf16[256,768]{1,0:T(8,128)(2,1)} %param.5) | copy-start | bytes 1179652
  102.1 20.8 %collective-permute-start.4 = (bf16[96,2048]{1,0:T(8,128)(2,1)S(1)}, bf16[96,2048]{1,0:T(8,128)(2,1)S(1)}, u32[]{:S(2)}, u32[]{:S(2)}) collective-permute-start(bf16[96,2048]{1,0:T(8,128)(2,1)S(1)} %pad_maximum_fusion), channel_id=1, source_target_pairs={{0,192},{64,0},{128,64},{192,128},{1,193},{65,1},{129,65},{193,129... | collective-permute-start | bytes 1179656 | tf_op jit(solution)/shard_map/ppermute | solution.py:78
  107.2 16.6 %collective-permute-start.5 = (bf16[96,2048]{1,0:T(8,128)(2,1)S(1)}, bf16[96,2048]{1,0:T(8,128)(2,1)S(1)}, u32[]{:S(2)}, u32[]{:S(2)}) collective-permute-start(bf16[96,2048]{1,0:T(8,128)(2,1)S(1)} %pad_maximum_fusion), channel_id=1, source_target_pairs={{0,128},{64,192},{128,0},{192,64},{1,129},{65,193},{129,1},{193,65... | collective-permute-start | bytes 1179656 | tf_op jit(solution)/shard_map/ppermute | solution.py:78
  109.7 18.9 %collective-permute-start.6 = (bf16[96,2048]{1,0:T(8,128)(2,1)S(1)}, bf16[96,2048]{1,0:T(8,128)(2,1)S(1)}, u32[]{:S(2)}, u32[]{:S(2)}) collective-permute-start(bf16[96,2048]{1,0:T(8,128)(2,1)S(1)} %pad_maximum_fusion), channel_id=1, source_target_pairs={{0,64},{64,128},{128,192},{192,0},{1,65},{65,129},{129,193},{193,1... | collective-permute-start | bytes 1179656 | tf_op jit(solution)/shard_map/ppermute | solution.py:78
  129.3 5.6 %collective-permute-start.7 = (bf16[384,2048]{1,0:T(8,128)(2,1)}, bf16[384,2048]{1,0:T(8,128)(2,1)}, u32[]{:S(2)}, u32[]{:S(2)}) collective-permute-start(bf16[384,2048]{1,0:T(8,128)(2,1)} %constant_dynamic-update-slice_fusion), channel_id=1, source_target_pairs={{0,32},{32,0},{1,33},{33,1},{2,34},{34,2},{3,35},{35,3},{4,36},{36... | collective-permute-start | bytes 4718600 | tf_op jit(solution)/shard_map/ppermute | solution.py:109
  140.2 75.7 %all-to-all-start.1 = ((bf16[16,16,2048]{2,1,0:T(8,128)(2,1)}), bf16[16,16,2048]{2,1,0:T(8,128)(2,1)S(1)}, u32[]{:S(2)}, u32[]{:S(2)}) async-start(bf16[16,16,2048]{2,1,0:T(8,128)(2,1)} %bitcast.22), calls=%async_computation.1 | async-start | bytes 2097152 | tf_op jit(solution)/shard_map/all_to_all | solution.py:23
  150.8 6.0 %collective-permute-start.9 = (bf16[384,2048]{1,0:T(8,128)(2,1)}, bf16[384,2048]{1,0:T(8,128)(2,1)}, u32[]{:S(2)}, u32[]{:S(2)}) collective-permute-start(bf16[384,2048]{1,0:T(8,128)(2,1)} %convolution_convert_fusion), channel_id=1, source_target_pairs={{0,32},{32,0},{1,33},{33,1},{2,34},{34,2},{3,35},{35,3},{4,36},{36... | collective-permute-start | bytes 4718600 | tf_op jit(solution)/shard_map/ppermute | solution.py:133
  161.5 14.1 %collective-permute-start.12 = (bf16[96,2048]{1,0:T(8,128)(2,1)}, bf16[96,2048]{1,0:T(8,128)(2,1)S(1)}, u32[]{:S(2)}, u32[]{:S(2)}) collective-permute-start(bf16[96,2048]{1,0:T(8,128)(2,1)} %get-tuple-element.45), channel_id=1, source_target_pairs={{0,192},{64,0},{128,64},{192,128},{1,193},{65,1},{129,65},{193,129... | collective-permute-start | bytes 1179656 | tf_op jit(solution)/shard_map/ppermute | solution.py:85
  164.1 23.1 %collective-permute-start.11 = (bf16[96,2048]{1,0:T(8,128)(2,1)}, bf16[96,2048]{1,0:T(8,128)(2,1)}, u32[]{:S(2)}, u32[]{:S(2)}) collective-permute-start(bf16[96,2048]{1,0:T(8,128)(2,1)} %get-tuple-element.46), channel_id=1, source_target_pairs={{0,64},{64,128},{128,192},{192,0},{1,65},{65,129},{129,193},{193,1... | collective-permute-start | bytes 1179656 | tf_op jit(solution)/shard_map/ppermute | solution.py:85
  167.4 19.8 %collective-permute-start.10 = (bf16[96,2048]{1,0:T(8,128)(2,1)}, bf16[96,2048]{1,0:T(8,128)(2,1)}, u32[]{:S(2)}, u32[]{:S(2)}) collective-permute-start(bf16[96,2048]{1,0:T(8,128)(2,1)} %get-tuple-element.44), channel_id=1, source_target_pairs={{0,128},{64,192},{128,0},{192,64},{1,129},{65,193},{129,1},{193,65... | collective-permute-start | bytes 1179656 | tf_op jit(solution)/shard_map/ppermute | solution.py:85
  187.2 28.8 %copy-start.4 = (f32[256]{0:T(256)S(1)}, f32[256]{0:T(256)}, u32[]{:S(2)}) copy-start(f32[256]{0:T(256)} %copy-done.3) | copy-start | bytes 3076
  190.3 38.9 %collective-permute-start.15 = (bf16[24,2048]{1,0:T(8,128)(2,1)}, bf16[24,2048]{1,0:T(8,128)(2,1)S(1)}, u32[]{:S(2)}, u32[]{:S(2)}) collective-permute-start(bf16[24,2048]{1,0:T(8,128)(2,1)} %get-tuple-element.48), channel_id=1, source_target_pairs={{0,768},{256,0},{512,256},{768,512},{1,769},{257,1},{513,257},{769... | collective-permute-start | bytes 294920 | tf_op jit(solution)/shard_map/ppermute | solution.py:85
  193.8 35.4 %collective-permute-start.14 = (bf16[24,2048]{1,0:T(8,128)(2,1)S(1)}, bf16[24,2048]{1,0:T(8,128)(2,1)S(1)}, u32[]{:S(2)}, u32[]{:S(2)}) collective-permute-start(bf16[24,2048]{1,0:T(8,128)(2,1)S(1)} %get-tuple-element.49), channel_id=1, source_target_pairs={{0,256},{256,512},{512,768},{768,0},{1,257},{257,513},{513,769},{7... | collective-permute-start | bytes 294920 | tf_op jit(solution)/shard_map/ppermute | solution.py:85
  204.8 55.9 %collective-permute-start.13 = (bf16[24,2048]{1,0:T(8,128)(2,1)S(1)}, bf16[24,2048]{1,0:T(8,128)(2,1)}, u32[]{:S(2)}, u32[]{:S(2)}) collective-permute-start(bf16[24,2048]{1,0:T(8,128)(2,1)S(1)} %get-tuple-element.47), channel_id=1, source_target_pairs={{0,512},{256,768},{512,0},{768,256},{1,513},{257,769},{513,1},{769... | collective-permute-start | bytes 294920 | tf_op jit(solution)/shard_map/ppermute | solution.py:85
  216.6 0.7 copy-start.6
  216.6 0.7 copy-start.8
  216.6 0.7 copy-start.12
  216.6 0.7 copy-start.14
  216.6 0.7 copy-start.16
  216.6 0.7 copy-start.18
  217.8 44.7 %collective-permute-start.8 = (bf16[32,2176]{1,0:T(8,128)(2,1)S(1)}, bf16[32,2176]{1,0:T(8,128)(2,1)S(1)}, u32[]{:S(2)}, u32[]{:S(2)}) collective-permute-start(bf16[32,2176]{1,0:T(8,128)(2,1)S(1)} %fusion.23), channel_id=1, source_target_pairs={{0,16},{16,0},{1,17},{17,1},{2,18},{18,2},{3,19},{19,3},{4,20},{20... | collective-permute-start | bytes 417800 | tf_op jit(solution)/shard_map/ppermute | solution.py:145
  (5 other events, 3.0 us)

commit v5 on v4

--- a/solution.py
+++ b/solution.py
@@ -76,15 +76,17 @@
 
 def gather(own, axis):
     got = {4 - step: lax.ppermute(own, axis, forward(step)) for step in (2, 1, 3)}
-    return jnp.concatenate([own, got[1], got[2], got[3]], axis=0)
+    return [own, got[1], got[2], got[3]]
 
 
 def scatter(blocks, axis):
-    total = blocks[0].astype(F32)
-    for step in (2, 1, 3):
-        got = lax.ppermute(blocks[step].astype(BF16), axis, forward(step))
-        total = total + got.astype(F32)
-    return total
+    return [blocks[0]] + [
+        lax.ppermute(blocks[step].astype(BF16), axis, forward(step)) for step in (2, 1, 3)
+    ]
+
+
+def total(parts):
+    return sum((p.astype(F32) for p in parts[1:]), parts[0].astype(F32))
 
 
 def turned(blocks, dim, start):
@@ -105,8 +107,8 @@
     columns = [ids.T.astype(BF16), *pieces_of(gates.T, 3)]
     sent_on = lax.ppermute(beside(cotangent, columns), HALF, SWAP)
 
-    w_self = gather(gather(w_down.reshape(rows, width), ZH), Y)
-    w_other = lax.ppermute(w_self, CORE, SWAP)
+    wz = jnp.concatenate(gather(w_down.reshape(rows, width), ZH), axis=0)
+    wy = gather(wz, Y)
 
     extra = sent_on[:, width : width + 4 * top].astype(F32).T
     ids_both = jnp.concatenate([ids.T, extra[:top].astype(jnp.int32)], axis=1)
@@ -132,17 +134,21 @@
     for_other = dot(hid_other, grads, ((1,), (0,))).astype(BF16)
     got = lax.ppermute(for_other, CORE, SWAP)
     kept = dot(hid_self, grads, ((1,), (0,))) + got.astype(F32)
-    by_y = scatter(kept.reshape(RING, RING * rows, width), Y)
-    weight_grads = scatter(by_y.reshape(RING, rows, width), ZH)
-    weight_grads = weight_grads.astype(BF16).reshape(1, rows, width)
+    by_y = total(scatter(kept.reshape(RING, RING * rows, width), Y))
+    by_z = scatter(by_y.reshape(RING, rows, width), ZH)
 
+    wy, kept = lax.optimization_barrier((wy, kept))
+    w_self = jnp.concatenate(wy, axis=0)
+    w_other = lax.ppermute(w_self, CORE, SWAP)
     out = dot(hid_self, w_self, ((0,), (0,))) + dot(hid_other, w_other, ((0,), (0,)))
     out = out.astype(BF16).reshape(groups, N_HALF * capacity, width)
     out, grads = lax.optimization_barrier((out, grads))
     back = exchange(out, GRP).reshape(slots, width)
     mixed, gate_grads = combine(back, fills, same, slot_gate, picked)
     passed = beside(mixed[tokens:].astype(BF16), pieces_of(gate_grads[:, tokens:], 2))
+    passed, by_z[0] = lax.optimization_barrier((passed, by_z[0]))
     passed = lax.ppermute(passed, HALF, SWAP)
+    weight_grads = total(by_z).astype(BF16).reshape(1, rows, width)
     mixed = (mixed[:tokens] + passed[:, :width].astype(F32)).astype(BF16)
     extra = passed[:, width : width + 2 * top].astype(F32)
     gate_grads = gate_grads[:, :tokens].T + extra[:, :top] + extra[:, top:]

time: 265 us -> 266 us (level)
  the two profiles are of different devices: /device:TPU:66 before, /device:TPU:1 now
where the time goes in v5:
time: 266 us; the launch traced here: 263 us
  starting transfers between devices  143 us (54%)
  waiting for transfers between devices  92.5 us (35%)
  other arithmetic  10.2 us (4%)
  matrix products  9.35 us (4%)
  local copies, waits for them, and re-layouts  6.95 us (3%)
    ppermute x6, starting transfers between devices, gather(): lax.ppermute(own, axis, forward(step))  48.2 us
    ppermute x6, starting transfers between devices, scatter(): lax.ppermute(blocks[step].astype(BF16), axis, forward(step))  44.4 us
    all_to_all x2, starting transfers between devices, exchange(): return lax.all_to_all(rows, axis, split_axis=0, concat_axis=0, tiled=True)  28.2 us
    ppermute x6, waiting for transfers between devices, scatter(): lax.ppermute(blocks[step].astype(BF16), axis, forward(step))  23.5 us
    ppermute x6, waiting for transfers between devices, gather(): lax.ppermute(own, axis, forward(step))  23 us
    all_to_all x2, waiting for transfers between devices, exchange(): return lax.all_to_all(rows, axis, split_axis=0, concat_axis=0, tiled=True)  21.8 us
    ppermute x1, waiting for transfers between devices, per_device(): sent_on = lax.ppermute(beside(cotangent, columns), HALF, SWAP)  11.3 us
    ppermute x1, waiting for transfers between devices, per_device(): passed = lax.ppermute(passed, HALF, SWAP)  9.81 us
  transfers between devices with their start and end apart: 18, of which 12 were waited for; matrix products, arithmetic and copies ran while one was open for 5% of the time, Pallas kernels for 0%

profile of v5, /device:TPU:1, one launch (start us, length us, event | category | flops | bytes accessed | tf_op | source)
XLA Modules:
  0.0 263.2 jit_solution(4865270796219263146)
XLA Ops:
  3.1 9.6 %collective-permute-start = (bf16[32,2176]{1,0:T(8,128)(2,1)S(1)}, bf16[32,2176]{1,0:T(8,128)(2,1)S(1)}, u32[]{:S(2)}, u32[]{:S(2)}) collective-permute-start(bf16[32,2176]{1,0:T(8,128)(2,1)S(1)} %fusion.19), channel_id=1, source_target_pairs={{0,16},{16,0},{1,17},{17,1},{2,18},{18,2},{3,19},{19,3},{4,20},{20... | collective-permute-start | bytes 417800 | tf_op jit(solution)/shard_map/ppermute | solution.py:108
  12.8 11.3 %collective-permute-done = bf16[32,2176]{1,0:T(8,128)(2,1)S(1)} collective-permute-done((bf16[32,2176]{1,0:T(8,128)(2,1)S(1)}, bf16[32,2176]{1,0:T(8,128)(2,1)S(1)}, u32[]{:S(2)}, u32[]{:S(2)}) %collective-permute-start) | collective-permute-done | bytes 139296 | tf_op jit(solution)/shard_map/ppermute | solution.py:108
  27.6 7.9 %all-to-all-start = ((bf16[16,16,2048]{2,1,0:T(8,128)(2,1)}), bf16[16,16,2048]{2,1,0:T(8,128)(2,1)S(1)}, u32[]{:S(2)}, u32[]{:S(2)}) async-start(bf16[16,16,2048]{2,1,0:T(8,128)(2,1)} %bitcast.22), calls=%async_computation | async-start | bytes 2097152 | tf_op jit(solution)/shard_map/all_to_all | solution.py:23
  36.2 21.8 %all-to-all-done = bf16[16,16,2048]{2,1,0:T(8,128)(2,1)S(1)} async-done(((bf16[16,16,2048]{2,1,0:T(8,128)(2,1)}), bf16[16,16,2048]{2,1,0:T(8,128)(2,1)S(1)}, u32[]{:S(2)}, u32[]{:S(2)}) %all-to-all-start) | async-done | bytes 1048608 | tf_op jit(solution)/shard_map/all_to_all | solution.py:23
  58.7 4.9 %collective-permute-start.7 = (bf16[384,2048]{1,0:T(8,128)(2,1)S(1)}, bf16[384,2048]{1,0:T(8,128)(2,1)S(1)}, u32[]{:S(2)}, u32[]{:S(2)}) collective-permute-start(bf16[384,2048]{1,0:T(8,128)(2,1)S(1)} %convolution_convert_fusion), channel_id=1, source_target_pairs={{0,32},{32,0},{1,33},{33,1},{2,34},{34,2},{3,35},{35,3},{4,36},{36... | collective-permute-start | bytes 4718600 | tf_op jit(solution)/shard_map/ppermute | solution.py:135
  63.5 18.8 %collective-permute-start.1 = (bf16[24,2048]{1,0:T(8,128)(2,1)S(1)}, bf16[24,2048]{1,0:T(8,128)(2,1)S(1)}, u32[]{:S(2)}, u32[]{:S(2)}) collective-permute-start(bf16[24,2048]{1,0:T(8,128)(2,1)S(1)} %bitcast.98), channel_id=1, source_target_pairs={{0,768},{256,0},{512,256},{768,512},{1,769},{257,1},{513,257},{769... | collective-permute-start | bytes 294920 | tf_op jit(solution)/shard_map/ppermute | solution.py:78
  82.3 8.5 %collective-permute-start.2 = (bf16[24,2048]{1,0:T(8,128)(2,1)S(1)}, bf16[24,2048]{1,0:T(8,128)(2,1)S(1)}, u32[]{:S(2)}, u32[]{:S(2)}) collective-permute-start(bf16[24,2048]{1,0:T(8,128)(2,1)S(1)} %bitcast.99), channel_id=1, source_target_pairs={{0,512},{256,768},{512,0},{768,256},{1,513},{257,769},{513,1},{769... | collective-permute-start | bytes 294920 | tf_op jit(solution)/shard_map/ppermute | solution.py:78
  90.8 11.5 %collective-permute-start.3 = (bf16[24,2048]{1,0:T(8,128)(2,1)S(1)}, bf16[24,2048]{1,0:T(8,128)(2,1)S(1)}, u32[]{:S(2)}, u32[]{:S(2)}) collective-permute-start(bf16[24,2048]{1,0:T(8,128)(2,1)S(1)} %bitcast.100), channel_id=1, source_target_pairs={{0,256},{256,512},{512,768},{768,0},{1,257},{257,513},{513,769},{7... | collective-permute-start | bytes 294920 | tf_op jit(solution)/shard_map/ppermute | solution.py:78
  102.3 4.9 %collective-permute-done.2 = bf16[24,2048]{1,0:T(8,128)(2,1)S(1)} collective-permute-done((bf16[24,2048]{1,0:T(8,128)(2,1)S(1)}, bf16[24,2048]{1,0:T(8,128)(2,1)S(1)}, u32[]{:S(2)}, u32[]{:S(2)}) %collective-permute-start.2) | collective-permute-done | bytes 98336 | tf_op jit(solution)/shard_map/ppermute | solution.py:78
  107.2 2.9 %collective-permute-done.3 = bf16[24,2048]{1,0:T(8,128)(2,1)S(1)} collective-permute-done((bf16[24,2048]{1,0:T(8,128)(2,1)S(1)}, bf16[24,2048]{1,0:T(8,128)(2,1)S(1)}, u32[]{:S(2)}, u32[]{:S(2)}) %collective-permute-start.3) | collective-permute-done | bytes 98336 | tf_op jit(solution)/shard_map/ppermute | solution.py:78
  110.2 4.6 %collective-permute-start.4 = (bf16[96,2048]{1,0:T(8,128)(2,1)S(1)}, bf16[96,2048]{1,0:T(8,128)(2,1)S(1)}, u32[]{:S(2)}, u32[]{:S(2)}) collective-permute-start(bf16[96,2048]{1,0:T(8,128)(2,1)S(1)} %pad_maximum_fusion), channel_id=1, source_target_pairs={{0,192},{64,0},{128,64},{192,128},{1,193},{65,1},{129,65},{193,129... | collective-permute-start | bytes 1179656 | tf_op jit(solution)/shard_map/ppermute | solution.py:78
  114.8 2.3 collective-permute-start.5
  117.1 2.6 collective-permute-start.6
  119.7 2.7 %fusion.57 = (bf16[384,2048]{1,0:T(8,128)(2,1)}, f32[384,2048]{1,0:T(8,128)}) fusion(bf16[384,2048]{1,0:T(8,128)(2,1)S(1)} %collective-permute-done.7, bf16[384,256]{1,0:T(8,128)(2,1)S(1)} %get-tuple-element.14, bf16[256,2048]{1,0:T(8,128)(2,1)S(1)} %bitcast.85), kind=kOutput, calls=%fused_computation.146 | convolution fusion | flops 405012480 | bytes 7536640 | tf_op jit(solution)/shard_map/dot_general | solution.py:19
  122.5 3.7 %collective-permute-done.5 = bf16[96,2048]{1,0:T(8,128)(2,1)S(1)} collective-permute-done((bf16[96,2048]{1,0:T(8,128)(2,1)S(1)}, bf16[96,2048]{1,0:T(8,128)(2,1)S(1)}, u32[]{:S(2)}, u32[]{:S(2)}) %collective-permute-start.5) | collective-permute-done | bytes 393248 | tf_op jit(solution)/shard_map/ppermute | solution.py:78
  126.2 11.4 %collective-permute-done.6 = bf16[96,2048]{1,0:T(8,128)(2,1)S(1)} collective-permute-done((bf16[96,2048]{1,0:T(8,128)(2,1)S(1)}, bf16[96,2048]{1,0:T(8,128)(2,1)S(1)}, u32[]{:S(2)}, u32[]{:S(2)}) %collective-permute-start.6) | collective-permute-done | bytes 393248 | tf_op jit(solution)/shard_map/ppermute | solution.py:78
  137.8 2.5 collective-permute-start.8
  140.3 3.0 %collective-permute-done.8 = bf16[384,2048]{1,0:T(8,128)(2,1)S(1)} collective-permute-done((bf16[384,2048]{1,0:T(8,128)(2,1)S(1)}, bf16[384,2048]{1,0:T(8,128)(2,1)S(1)}, u32[]{:S(2)}, u32[]{:S(2)}) %collective-permute-start.8) | collective-permute-done | bytes 1572896 | tf_op jit(solution)/shard_map/ppermute | solution.py:142
  145.2 1.8 fusion
  147.0 20.3 %all-to-all-start.1 = ((bf16[16,16,2048]{2,1,0:T(8,128)(2,1)}), bf16[16,16,2048]{2,1,0:T(8,128)(2,1)S(1)}, u32[]{:S(2)}, u32[]{:S(2)}) async-start(bf16[16,16,2048]{2,1,0:T(8,128)(2,1)} %bitcast.24), calls=%async_computation.1 | async-start | bytes 2097152 | tf_op jit(solution)/shard_map/all_to_all | solution.py:23
  167.4 2.3 fusion.58
  169.6 1.9 collective-permute-start.10
  171.6 4.6 %collective-permute-start.11 = (bf16[96,2048]{1,0:T(8,128)(2,1)}, bf16[96,2048]{1,0:T(8,128)(2,1)}, u32[]{:S(2)}, u32[]{:S(2)}) collective-permute-start(bf16[96,2048]{1,0:T(8,128)(2,1)} %get-tuple-element.57), channel_id=1, source_target_pairs={{0,192},{64,0},{128,64},{192,128},{1,193},{65,1},{129,65},{193,129... | collective-permute-start | bytes 1179656 | tf_op jit(solution)/shard_map/ppermute | solution.py:84
  176.1 1.9 collective-permute-start.9
  178.1 5.3 %collective-permute-done.10 = bf16[96,2048]{1,0:T(8,128)(2,1)S(1)} collective-permute-done((bf16[96,2048]{1,0:T(8,128)(2,1)}, bf16[96,2048]{1,0:T(8,128)(2,1)S(1)}, u32[]{:S(2)}, u32[]{:S(2)}) %collective-permute-start.10) | collective-permute-done | bytes 393248 | tf_op jit(solution)/shard_map/ppermute | solution.py:84
  184.7 5.6 %collective-permute-done.9 = bf16[96,2048]{1,0:T(8,128)(2,1)} collective-permute-done((bf16[96,2048]{1,0:T(8,128)(2,1)}, bf16[96,2048]{1,0:T(8,128)(2,1)}, u32[]{:S(2)}, u32[]{:S(2)}) %collective-permute-start.9) | collective-permute-done | bytes 393248 | tf_op jit(solution)/shard_map/ppermute | solution.py:84
  192.6 22.0 %collective-permute-start.13 = (bf16[24,2048]{1,0:T(8,128)(2,1)}, bf16[24,2048]{1,0:T(8,128)(2,1)}, u32[]{:S(2)}, u32[]{:S(2)}) collective-permute-start(bf16[24,2048]{1,0:T(8,128)(2,1)} %get-tuple-element.59), channel_id=1, source_target_pairs={{0,512},{256,768},{512,0},{768,256},{1,513},{257,769},{513,1},{769... | collective-permute-start | bytes 294920 | tf_op jit(solution)/shard_map/ppermute | solution.py:84
  214.6 1.9 collective-permute-start.14
  216.5 12.1 %collective-permute-start.15 = (bf16[24,2048]{1,0:T(8,128)(2,1)}, bf16[24,2048]{1,0:T(8,128)(2,1)}, u32[]{:S(2)}, u32[]{:S(2)}) collective-permute-start(bf16[24,2048]{1,0:T(8,128)(2,1)} %get-tuple-element.60), channel_id=1, source_target_pairs={{0,768},{256,0},{512,256},{768,512},{1,769},{257,1},{513,257},{769... | collective-permute-start | bytes 294920 | tf_op jit(solution)/shard_map/ppermute | solution.py:84
  233.9 4.9 %collective-permute-start.12 = (bf16[32,2176]{1,0:T(8,128)(2,1)S(1)}, bf16[32,2176]{1,0:T(8,128)(2,1)S(1)}, u32[]{:S(2)}, u32[]{:S(2)}) collective-permute-start(bf16[32,2176]{1,0:T(8,128)(2,1)S(1)} %fusion.20), channel_id=1, source_target_pairs={{0,16},{16,0},{1,17},{17,1},{2,18},{18,2},{3,19},{19,3},{4,20},{20... | collective-permute-start | bytes 417800 | tf_op jit(solution)/shard_map/ppermute | solution.py:150
  238.9 11.3 %collective-permute-done.15 = bf16[24,2048]{1,0:T(8,128)(2,1)} collective-permute-done((bf16[24,2048]{1,0:T(8,128)(2,1)}, bf16[24,2048]{1,0:T(8,128)(2,1)}, u32[]{:S(2)}, u32[]{:S(2)}) %collective-permute-start.15) | collective-permute-done | bytes 98336 | tf_op jit(solution)/shard_map/ppermute | solution.py:84
  252.0 9.8 %collective-permute-done.12 = bf16[32,2176]{1,0:T(8,128)(2,1)S(1)} collective-permute-done((bf16[32,2176]{1,0:T(8,128)(2,1)S(1)}, bf16[32,2176]{1,0:T(8,128)(2,1)S(1)}, u32[]{:S(2)}, u32[]{:S(2)}) %collective-permute-start.12) | collective-permute-done | bytes 139296 | tf_op jit(solution)/shard_map/ppermute | solution.py:150
  (113 shorter events, 21.0 us)
Async XLA Ops:
  0.6 25.5 %copy-start.4 = (bf16[32,2048]{1,0:T(8,128)(2,1)S(1)}, bf16[32,2048]{1,0:T(8,128)(2,1)}, u32[]{:S(2)}) copy-start(bf16[32,2048]{1,0:T(8,128)(2,1)} %param.9) | copy-start | bytes 393220
  3.1 21.0 %collective-permute-start = (bf16[32,2176]{1,0:T(8,128)(2,1)S(1)}, bf16[32,2176]{1,0:T(8,128)(2,1)S(1)}, u32[]{:S(2)}, u32[]{:S(2)}) collective-permute-start(bf16[32,2176]{1,0:T(8,128)(2,1)S(1)} %fusion.19), channel_id=1, source_target_pairs={{0,16},{16,0},{1,17},{17,1},{2,18},{18,2},{3,19},{19,3},{4,20},{20... | collective-permute-start | bytes 417800 | tf_op jit(solution)/shard_map/ppermute | solution.py:108
  12.7 13.0 %copy-start.19 = (s32[256]{0:T(256)}, s32[256]{0:T(256)S(1)}, u32[]{:S(2)}) copy-start(s32[256]{0:T(256)S(1)} %fusion.49) | copy-start | bytes 3076
  12.8 13.0 %copy-start.21 = (s32[64]{0:T(128)}, s32[64]{0:T(128)S(1)}, u32[]{:S(2)}) copy-start(s32[64]{0:T(128)S(1)} %and_select_fusion.1) | copy-start | bytes 772
  12.8 13.0 %copy-start.9 = (s32[256]{0:T(256)}, s32[256]{0:T(256)S(1)}, u32[]{:S(2)}) copy-start(s32[256]{0:T(256)S(1)} %get-tuple-element.86) | copy-start | bytes 3076
  25.0 0.8 copy-start.15
  25.0 0.8 copy-start.17
  26.1 1.5 copy-start.7
  27.6 7.9 %copy-start.5 = (bf16[256,768]{1,0:T(8,128)(2,1)S(1)}, bf16[256,768]{1,0:T(8,128)(2,1)}, u32[]{:S(2)}) copy-start(bf16[256,768]{1,0:T(8,128)(2,1)} %param.5) | copy-start | bytes 1179652
  27.6 30.5 %all-to-all-start = ((bf16[16,16,2048]{2,1,0:T(8,128)(2,1)}), bf16[16,16,2048]{2,1,0:T(8,128)(2,1)S(1)}, u32[]{:S(2)}, u32[]{:S(2)}) async-start(bf16[16,16,2048]{2,1,0:T(8,128)(2,1)} %bitcast.22), calls=%async_computation | async-start | bytes 2097152 | tf_op jit(solution)/shard_map/all_to_all | solution.py:23
  36.2 27.3 %copy-start.6 = (bf16[1,24,2048]{2,1,0:T(8,128)(2,1)S(1)}, bf16[1,24,2048]{2,1,0:T(8,128)(2,1)}, u32[]{:S(2)}) copy-start(bf16[1,24,2048]{2,1,0:T(8,128)(2,1)} %param.6) | copy-start | bytes 294916
  58.7 61.1 %collective-permute-start.7 = (bf16[384,2048]{1,0:T(8,128)(2,1)S(1)}, bf16[384,2048]{1,0:T(8,128)(2,1)S(1)}, u32[]{:S(2)}, u32[]{:S(2)}) collective-permute-start(bf16[384,2048]{1,0:T(8,128)(2,1)S(1)} %convolution_convert_fusion), channel_id=1, source_target_pairs={{0,32},{32,0},{1,33},{33,1},{2,34},{34,2},{3,35},{35,3},{4,36},{36... | collective-permute-start | bytes 4718600 | tf_op jit(solution)/shard_map/ppermute | solution.py:135
  63.5 38.8 %collective-permute-start.1 = (bf16[24,2048]{1,0:T(8,128)(2,1)S(1)}, bf16[24,2048]{1,0:T(8,128)(2,1)S(1)}, u32[]{:S(2)}, u32[]{:S(2)}) collective-permute-start(bf16[24,2048]{1,0:T(8,128)(2,1)S(1)} %bitcast.98), channel_id=1, source_target_pairs={{0,768},{256,0},{512,256},{768,512},{1,769},{257,1},{513,257},{769... | collective-permute-start | bytes 294920 | tf_op jit(solution)/shard_map/ppermute | solution.py:78
  82.3 24.9 %collective-permute-start.2 = (bf16[24,2048]{1,0:T(8,128)(2,1)S(1)}, bf16[24,2048]{1,0:T(8,128)(2,1)S(1)}, u32[]{:S(2)}, u32[]{:S(2)}) collective-permute-start(bf16[24,2048]{1,0:T(8,128)(2,1)S(1)} %bitcast.99), channel_id=1, source_target_pairs={{0,512},{256,768},{512,0},{768,256},{1,513},{257,769},{513,1},{769... | collective-permute-start | bytes 294920 | tf_op jit(solution)/shard_map/ppermute | solution.py:78
  90.8 19.4 %collective-permute-start.3 = (bf16[24,2048]{1,0:T(8,128)(2,1)S(1)}, bf16[24,2048]{1,0:T(8,128)(2,1)S(1)}, u32[]{:S(2)}, u32[]{:S(2)}) collective-permute-start(bf16[24,2048]{1,0:T(8,128)(2,1)S(1)} %bitcast.100), channel_id=1, source_target_pairs={{0,256},{256,512},{512,768},{768,0},{1,257},{257,513},{513,769},{7... | collective-permute-start | bytes 294920 | tf_op jit(solution)/shard_map/ppermute | solution.py:78
  110.2 12.3 %collective-permute-start.4 = (bf16[96,2048]{1,0:T(8,128)(2,1)S(1)}, bf16[96,2048]{1,0:T(8,128)(2,1)S(1)}, u32[]{:S(2)}, u32[]{:S(2)}) collective-permute-start(bf16[96,2048]{1,0:T(8,128)(2,1)S(1)} %pad_maximum_fusion), channel_id=1, source_target_pairs={{0,192},{64,0},{128,64},{192,128},{1,193},{65,1},{129,65},{193,129... | collective-permute-start | bytes 1179656 | tf_op jit(solution)/shard_map/ppermute | solution.py:78
  114.8 11.3 %collective-permute-start.5 = (bf16[96,2048]{1,0:T(8,128)(2,1)S(1)}, bf16[96,2048]{1,0:T(8,128)(2,1)S(1)}, u32[]{:S(2)}, u32[]{:S(2)}) collective-permute-start(bf16[96,2048]{1,0:T(8,128)(2,1)S(1)} %pad_maximum_fusion), channel_id=1, source_target_pairs={{0,128},{64,192},{128,0},{192,64},{1,129},{65,193},{129,1},{193,65... | collective-permute-start | bytes 1179656 | tf_op jit(solution)/shard_map/ppermute | solution.py:78
  117.1 20.5 %collective-permute-start.6 = (bf16[96,2048]{1,0:T(8,128)(2,1)S(1)}, bf16[96,2048]{1,0:T(8,128)(2,1)S(1)}, u32[]{:S(2)}, u32[]{:S(2)}) collective-permute-start(bf16[96,2048]{1,0:T(8,128)(2,1)S(1)} %pad_maximum_fusion), channel_id=1, source_target_pairs={{0,64},{64,128},{128,192},{192,0},{1,65},{65,129},{129,193},{193,1... | collective-permute-start | bytes 1179656 | tf_op jit(solution)/shard_map/ppermute | solution.py:78
  137.8 7.5 %copy-start = (bf16[384,2048]{1,0:T(8,128)(2,1)}, bf16[384,2048]{1,0:T(8,128)(2,1)S(1)}, u32[]{:S(2)}) copy-start(bf16[384,2048]{1,0:T(8,128)(2,1)S(1)} %constant_dynamic-update-slice_fusion) | copy-start | bytes 4718596
  137.8 5.5 %collective-permute-start.8 = (bf16[384,2048]{1,0:T(8,128)(2,1)S(1)}, bf16[384,2048]{1,0:T(8,128)(2,1)S(1)}, u32[]{:S(2)}, u32[]{:S(2)}) collective-permute-start(bf16[384,2048]{1,0:T(8,128)(2,1)S(1)} %constant_dynamic-update-slice_fusion), channel_id=1, source_target_pairs={{0,32},{32,0},{1,33},{33,1},{2,34},{34,2},{3,35},{35,3},{4,36},{36... | collective-permute-start | bytes 4718600 | tf_op jit(solution)/shard_map/ppermute | solution.py:142
  143.3 1.2 copy-start.2
  147.0 85.1 %all-to-all-start.1 = ((bf16[16,16,2048]{2,1,0:T(8,128)(2,1)}), bf16[16,16,2048]{2,1,0:T(8,128)(2,1)S(1)}, u32[]{:S(2)}, u32[]{:S(2)}) async-start(bf16[16,16,2048]{2,1,0:T(8,128)(2,1)} %bitcast.24), calls=%async_computation.1 | async-start | bytes 2097152 | tf_op jit(solution)/shard_map/all_to_all | solution.py:23
  169.6 13.8 %collective-permute-start.10 = (bf16[96,2048]{1,0:T(8,128)(2,1)}, bf16[96,2048]{1,0:T(8,128)(2,1)S(1)}, u32[]{:S(2)}, u32[]{:S(2)}) collective-permute-start(bf16[96,2048]{1,0:T(8,128)(2,1)} %get-tuple-element.58), channel_id=1, source_target_pairs={{0,64},{64,128},{128,192},{192,0},{1,65},{65,129},{129,193},{193,1... | collective-permute-start | bytes 1179656 | tf_op jit(solution)/shard_map/ppermute | solution.py:84
  171.6 13.1 %collective-permute-start.11 = (bf16[96,2048]{1,0:T(8,128)(2,1)}, bf16[96,2048]{1,0:T(8,128)(2,1)}, u32[]{:S(2)}, u32[]{:S(2)}) collective-permute-start(bf16[96,2048]{1,0:T(8,128)(2,1)} %get-tuple-element.57), channel_id=1, source_target_pairs={{0,192},{64,0},{128,64},{192,128},{1,193},{65,1},{129,65},{193,129... | collective-permute-start | bytes 1179656 | tf_op jit(solution)/shard_map/ppermute | solution.py:84
  176.1 14.1 %collective-permute-start.9 = (bf16[96,2048]{1,0:T(8,128)(2,1)}, bf16[96,2048]{1,0:T(8,128)(2,1)}, u32[]{:S(2)}, u32[]{:S(2)}) collective-permute-start(bf16[96,2048]{1,0:T(8,128)(2,1)} %get-tuple-element.56), channel_id=1, source_target_pairs={{0,128},{64,192},{128,0},{192,64},{1,129},{65,193},{129,1},{193,65... | collective-permute-start | bytes 1179656 | tf_op jit(solution)/shard_map/ppermute | solution.py:84
  178.1 50.5 %copy-start.1 = (bf16[384,2048]{1,0:T(8,128)(2,1)S(1)}, bf16[384,2048]{1,0:T(8,128)(2,1)}, u32[]{:S(2)}) copy-start(bf16[384,2048]{1,0:T(8,128)(2,1)} %copy-done) | copy-start | bytes 4718596
  192.6 46.3 %collective-permute-start.13 = (bf16[24,2048]{1,0:T(8,128)(2,1)}, bf16[24,2048]{1,0:T(8,128)(2,1)}, u32[]{:S(2)}, u32[]{:S(2)}) collective-permute-start(bf16[24,2048]{1,0:T(8,128)(2,1)} %get-tuple-element.59), channel_id=1, source_target_pairs={{0,512},{256,768},{512,0},{768,256},{1,513},{257,769},{513,1},{769... | collective-permute-start | bytes 294920 | tf_op jit(solution)/shard_map/ppermute | solution.py:84
  214.6 24.3 %collective-permute-start.14 = (bf16[24,2048]{1,0:T(8,128)(2,1)}, bf16[24,2048]{1,0:T(8,128)(2,1)}, u32[]{:S(2)}, u32[]{:S(2)}) collective-permute-start(bf16[24,2048]{1,0:T(8,128)(2,1)} %get-tuple-element.61), channel_id=1, source_target_pairs={{0,256},{256,512},{512,768},{768,0},{1,257},{257,513},{513,769},{7... | collective-permute-start | bytes 294920 | tf_op jit(solution)/shard_map/ppermute | solution.py:84
  216.5 33.7 %collective-permute-start.15 = (bf16[24,2048]{1,0:T(8,128)(2,1)}, bf16[24,2048]{1,0:T(8,128)(2,1)}, u32[]{:S(2)}, u32[]{:S(2)}) collective-permute-start(bf16[24,2048]{1,0:T(8,128)(2,1)} %get-tuple-element.60), channel_id=1, source_target_pairs={{0,768},{256,0},{512,256},{768,512},{1,769},{257,1},{513,257},{769... | collective-permute-start | bytes 294920 | tf_op jit(solution)/shard_map/ppermute | solution.py:84
  228.6 1.4 copy-start.3
  231.0 1.1 copy-start.8
  233.9 27.9 %collective-permute-start.12 = (bf16[32,2176]{1,0:T(8,128)(2,1)S(1)}, bf16[32,2176]{1,0:T(8,128)(2,1)S(1)}, u32[]{:S(2)}, u32[]{:S(2)}) collective-permute-start(bf16[32,2176]{1,0:T(8,128)(2,1)S(1)} %fusion.20), channel_id=1, source_target_pairs={{0,16},{16,0},{1,17},{17,1},{2,18},{18,2},{3,19},{19,3},{4,20},{20... | collective-permute-start | bytes 417800 | tf_op jit(solution)/shard_map/ppermute | solution.py:150
  (9 other events, 6.2 us)

commit v6 on v5

--- a/solution.py
+++ b/solution.py
@@ -103,6 +103,7 @@
     core, half = lax.axis_index(CORE), lax.axis_index(HALF)
     zh, y = lax.axis_index(ZH), lax.axis_index(Y)
     part = RING * RING * rows
+    half_slots = slots // 2
 
     columns = [ids.T.astype(BF16), *pieces_of(gates.T, 3)]
     sent_on = lax.ppermute(beside(cotangent, columns), HALF, SWAP)
@@ -122,14 +123,29 @@
     sent = (slot_gate * picked.astype(F32)).astype(BF16).reshape(groups, N_HALF * capacity, width)
     grads = exchange(sent, GRP).reshape(slots, width)
 
-    hid = hidden.reshape(N_HALF, groups, capacity, inner)
-    hid = jnp.where(half == 0, hid, hid[::-1]).transpose(1, 0, 2, 3).reshape(slots, inner)
-    hid_t = hid.T.reshape(RING, RING, N_CORE, rows, slots).transpose(2, 1, 0, 3, 4)
-    hid_t = turned(turned(hid_t, 2, zh), 1, y)
-    hid_t = hid_t.reshape(N_CORE, part, slots)
-    hid_self = lax.dynamic_index_in_dim(hid_t, core, 0, keepdims=False)
-    hid_other = lax.dynamic_index_in_dim(hid_t, 1 - core, 0, keepdims=False)
-    hid_self, hid_other = lax.optimization_barrier((hid_self, hid_other))
+    hid = hidden.reshape(N_HALF, half_slots, inner)
+    hid = jnp.where(half == 0, hid, hid[::-1])
+
+    def by_place(rows_of):
+        cut = rows_of.T.reshape(RING, RING, N_CORE, rows, slots).transpose(2, 1, 0, 3, 4)
+        cut = turned(turned(cut, 2, zh), 1, y).reshape(N_CORE, part, slots)
+        return tuple(
+            lax.dynamic_index_in_dim(cut, c, 0, keepdims=False) for c in (core, 1 - core)
+        )
+
+    hid_p = by_place(hid.reshape(slots, inner))
+    hid = hid.reshape(N_HALF, groups, capacity, inner).transpose(1, 0, 2, 3)
+    hid_self, hid_other = by_place(hid.reshape(slots, inner))
+
+    def share(source):
+        def cut(v):
+            return v.reshape(groups, N_HALF, capacity, -1)[:, source].reshape(half_slots, -1)
+
+        mine = slice(source * tokens, (source + 1) * tokens)
+        return cut(fills)[:, mine], [cut(v)[:, mine] for v in same], cut(slot_gate), cut(picked)
+
+    early = (hid_p, hid_self, hid_other, share(0), share(1))
+    hid_p, hid_self, hid_other, share_own, share_par = lax.optimization_barrier(early)
 
     for_other = dot(hid_other, grads, ((1,), (0,))).astype(BF16)
     got = lax.ppermute(for_other, CORE, SWAP)
@@ -137,21 +153,29 @@
     by_y = total(scatter(kept.reshape(RING, RING * rows, width), Y))
     by_z = scatter(by_y.reshape(RING, rows, width), ZH)
 
-    wy, kept = lax.optimization_barrier((wy, kept))
     w_self = jnp.concatenate(wy, axis=0)
     w_other = lax.ppermute(w_self, CORE, SWAP)
-    out = dot(hid_self, w_self, ((0,), (0,))) + dot(hid_other, w_other, ((0,), (0,)))
-    out = out.astype(BF16).reshape(groups, N_HALF * capacity, width)
-    out, grads = lax.optimization_barrier((out, grads))
-    back = exchange(out, GRP).reshape(slots, width)
-    mixed, gate_grads = combine(back, fills, same, slot_gate, picked)
-    passed = beside(mixed[tokens:].astype(BF16), pieces_of(gate_grads[:, tokens:], 2))
+
+    def project(lo):
+        own, other = (h[:, lo : lo + half_slots] for h in hid_p)
+        out = dot(own, w_self, ((0,), (0,))) + dot(other, w_other, ((0,), (0,)))
+        return out.astype(BF16).reshape(groups, capacity, width)
+
+    out_par, grads = lax.optimization_barrier((project(half_slots), grads))
+    back_par = exchange(out_par, GRP)
+    out_own, back_par = lax.optimization_barrier((project(0), back_par))
+    back_own = exchange(out_own, GRP).reshape(half_slots, width)
+    passed, gg = combine(back_par.reshape(half_slots, width), *share_par)
+    passed = beside(passed.astype(BF16), pieces_of(gg, 2))
     passed, by_z[0] = lax.optimization_barrier((passed, by_z[0]))
+    back_own, _ = lax.optimization_barrier((back_own, passed))
     passed = lax.ppermute(passed, HALF, SWAP)
+    mixed, gg = combine(back_own, *share_own)
+    passed, mixed, gg = lax.optimization_barrier((passed, mixed, gg))
+    mixed = (mixed + passed[:, :width].astype(F32)).astype(BF16)
+    extra = passed[:, width : width + 2 * top].astype(F32)
+    gate_grads = gg.T + extra[:, :top] + extra[:, top:]
     weight_grads = total(by_z).astype(BF16).reshape(1, rows, width)
-    mixed = (mixed[:tokens] + passed[:, :width].astype(F32)).astype(BF16)
-    extra = passed[:, width : width + 2 * top].astype(F32)
-    gate_grads = gate_grads[:, :tokens].T + extra[:, :top] + extra[:, top:]
 
     hg_self = dot(w_self, grads, ((1,), (1,))).astype(BF16)
     hg_other = dot(w_other, grads, ((1,), (1,))).astype(BF16)

time: 266 us -> 267 us (level)
  waiting for transfers between devices: 92.5 us -> 73.2 us
  matrix products: 9.35 us -> 20.6 us
  local copies, waits for them, and re-layouts: 6.95 us -> 14.5 us
  starting transfers between devices: 143 us -> 146 us
    all_to_all x2 -> x3, waiting for transfers between devices: 21.8 us -> 2.97 us  [exchange(): return lax.all_to_all(rows, axis, split_axis=0, concat_axis=0, tiled=True)]
    ppermute x1, waiting for transfers between devices: 9.81 us -> 23.2 us  [per_device(): passed = lax.ppermute(passed, HALF, SWAP)]
    ppermute x6, waiting for transfers between devices: 23.5 us -> 11.7 us  [scatter(): lax.ppermute(blocks[step].astype(BF16), axis, forward(step))]
    all_to_all x2 -> x3, starting transfers between devices: 28.2 us -> 39.7 us  [exchange(): return lax.all_to_all(rows, axis, split_axis=0, concat_axis=0, tiled=True)]
    ppermute x6, starting transfers between devices: 44.4 us -> 33.1 us  [scatter(): lax.ppermute(blocks[step].astype(BF16), axis, forward(step))]
    dot_general x10 -> x14, matrix products: 9.35 us -> 20.6 us  [dot(): return lax.dot_general(a, b, (dims, ((), ())), preferred_element_type=F32)]
    ppermute x1, starting transfers between devices: 4.94 us -> 11.1 us  [per_device(): passed = lax.ppermute(passed, HALF, SWAP)]
    another operation x0 -> x7, local copies, waits for them, and re-layouts: none -> 5.45 us  [cut(): v.reshape(groups, N_HALF, capacity, -1)[:, source].reshape(half_slots, -1)]
  transfers between devices with their start and end apart: 18 -> 19, of which waited for: 12 -> 12; matrix products, arithmetic and copies ran while one was open for 5% -> 14% of each run, Pallas kernels for 0% -> 0%
where the time goes in v6:
time: 267 us; the launch traced here: 266 us
  starting transfers between devices  146 us (55%)
  waiting for transfers between devices  73.2 us (27%)
  matrix products  20.6 us (8%)
  local copies, waits for them, and re-layouts  14.5 us (5%)
  other arithmetic  10.2 us (4%)
    ppermute x6, starting transfers between devices, gather(): lax.ppermute(own, axis, forward(step))  48.2 us
    all_to_all x3, starting transfers between devices, exchange(): return lax.all_to_all(rows, axis, split_axis=0, concat_axis=0, tiled=True)  39.7 us
    ppermute x6, starting transfers between devices, scatter(): lax.ppermute(blocks[step].astype(BF16), axis, forward(step))  33.1 us
    ppermute x6, waiting for transfers between devices, gather(): lax.ppermute(own, axis, forward(step))  24 us
    ppermute x1, waiting for transfers between devices, per_device(): passed = lax.ppermute(passed, HALF, SWAP)  23.2 us
    dot_general x14, matrix products, dot(): return lax.dot_general(a, b, (dims, ((), ())), preferred_element_type=F32)  20.6 us
    ppermute x6, waiting for transfers between devices, scatter(): lax.ppermute(blocks[step].astype(BF16), axis, forward(step))  11.7 us
    ppermute x1, waiting for transfers between devices, per_device(): sent_on = lax.ppermute(beside(cotangent, columns), HALF, SWAP)  11.3 us
  transfers between devices with their start and end apart: 19, of which 12 were waited for; matrix products, arithmetic and copies ran while one was open for 14% of the time, Pallas kernels for 0%

profile of v6, /device:TPU:1, one launch (start us, length us, event | category | flops | bytes accessed | tf_op | source)
XLA Modules:
  0.0 266.2 jit_solution(12611453068103856562)
XLA Ops:
  3.1 9.6 %collective-permute-start = (bf16[32,2176]{1,0:T(8,128)(2,1)S(1)}, bf16[32,2176]{1,0:T(8,128)(2,1)S(1)}, u32[]{:S(2)}, u32[]{:S(2)}) collective-permute-start(bf16[32,2176]{1,0:T(8,128)(2,1)S(1)} %fusion.24), channel_id=1, source_target_pairs={{0,16},{16,0},{1,17},{17,1},{2,18},{18,2},{3,19},{19,3},{4,20},{20... | collective-permute-start | bytes 417800 | tf_op jit(solution)/shard_map/ppermute | solution.py:109
  12.8 11.3 %collective-permute-done = bf16[32,2176]{1,0:T(8,128)(2,1)S(1)} collective-permute-done((bf16[32,2176]{1,0:T(8,128)(2,1)S(1)}, bf16[32,2176]{1,0:T(8,128)(2,1)S(1)}, u32[]{:S(2)}, u32[]{:S(2)}) %collective-permute-start) | collective-permute-done | bytes 139296 | tf_op jit(solution)/shard_map/ppermute | solution.py:109
  27.8 7.9 %all-to-all-start = ((bf16[16,16,2048]{2,1,0:T(8,128)(2,1)}), bf16[16,16,2048]{2,1,0:T(8,128)(2,1)S(1)}, u32[]{:S(2)}, u32[]{:S(2)}) async-start(bf16[16,16,2048]{2,1,0:T(8,128)(2,1)} %bitcast.47), calls=%async_computation | async-start | bytes 2097152 | tf_op jit(solution)/shard_map/all_to_all | solution.py:23
  35.7 18.8 %collective-permute-start.1 = (bf16[24,2048]{1,0:T(8,128)(2,1)S(1)}, bf16[24,2048]{1,0:T(8,128)(2,1)S(1)}, u32[]{:S(2)}, u32[]{:S(2)}) collective-permute-start(bf16[24,2048]{1,0:T(8,128)(2,1)S(1)} %bitcast.159), channel_id=1, source_target_pairs={{0,768},{256,0},{512,256},{768,512},{1,769},{257,1},{513,257},{769... | collective-permute-start | bytes 294920 | tf_op jit(solution)/shard_map/ppermute | solution.py:78
  54.5 8.5 %collective-permute-start.2 = (bf16[24,2048]{1,0:T(8,128)(2,1)S(1)}, bf16[24,2048]{1,0:T(8,128)(2,1)S(1)}, u32[]{:S(2)}, u32[]{:S(2)}) collective-permute-start(bf16[24,2048]{1,0:T(8,128)(2,1)S(1)} %bitcast.160), channel_id=1, source_target_pairs={{0,512},{256,768},{512,0},{768,256},{1,513},{257,769},{513,1},{769... | collective-permute-start | bytes 294920 | tf_op jit(solution)/shard_map/ppermute | solution.py:78
  63.0 11.5 %collective-permute-start.3 = (bf16[24,2048]{1,0:T(8,128)(2,1)S(1)}, bf16[24,2048]{1,0:T(8,128)(2,1)}, u32[]{:S(2)}, u32[]{:S(2)}) collective-permute-start(bf16[24,2048]{1,0:T(8,128)(2,1)S(1)} %bitcast.161), channel_id=1, source_target_pairs={{0,256},{256,512},{512,768},{768,0},{1,257},{257,513},{513,769},{7... | collective-permute-start | bytes 294920 | tf_op jit(solution)/shard_map/ppermute | solution.py:78
  76.6 2.1 collective-permute-done.2
  78.7 4.9 %collective-permute-done.3 = bf16[24,2048]{1,0:T(8,128)(2,1)} collective-permute-done((bf16[24,2048]{1,0:T(8,128)(2,1)S(1)}, bf16[24,2048]{1,0:T(8,128)(2,1)}, u32[]{:S(2)}, u32[]{:S(2)}) %collective-permute-start.3) | collective-permute-done | bytes 98336 | tf_op jit(solution)/shard_map/ppermute | solution.py:78
  84.5 4.6 %collective-permute-start.4 = (bf16[96,2048]{1,0:T(8,128)(2,1)S(1)}, bf16[96,2048]{1,0:T(8,128)(2,1)S(1)}, u32[]{:S(2)}, u32[]{:S(2)}) collective-permute-start(bf16[96,2048]{1,0:T(8,128)(2,1)S(1)} %pad_maximum_fusion), channel_id=1, source_target_pairs={{0,192},{64,0},{128,64},{192,128},{1,193},{65,1},{129,65},{193,129... | collective-permute-start | bytes 1179656 | tf_op jit(solution)/shard_map/ppermute | solution.py:78
  89.1 2.3 collective-permute-start.5
  91.4 2.6 collective-permute-start.6
  94.9 2.8 %collective-permute-done.4 = bf16[96,2048]{1,0:T(8,128)(2,1)S(1)} collective-permute-done((bf16[96,2048]{1,0:T(8,128)(2,1)S(1)}, bf16[96,2048]{1,0:T(8,128)(2,1)S(1)}, u32[]{:S(2)}, u32[]{:S(2)}) %collective-permute-start.4) | collective-permute-done | bytes 393248 | tf_op jit(solution)/shard_map/ppermute | solution.py:78
  97.8 4.3 %collective-permute-done.5 = bf16[96,2048]{1,0:T(8,128)(2,1)S(1)} collective-permute-done((bf16[96,2048]{1,0:T(8,128)(2,1)S(1)}, bf16[96,2048]{1,0:T(8,128)(2,1)S(1)}, u32[]{:S(2)}, u32[]{:S(2)}) %collective-permute-start.5) | collective-permute-done | bytes 393248 | tf_op jit(solution)/shard_map/ppermute | solution.py:78
  102.1 9.9 %collective-permute-done.6 = bf16[96,2048]{1,0:T(8,128)(2,1)S(1)} collective-permute-done((bf16[96,2048]{1,0:T(8,128)(2,1)S(1)}, bf16[96,2048]{1,0:T(8,128)(2,1)S(1)}, u32[]{:S(2)}, u32[]{:S(2)}) %collective-permute-start.6) | collective-permute-done | bytes 393248 | tf_op jit(solution)/shard_map/ppermute | solution.py:78
  112.0 2.4 collective-permute-start.7
  120.9 2.3 slice_bitcast_fusion
  126.3 27.2 %all-to-all-start.1 = ((bf16[16,8,2048]{2,1,0:T(8,128)(2,1)}), bf16[16,8,2048]{2,1,0:T(8,128)(2,1)S(1)}, u32[]{:S(2)}, u32[]{:S(2)}) async-start(bf16[16,8,2048]{2,1,0:T(8,128)(2,1)} %fusion.2), calls=%async_computation.1 | async-start | bytes 1048576 | tf_op jit(solution)/shard_map/all_to_all | solution.py:23
  153.6 2.7 convolution_convert_fusion
  156.2 2.2 collective-permute-start.8
  158.4 1.9 fusion.30
  162.3 2.8 %broadcast_select_fusion = (bf16[384,256]{1,0:T(8,128)(2,1)}, bf16[384,256]{1,0:T(8,128)(2,1)}) fusion(bf16[384,256]{1,0:T(8,128)(2,1)S(1)} %convolution_convert_fusion.3, pred[]{:T(512)S(6)} %eq.188, bf16[384,2048]{1,0:T(8,128)(2,1)} %collective-permute-done.7, bf16[256,2048]{1,0:T(8,128)(2,1)S(1)} %bitcast.142), kind=kOutput, calls=%fused_computation.68 | convolution fusion | flops 402948096 | bytes 3211265 | tf_op jit(solution)/shard_map/dot_general | solution.py:19
  165.1 3.0 %all-to-all-done.1 = bf16[16,8,2048]{2,1,0:T(8,128)(2,1)S(1)} async-done(((bf16[16,8,2048]{2,1,0:T(8,128)(2,1)}), bf16[16,8,2048]{2,1,0:T(8,128)(2,1)S(1)}, u32[]{:S(2)}, u32[]{:S(2)}) %all-to-all-start.1) | async-done | bytes 524320 | tf_op jit(solution)/shard_map/all_to_all | solution.py:23
  168.0 4.6 %all-to-all-start.2 = ((bf16[16,8,2048]{2,1,0:T(8,128)(2,1)}), bf16[16,8,2048]{2,1,0:T(8,128)(2,1)S(1)}, u32[]{:S(2)}, u32[]{:S(2)}) async-start(bf16[16,8,2048]{2,1,0:T(8,128)(2,1)} %fusion.3), calls=%async_computation.2 | async-start | bytes 1048576 | tf_op jit(solution)/shard_map/all_to_all | solution.py:23
  172.7 3.6 %fusion.84 = (bf16[384,2048]{1,0:T(8,128)(2,1)S(1)}, f32[384,2048]{1,0:T(8,128)}) fusion(bf16[384,2048]{1,0:T(8,128)(2,1)} %collective-permute-done.8, bf16[384,256]{1,0:T(8,128)(2,1)S(1)} %get-tuple-element.43, bf16[256,2048]{1,0:T(8,128)(2,1)S(1)} %bitcast.143), kind=kOutput, calls=%fused_computation.216 | convolution fusion | flops 405012480 | bytes 7536640 | tf_op jit(solution)/shard_map/dot_general | solution.py:19
  179.2 4.6 %collective-permute-start.11 = (bf16[96,2048]{1,0:T(8,128)(2,1)}, bf16[96,2048]{1,0:T(8,128)(2,1)S(1)}, u32[]{:S(2)}, u32[]{:S(2)}) collective-permute-start(bf16[96,2048]{1,0:T(8,128)(2,1)} %get-tuple-element.99), channel_id=1, source_target_pairs={{0,192},{64,0},{128,64},{192,128},{1,193},{65,1},{129,65},{193,129... | collective-permute-start | bytes 1179656 | tf_op jit(solution)/shard_map/ppermute | solution.py:84
  187.2 2.3 collective-permute-done.10
  191.2 5.9 %collective-permute-done.9 = bf16[96,2048]{1,0:T(8,128)(2,1)} collective-permute-done((bf16[96,2048]{1,0:T(8,128)(2,1)S(1)}, bf16[96,2048]{1,0:T(8,128)(2,1)}, u32[]{:S(2)}, u32[]{:S(2)}) %collective-permute-start.9) | collective-permute-done | bytes 393248 | tf_op jit(solution)/shard_map/ppermute | solution.py:84
  199.7 10.7 %collective-permute-start.13 = (bf16[24,2048]{1,0:T(8,128)(2,1)}, bf16[24,2048]{1,0:T(8,128)(2,1)S(1)}, u32[]{:S(2)}, u32[]{:S(2)}) collective-permute-start(bf16[24,2048]{1,0:T(8,128)(2,1)} %get-tuple-element.103), channel_id=1, source_target_pairs={{0,512},{256,768},{512,0},{768,256},{1,513},{257,769},{513,1},{769... | collective-permute-start | bytes 294920 | tf_op jit(solution)/shard_map/ppermute | solution.py:84
  210.3 4.3 %collective-permute-start.14 = (bf16[24,2048]{1,0:T(8,128)(2,1)}, bf16[24,2048]{1,0:T(8,128)(2,1)S(1)}, u32[]{:S(2)}, u32[]{:S(2)}) collective-permute-start(bf16[24,2048]{1,0:T(8,128)(2,1)} %get-tuple-element.105), channel_id=1, source_target_pairs={{0,256},{256,512},{512,768},{768,0},{1,257},{257,513},{513,769},{7... | collective-permute-start | bytes 294920 | tf_op jit(solution)/shard_map/ppermute | solution.py:84
  214.7 9.6 %collective-permute-start.15 = (bf16[24,2048]{1,0:T(8,128)(2,1)}, bf16[24,2048]{1,0:T(8,128)(2,1)S(1)}, u32[]{:S(2)}, u32[]{:S(2)}) collective-permute-start(bf16[24,2048]{1,0:T(8,128)(2,1)} %get-tuple-element.104), channel_id=1, source_target_pairs={{0,768},{256,0},{512,256},{768,512},{1,769},{257,1},{513,257},{769... | collective-permute-start | bytes 294920 | tf_op jit(solution)/shard_map/ppermute | solution.py:84
  226.8 11.1 %collective-permute-start.12 = (bf16[32,2176]{1,0:T(8,128)(2,1)S(1)}, bf16[32,2176]{1,0:T(8,128)(2,1)S(1)}, u32[]{:S(2)}, u32[]{:S(2)}) collective-permute-start(bf16[32,2176]{1,0:T(8,128)(2,1)S(1)} %fusion.25), channel_id=1, source_target_pairs={{0,16},{16,0},{1,17},{17,1},{2,18},{18,2},{3,19},{19,3},{4,20},{20... | collective-permute-start | bytes 417800 | tf_op jit(solution)/shard_map/ppermute | solution.py:172
  241.5 23.2 %collective-permute-done.12 = bf16[32,2176]{1,0:T(8,128)(2,1)S(1)} collective-permute-done((bf16[32,2176]{1,0:T(8,128)(2,1)S(1)}, bf16[32,2176]{1,0:T(8,128)(2,1)S(1)}, u32[]{:S(2)}, u32[]{:S(2)}) %collective-permute-start.12) | collective-permute-done | bytes 139296 | tf_op jit(solution)/shard_map/ppermute | solution.py:172
  (147 shorter events, 39.3 us)
Async XLA Ops:
  0.6 25.4 %copy-start.4 = (bf16[32,2048]{1,0:T(8,128)(2,1)S(1)}, bf16[32,2048]{1,0:T(8,128)(2,1)}, u32[]{:S(2)}) copy-start(bf16[32,2048]{1,0:T(8,128)(2,1)} %param.9) | copy-start | bytes 393220
  3.1 21.0 %collective-permute-start = (bf16[32,2176]{1,0:T(8,128)(2,1)S(1)}, bf16[32,2176]{1,0:T(8,128)(2,1)S(1)}, u32[]{:S(2)}, u32[]{:S(2)}) collective-permute-start(bf16[32,2176]{1,0:T(8,128)(2,1)S(1)} %fusion.24), channel_id=1, source_target_pairs={{0,16},{16,0},{1,17},{17,1},{2,18},{18,2},{3,19},{19,3},{4,20},{20... | collective-permute-start | bytes 417800 | tf_op jit(solution)/shard_map/ppermute | solution.py:109
  12.8 15.1 %copy-start.22 = (s32[64]{0:T(128)}, s32[64]{0:T(128)S(1)}, u32[]{:S(2)}) copy-start(s32[64]{0:T(128)S(1)} %and_select_fusion.1) | copy-start | bytes 772
  27.8 46.7 %copy-start.2 = (bf16[256,768]{1,0:T(8,128)(2,1)S(1)}, bf16[256,768]{1,0:T(8,128)(2,1)}, u32[]{:S(2)}) copy-start(bf16[256,768]{1,0:T(8,128)(2,1)} %param.5) | copy-start | bytes 1179652
  27.8 98.5 %all-to-all-start = ((bf16[16,16,2048]{2,1,0:T(8,128)(2,1)}), bf16[16,16,2048]{2,1,0:T(8,128)(2,1)S(1)}, u32[]{:S(2)}, u32[]{:S(2)}) async-start(bf16[16,16,2048]{2,1,0:T(8,128)(2,1)} %bitcast.47), calls=%async_computation | async-start | bytes 2097152 | tf_op jit(solution)/shard_map/all_to_all | solution.py:23
  35.7 40.8 %collective-permute-start.1 = (bf16[24,2048]{1,0:T(8,128)(2,1)S(1)}, bf16[24,2048]{1,0:T(8,128)(2,1)S(1)}, u32[]{:S(2)}, u32[]{:S(2)}) collective-permute-start(bf16[24,2048]{1,0:T(8,128)(2,1)S(1)} %bitcast.159), channel_id=1, source_target_pairs={{0,768},{256,0},{512,256},{768,512},{1,769},{257,1},{513,257},{769... | collective-permute-start | bytes 294920 | tf_op jit(solution)/shard_map/ppermute | solution.py:78
  54.5 24.1 %collective-permute-start.2 = (bf16[24,2048]{1,0:T(8,128)(2,1)S(1)}, bf16[24,2048]{1,0:T(8,128)(2,1)S(1)}, u32[]{:S(2)}, u32[]{:S(2)}) collective-permute-start(bf16[24,2048]{1,0:T(8,128)(2,1)S(1)} %bitcast.160), channel_id=1, source_target_pairs={{0,512},{256,768},{512,0},{768,256},{1,513},{257,769},{513,1},{769... | collective-permute-start | bytes 294920 | tf_op jit(solution)/shard_map/ppermute | solution.py:78
  63.0 20.5 %collective-permute-start.3 = (bf16[24,2048]{1,0:T(8,128)(2,1)S(1)}, bf16[24,2048]{1,0:T(8,128)(2,1)}, u32[]{:S(2)}, u32[]{:S(2)}) collective-permute-start(bf16[24,2048]{1,0:T(8,128)(2,1)S(1)} %bitcast.161), channel_id=1, source_target_pairs={{0,256},{256,512},{512,768},{768,0},{1,257},{257,513},{513,769},{7... | collective-permute-start | bytes 294920 | tf_op jit(solution)/shard_map/ppermute | solution.py:78
  76.5 46.6 %copy-start.3 = (bf16[384,256]{1,0:T(8,128)(2,1)}, bf16[384,256]{1,0:T(8,128)(2,1)S(1)}, u32[]{:S(2)}) copy-start(bf16[384,256]{1,0:T(8,128)(2,1)S(1)} %get-tuple-element.35) | copy-start | bytes 589828
  84.5 30.2 %copy-start.21 = (s32[64]{0:T(128)S(1)}, s32[64]{0:T(128)}, u32[]{:S(2)}) copy-start(s32[64]{0:T(128)} %copy-done.20) | copy-start | bytes 772
  84.5 30.2 %copy-start.23 = (s32[64]{0:T(128)S(1)}, s32[64]{0:T(128)}, u32[]{:S(2)}) copy-start(s32[64]{0:T(128)} %copy-done.22) | copy-start | bytes 772
  84.5 13.2 %collective-permute-start.4 = (bf16[96,2048]{1,0:T(8,128)(2,1)S(1)}, bf16[96,2048]{1,0:T(8,128)(2,1)S(1)}, u32[]{:S(2)}, u32[]{:S(2)}) collective-permute-start(bf16[96,2048]{1,0:T(8,128)(2,1)S(1)} %pad_maximum_fusion), channel_id=1, source_target_pairs={{0,192},{64,0},{128,64},{192,128},{1,193},{65,1},{129,65},{193,129... | collective-permute-start | bytes 1179656 | tf_op jit(solution)/shard_map/ppermute | solution.py:78
  89.1 12.9 %collective-permute-start.5 = (bf16[96,2048]{1,0:T(8,128)(2,1)S(1)}, bf16[96,2048]{1,0:T(8,128)(2,1)S(1)}, u32[]{:S(2)}, u32[]{:S(2)}) collective-permute-start(bf16[96,2048]{1,0:T(8,128)(2,1)S(1)} %pad_maximum_fusion), channel_id=1, source_target_pairs={{0,128},{64,192},{128,0},{192,64},{1,129},{65,193},{129,1},{193,65... | collective-permute-start | bytes 1179656 | tf_op jit(solution)/shard_map/ppermute | solution.py:78
  91.4 20.6 %collective-permute-start.6 = (bf16[96,2048]{1,0:T(8,128)(2,1)S(1)}, bf16[96,2048]{1,0:T(8,128)(2,1)S(1)}, u32[]{:S(2)}, u32[]{:S(2)}) collective-permute-start(bf16[96,2048]{1,0:T(8,128)(2,1)S(1)} %pad_maximum_fusion), channel_id=1, source_target_pairs={{0,64},{64,128},{128,192},{192,0},{1,65},{65,129},{129,193},{193,1... | collective-permute-start | bytes 1179656 | tf_op jit(solution)/shard_map/ppermute | solution.py:78
  112.0 11.1 %collective-permute-start.7 = (bf16[384,2048]{1,0:T(8,128)(2,1)S(1)}, bf16[384,2048]{1,0:T(8,128)(2,1)}, u32[]{:S(2)}, u32[]{:S(2)}) collective-permute-start(bf16[384,2048]{1,0:T(8,128)(2,1)S(1)} %constant_dynamic-update-slice_fusion), channel_id=1, source_target_pairs={{0,32},{32,0},{1,33},{33,1},{2,34},{34,2},{3,35},{35,3},{4,36},{36... | collective-permute-start | bytes 4718600 | tf_op jit(solution)/shard_map/ppermute | solution.py:157
  126.3 41.7 %all-to-all-start.1 = ((bf16[16,8,2048]{2,1,0:T(8,128)(2,1)}), bf16[16,8,2048]{2,1,0:T(8,128)(2,1)S(1)}, u32[]{:S(2)}, u32[]{:S(2)}) async-start(bf16[16,8,2048]{2,1,0:T(8,128)(2,1)} %fusion.2), calls=%async_computation.1 | async-start | bytes 1048576 | tf_op jit(solution)/shard_map/all_to_all | solution.py:23
  156.2 16.4 %collective-permute-start.8 = (bf16[384,2048]{1,0:T(8,128)(2,1)}, bf16[384,2048]{1,0:T(8,128)(2,1)}, u32[]{:S(2)}, u32[]{:S(2)}) collective-permute-start(bf16[384,2048]{1,0:T(8,128)(2,1)} %convolution_convert_fusion), channel_id=1, source_target_pairs={{0,32},{32,0},{1,33},{33,1},{2,34},{34,2},{3,35},{35,3},{4,36},{36... | collective-permute-start | bytes 4718600 | tf_op jit(solution)/shard_map/ppermute | solution.py:151
  168.0 72.4 %all-to-all-start.2 = ((bf16[16,8,2048]{2,1,0:T(8,128)(2,1)}), bf16[16,8,2048]{2,1,0:T(8,128)(2,1)S(1)}, u32[]{:S(2)}, u32[]{:S(2)}) async-start(bf16[16,8,2048]{2,1,0:T(8,128)(2,1)} %fusion.3), calls=%async_computation.2 | async-start | bytes 1048576 | tf_op jit(solution)/shard_map/all_to_all | solution.py:23
  177.3 12.2 %collective-permute-start.10 = (bf16[96,2048]{1,0:T(8,128)(2,1)}, bf16[96,2048]{1,0:T(8,128)(2,1)S(1)}, u32[]{:S(2)}, u32[]{:S(2)}) collective-permute-start(bf16[96,2048]{1,0:T(8,128)(2,1)} %get-tuple-element.100), channel_id=1, source_target_pairs={{0,64},{64,128},{128,192},{192,0},{1,65},{65,129},{129,193},{193,1... | collective-permute-start | bytes 1179656 | tf_op jit(solution)/shard_map/ppermute | solution.py:84
  179.2 12.0 %collective-permute-start.11 = (bf16[96,2048]{1,0:T(8,128)(2,1)}, bf16[96,2048]{1,0:T(8,128)(2,1)S(1)}, u32[]{:S(2)}, u32[]{:S(2)}) collective-permute-start(bf16[96,2048]{1,0:T(8,128)(2,1)} %get-tuple-element.99), channel_id=1, source_target_pairs={{0,192},{64,0},{128,64},{192,128},{1,193},{65,1},{129,65},{193,129... | collective-permute-start | bytes 1179656 | tf_op jit(solution)/shard_map/ppermute | solution.py:84
  183.8 13.4 %collective-permute-start.9 = (bf16[96,2048]{1,0:T(8,128)(2,1)S(1)}, bf16[96,2048]{1,0:T(8,128)(2,1)}, u32[]{:S(2)}, u32[]{:S(2)}) collective-permute-start(bf16[96,2048]{1,0:T(8,128)(2,1)S(1)} %get-tuple-element.98), channel_id=1, source_target_pairs={{0,128},{64,192},{128,0},{192,64},{1,129},{65,193},{129,1},{193,65... | collective-permute-start | bytes 1179656 | tf_op jit(solution)/shard_map/ppermute | solution.py:84
  197.1 27.2 %copy-start.1 = (bf16[128,2048]{1,0:T(8,128)(2,1)S(1)}, bf16[128,2048]{1,0:T(8,128)(2,1)}, u32[]{:S(2)}) copy-start(bf16[128,2048]{1,0:T(8,128)(2,1)} %get-tuple-element.39) | copy-start | bytes 1572868
  198.9 25.7 %copy-start.11 = (pred[128,32]{1,0:T(32,128)(4,1)S(1)}, pred[128,32]{1,0:T(32,128)(4,1)}, u32[]{:S(2)}) copy-start(pred[128,32]{1,0:T(32,128)(4,1)} %slice.251) | copy-start | bytes 12292
  198.9 25.7 %copy-start.12 = (pred[128,32]{1,0:T(32,128)(4,1)S(1)}, pred[128,32]{1,0:T(32,128)(4,1)}, u32[]{:S(2)}) copy-start(pred[128,32]{1,0:T(32,128)(4,1)} %slice.253) | copy-start | bytes 12292
  198.9 25.7 %copy-start.13 = (pred[128,32]{1,0:T(32,128)(4,1)S(1)}, pred[128,32]{1,0:T(32,128)(4,1)}, u32[]{:S(2)}) copy-start(pred[128,32]{1,0:T(32,128)(4,1)} %slice.255) | copy-start | bytes 12292
  198.9 25.7 %copy-start.14 = (pred[128,32]{1,0:T(32,128)(4,1)S(1)}, pred[128,32]{1,0:T(32,128)(4,1)}, u32[]{:S(2)}) copy-start(pred[128,32]{1,0:T(32,128)(4,1)} %slice.257) | copy-start | bytes 12292
  199.7 38.2 %collective-permute-start.13 = (bf16[24,2048]{1,0:T(8,128)(2,1)}, bf16[24,2048]{1,0:T(8,128)(2,1)S(1)}, u32[]{:S(2)}, u32[]{:S(2)}) collective-permute-start(bf16[24,2048]{1,0:T(8,128)(2,1)} %get-tuple-element.103), channel_id=1, source_target_pairs={{0,512},{256,768},{512,0},{768,256},{1,513},{257,769},{513,1},{769... | collective-permute-start | bytes 294920 | tf_op jit(solution)/shard_map/ppermute | solution.py:84
  210.3 27.6 %collective-permute-start.14 = (bf16[24,2048]{1,0:T(8,128)(2,1)}, bf16[24,2048]{1,0:T(8,128)(2,1)S(1)}, u32[]{:S(2)}, u32[]{:S(2)}) collective-permute-start(bf16[24,2048]{1,0:T(8,128)(2,1)} %get-tuple-element.105), channel_id=1, source_target_pairs={{0,256},{256,512},{512,768},{768,0},{1,257},{257,513},{513,769},{7... | collective-permute-start | bytes 294920 | tf_op jit(solution)/shard_map/ppermute | solution.py:84
  214.7 25.0 %collective-permute-start.15 = (bf16[24,2048]{1,0:T(8,128)(2,1)}, bf16[24,2048]{1,0:T(8,128)(2,1)S(1)}, u32[]{:S(2)}, u32[]{:S(2)}) collective-permute-start(bf16[24,2048]{1,0:T(8,128)(2,1)} %get-tuple-element.104), channel_id=1, source_target_pairs={{0,768},{256,0},{512,256},{768,512},{1,769},{257,1},{513,257},{769... | collective-permute-start | bytes 294920 | tf_op jit(solution)/shard_map/ppermute | solution.py:84
  224.6 15.8 %copy-start = (bf16[128,2048]{1,0:T(8,128)(2,1)S(1)}, bf16[128,2048]{1,0:T(8,128)(2,1)}, u32[]{:S(2)}) copy-start(bf16[128,2048]{1,0:T(8,128)(2,1)} %get-tuple-element.51) | copy-start | bytes 1572868
  225.8 14.8 %copy-start.8 = (pred[128,64]{1,0:T(32,128)(4,1)S(1)}, pred[128,64]{1,0:T(32,128)(4,1)}, u32[]{:S(2)}) copy-start(pred[128,64]{1,0:T(32,128)(4,1)} %get-tuple-element.125) | copy-start | bytes 24580
  226.8 37.9 %collective-permute-start.12 = (bf16[32,2176]{1,0:T(8,128)(2,1)S(1)}, bf16[32,2176]{1,0:T(8,128)(2,1)S(1)}, u32[]{:S(2)}, u32[]{:S(2)}) collective-permute-start(bf16[32,2176]{1,0:T(8,128)(2,1)S(1)} %fusion.25), channel_id=1, source_target_pairs={{0,16},{16,0},{1,17},{17,1},{2,18},{18,2},{3,19},{19,3},{4,20},{20... | collective-permute-start | bytes 417800 | tf_op jit(solution)/shard_map/ppermute | solution.py:172
  (11 other events, 59.9 us)

commit v7 on v5

--- a/solution.py
+++ b/solution.py
@@ -107,8 +107,17 @@
     columns = [ids.T.astype(BF16), *pieces_of(gates.T, 3)]
     sent_on = lax.ppermute(beside(cotangent, columns), HALF, SWAP)
 
-    wz = jnp.concatenate(gather(w_down.reshape(rows, width), ZH), axis=0)
-    wy = gather(wz, Y)
+    wz = gather(w_down.reshape(rows, width), ZH)
+
+    hid = hidden.reshape(N_HALF, groups, capacity, inner)
+    hid = jnp.where(half == 0, hid, hid[::-1]).transpose(1, 0, 2, 3).reshape(slots, inner)
+    hid_t = hid.T.reshape(RING, RING, N_CORE, rows, slots).transpose(2, 1, 0, 3, 4)
+    hid_t = turned(turned(hid_t, 2, zh), 1, y)
+    hid_t = hid_t.reshape(N_CORE, part, slots)
+    hid_self = lax.dynamic_index_in_dim(hid_t, core, 0, keepdims=False)
+    hid_other = lax.dynamic_index_in_dim(hid_t, 1 - core, 0, keepdims=False)
+    wz, hid_self, hid_other = lax.optimization_barrier((wz, hid_self, hid_other))
+    wy = gather(jnp.concatenate(wz, axis=0), Y)
 
     extra = sent_on[:, width : width + 4 * top].astype(F32).T
     ids_both = jnp.concatenate([ids.T, extra[:top].astype(jnp.int32)], axis=1)
@@ -122,24 +131,15 @@
     sent = (slot_gate * picked.astype(F32)).astype(BF16).reshape(groups, N_HALF * capacity, width)
     grads = exchange(sent, GRP).reshape(slots, width)
 
-    hid = hidden.reshape(N_HALF, groups, capacity, inner)
-    hid = jnp.where(half == 0, hid, hid[::-1]).transpose(1, 0, 2, 3).reshape(slots, inner)
-    hid_t = hid.T.reshape(RING, RING, N_CORE, rows, slots).transpose(2, 1, 0, 3, 4)
-    hid_t = turned(turned(hid_t, 2, zh), 1, y)
-    hid_t = hid_t.reshape(N_CORE, part, slots)
-    hid_self = lax.dynamic_index_in_dim(hid_t, core, 0, keepdims=False)
-    hid_other = lax.dynamic_index_in_dim(hid_t, 1 - core, 0, keepdims=False)
-    hid_self, hid_other = lax.optimization_barrier((hid_self, hid_other))
-
     for_other = dot(hid_other, grads, ((1,), (0,))).astype(BF16)
     got = lax.ppermute(for_other, CORE, SWAP)
     kept = dot(hid_self, grads, ((1,), (0,))) + got.astype(F32)
     by_y = total(scatter(kept.reshape(RING, RING * rows, width), Y))
     by_z = scatter(by_y.reshape(RING, rows, width), ZH)
 
-    wy, kept = lax.optimization_barrier((wy, kept))
     w_self = jnp.concatenate(wy, axis=0)
     w_other = lax.ppermute(w_self, CORE, SWAP)
+    w_other, _ = lax.optimization_barrier((w_other, for_other))
     out = dot(hid_self, w_self, ((0,), (0,))) + dot(hid_other, w_other, ((0,), (0,)))
     out = out.astype(BF16).reshape(groups, N_HALF * capacity, width)
     out, grads = lax.optimization_barrier((out, grads))

time: 266 us -> 260 us (0.977)
  matrix products: 9.35 us -> 17 us
  waiting for transfers between devices: 92.5 us -> 85.2 us
  starting transfers between devices: 143 us -> 137 us
    all_to_all x2, waiting for transfers between devices: 21.8 us -> 0.01 us  [exchange(): return lax.all_to_all(rows, axis, split_axis=0, concat_axis=0, tiled=True)]
    ppermute x6, starting transfers between devices: 44.4 us -> 35.6 us  [scatter(): lax.ppermute(blocks[step].astype(BF16), axis, forward(step))]
    ppermute x1, starting transfers between devices: 2.49 us -> 10.6 us  [per_device(): w_other = lax.ppermute(w_self, CORE, SWAP)]
    ppermute x1, waiting for transfers between devices: 9.81 us -> 17.6 us  [per_device(): passed = lax.ppermute(passed, HALF, SWAP)]
    dot_general x10, matrix products: 9.35 us -> 17 us  [dot(): return lax.dot_general(a, b, (dims, ((), ())), preferred_element_type=F32)]
    ppermute x6, waiting for transfers between devices: 23 us -> 29 us  [gather(): lax.ppermute(own, axis, forward(step))]
    all_to_all x2, starting transfers between devices: 28.2 us -> 23.7 us  [exchange(): return lax.all_to_all(rows, axis, split_axis=0, concat_axis=0, tiled=True)]
  transfers between devices with their start and end apart: 18 -> 18, of which waited for: 12 -> 13; matrix products, arithmetic and copies ran while one was open for 5% -> 9% of each run, Pallas kernels for 0% -> 0%
where the time goes in v7:
time: 260 us; the launch traced here: 259 us
  starting transfers between devices  137 us (53%)
  waiting for transfers between devices  85.2 us (33%)
  matrix products  17 us (7%)
  other arithmetic  10.1 us (4%)
  local copies, waits for them, and re-layouts  8.55 us (3%)
    ppermute x6, starting transfers between devices, gather(): lax.ppermute(own, axis, forward(step))  48 us
    ppermute x6, starting transfers between devices, scatter(): lax.ppermute(blocks[step].astype(BF16), axis, forward(step))  35.6 us
    ppermute x6, waiting for transfers between devices, gather(): lax.ppermute(own, axis, forward(step))  29 us
    ppermute x6, waiting for transfers between devices, scatter(): lax.ppermute(blocks[step].astype(BF16), axis, forward(step))  25.7 us
    all_to_all x2, starting transfers between devices, exchange(): return lax.all_to_all(rows, axis, split_axis=0, concat_axis=0, tiled=True)  23.7 us
    ppermute x1, waiting for transfers between devices, per_device(): passed = lax.ppermute(passed, HALF, SWAP)  17.6 us
    dot_general x10, matrix products, dot(): return lax.dot_general(a, b, (dims, ((), ())), preferred_element_type=F32)  17 us
    ppermute x1, waiting for transfers between devices, per_device(): sent_on = lax.ppermute(beside(cotangent, columns), HALF, SWAP)  11.3 us
  transfers between devices with their start and end apart: 18, of which 13 were waited for; matrix products, arithmetic and copies ran while one was open for 9% of the time, Pallas kernels for 0%

profile of v7, /device:TPU:1, one launch (start us, length us, event | category | flops | bytes accessed | tf_op | source)
XLA Modules:
  0.0 259.1 jit_solution(12255352801039065407)
XLA Ops:
  3.1 9.6 %collective-permute-start = (bf16[32,2176]{1,0:T(8,128)(2,1)S(1)}, bf16[32,2176]{1,0:T(8,128)(2,1)S(1)}, u32[]{:S(2)}, u32[]{:S(2)}) collective-permute-start(bf16[32,2176]{1,0:T(8,128)(2,1)S(1)} %fusion.19), channel_id=1, source_target_pairs={{0,16},{16,0},{1,17},{17,1},{2,18},{18,2},{3,19},{19,3},{4,20},{20... | collective-permute-start | bytes 417800 | tf_op jit(solution)/shard_map/ppermute | solution.py:108
  12.8 11.3 %collective-permute-done = bf16[32,2176]{1,0:T(8,128)(2,1)S(1)} collective-permute-done((bf16[32,2176]{1,0:T(8,128)(2,1)S(1)}, bf16[32,2176]{1,0:T(8,128)(2,1)S(1)}, u32[]{:S(2)}, u32[]{:S(2)}) %collective-permute-start) | collective-permute-done | bytes 139296 | tf_op jit(solution)/shard_map/ppermute | solution.py:108
  27.8 7.9 %all-to-all-start = ((bf16[16,16,2048]{2,1,0:T(8,128)(2,1)}), bf16[16,16,2048]{2,1,0:T(8,128)(2,1)S(1)}, u32[]{:S(2)}, u32[]{:S(2)}) async-start(bf16[16,16,2048]{2,1,0:T(8,128)(2,1)} %bitcast.22), calls=%async_computation | async-start | bytes 2097152 | tf_op jit(solution)/shard_map/all_to_all | solution.py:23
  35.7 15.4 %collective-permute-start.3 = (bf16[24,2048]{1,0:T(8,128)(2,1)S(1)}, bf16[24,2048]{1,0:T(8,128)(2,1)S(1)}, u32[]{:S(2)}, u32[]{:S(2)}) collective-permute-start(bf16[24,2048]{1,0:T(8,128)(2,1)S(1)} %bitcast.98), channel_id=1, source_target_pairs={{0,256},{256,512},{512,768},{768,0},{1,257},{257,513},{513,769},{7... | collective-permute-start | bytes 294920 | tf_op jit(solution)/shard_map/ppermute | solution.py:78
  51.2 15.1 %collective-permute-start.2 = (bf16[24,2048]{1,0:T(8,128)(2,1)S(1)}, bf16[24,2048]{1,0:T(8,128)(2,1)S(1)}, u32[]{:S(2)}, u32[]{:S(2)}) collective-permute-start(bf16[24,2048]{1,0:T(8,128)(2,1)S(1)} %bitcast.99), channel_id=1, source_target_pairs={{0,512},{256,768},{512,0},{768,256},{1,513},{257,769},{513,1},{769... | collective-permute-start | bytes 294920 | tf_op jit(solution)/shard_map/ppermute | solution.py:78
  66.3 8.2 %collective-permute-start.1 = (bf16[24,2048]{1,0:T(8,128)(2,1)S(1)}, bf16[24,2048]{1,0:T(8,128)(2,1)S(1)}, u32[]{:S(2)}, u32[]{:S(2)}) collective-permute-start(bf16[24,2048]{1,0:T(8,128)(2,1)S(1)} %bitcast.100), channel_id=1, source_target_pairs={{0,768},{256,0},{512,256},{768,512},{1,769},{257,1},{513,257},{769... | collective-permute-start | bytes 294920 | tf_op jit(solution)/shard_map/ppermute | solution.py:78
  75.2 13.2 %collective-permute-done.3 = bf16[24,2048]{1,0:T(8,128)(2,1)S(1)} collective-permute-done((bf16[24,2048]{1,0:T(8,128)(2,1)S(1)}, bf16[24,2048]{1,0:T(8,128)(2,1)S(1)}, u32[]{:S(2)}, u32[]{:S(2)}) %collective-permute-start.3) | collective-permute-done | bytes 98336 | tf_op jit(solution)/shard_map/ppermute | solution.py:78
  88.4 7.6 %collective-permute-done.2 = bf16[24,2048]{1,0:T(8,128)(2,1)S(1)} collective-permute-done((bf16[24,2048]{1,0:T(8,128)(2,1)S(1)}, bf16[24,2048]{1,0:T(8,128)(2,1)S(1)}, u32[]{:S(2)}, u32[]{:S(2)}) %collective-permute-start.2) | collective-permute-done | bytes 98336 | tf_op jit(solution)/shard_map/ppermute | solution.py:78
  98.6 4.4 %collective-permute-start.4 = (bf16[96,2048]{1,0:T(8,128)(2,1)S(1)}, bf16[96,2048]{1,0:T(8,128)(2,1)S(1)}, u32[]{:S(2)}, u32[]{:S(2)}) collective-permute-start(bf16[96,2048]{1,0:T(8,128)(2,1)S(1)} %get-tuple-element.66), channel_id=1, source_target_pairs={{0,192},{64,0},{128,64},{192,128},{1,193},{65,1},{129,65},{193,129... | collective-permute-start | bytes 1179656 | tf_op jit(solution)/shard_map/ppermute | solution.py:78
  103.0 2.4 collective-permute-start.5
  105.4 2.4 collective-permute-start.6
  107.9 4.3 %collective-permute-done.4 = bf16[96,2048]{1,0:T(8,128)(2,1)S(1)} collective-permute-done((bf16[96,2048]{1,0:T(8,128)(2,1)S(1)}, bf16[96,2048]{1,0:T(8,128)(2,1)S(1)}, u32[]{:S(2)}, u32[]{:S(2)}) %collective-permute-start.4) | collective-permute-done | bytes 393248 | tf_op jit(solution)/shard_map/ppermute | solution.py:78
  113.9 3.7 %collective-permute-done.6 = bf16[96,2048]{1,0:T(8,128)(2,1)S(1)} collective-permute-done((bf16[96,2048]{1,0:T(8,128)(2,1)S(1)}, bf16[96,2048]{1,0:T(8,128)(2,1)S(1)}, u32[]{:S(2)}, u32[]{:S(2)}) %collective-permute-start.6) | collective-permute-done | bytes 393248 | tf_op jit(solution)/shard_map/ppermute | solution.py:78
  118.4 10.6 %collective-permute-start.7 = (bf16[384,2048]{1,0:T(8,128)(2,1)}, bf16[384,2048]{1,0:T(8,128)(2,1)}, u32[]{:S(2)}, u32[]{:S(2)}) collective-permute-start(bf16[384,2048]{1,0:T(8,128)(2,1)} %constant_dynamic-update-slice_fusion.4), channel_id=1, source_target_pairs={{0,32},{32,0},{1,33},{33,1},{2,34},{34,2},{3,35},{35,3},{4,36},{36... | collective-permute-start | bytes 4718600 | tf_op jit(solution)/shard_map/ppermute | solution.py:141
  132.4 2.1 fusion.61
  134.6 3.1 %fusion = bf16[256,2048]{1,0:T(8,128)(2,1)} fusion(f32[256,2048]{1,0:T(8,128)S(1)} %fusion.61, bf16[384,256]{1,0:T(8,128)(2,1)S(1)} %get-tuple-element.15, bf16[384,2048]{1,0:T(8,128)(2,1)} %constant_dynamic-update-slice_fusion.4), kind=kOutput, calls=%fused_computation.5 | convolution fusion | flops 403701760 | bytes 4915200 | tf_op jit(solution)/shard_map/dot_general | solution.py:19
  137.7 15.8 %all-to-all-start.1 = ((bf16[16,16,2048]{2,1,0:T(8,128)(2,1)}), bf16[16,16,2048]{2,1,0:T(8,128)(2,1)S(1)}, u32[]{:S(2)}, u32[]{:S(2)}) async-start(bf16[16,16,2048]{2,1,0:T(8,128)(2,1)} %bitcast.24), calls=%async_computation.1 | async-start | bytes 2097152 | tf_op jit(solution)/shard_map/all_to_all | solution.py:23
  153.5 2.6 collective-permute-start.8
  160.2 3.6 %fusion.60 = (bf16[384,2048]{1,0:T(8,128)(2,1)S(1)}, f32[384,2048]{1,0:T(8,128)}) fusion(bf16[384,2048]{1,0:T(8,128)(2,1)} %collective-permute-done.8, bf16[384,256]{1,0:T(8,128)(2,1)S(1)} %get-tuple-element.15, bf16[256,2048]{1,0:T(8,128)(2,1)S(1)} %bitcast.87), kind=kOutput, calls=%fused_computation.155 | convolution fusion | flops 405012480 | bytes 7536640 | tf_op jit(solution)/shard_map/dot_general | solution.py:19
  164.8 2.3 collective-permute-start.9
  167.1 2.8 %collective-permute-start.11 = (bf16[96,2048]{1,0:T(8,128)(2,1)}, bf16[96,2048]{1,0:T(8,128)(2,1)}, u32[]{:S(2)}, u32[]{:S(2)}) collective-permute-start(bf16[96,2048]{1,0:T(8,128)(2,1)} %get-tuple-element.57), channel_id=1, source_target_pairs={{0,192},{64,0},{128,64},{192,128},{1,193},{65,1},{129,65},{193,129... | collective-permute-start | bytes 1179656 | tf_op jit(solution)/shard_map/ppermute | solution.py:84
  170.0 2.4 collective-permute-start.10
  173.9 5.3 %collective-permute-done.9 = bf16[96,2048]{1,0:T(8,128)(2,1)S(1)} collective-permute-done((bf16[96,2048]{1,0:T(8,128)(2,1)}, bf16[96,2048]{1,0:T(8,128)(2,1)S(1)}, u32[]{:S(2)}, u32[]{:S(2)}) %collective-permute-start.9) | collective-permute-done | bytes 393248 | tf_op jit(solution)/shard_map/ppermute | solution.py:84
  179.2 6.5 %collective-permute-done.11 = bf16[96,2048]{1,0:T(8,128)(2,1)} collective-permute-done((bf16[96,2048]{1,0:T(8,128)(2,1)}, bf16[96,2048]{1,0:T(8,128)(2,1)}, u32[]{:S(2)}, u32[]{:S(2)}) %collective-permute-start.11) | collective-permute-done | bytes 393248 | tf_op jit(solution)/shard_map/ppermute | solution.py:84
  185.6 2.4 collective-permute-done.10
  190.3 14.0 %collective-permute-start.13 = (bf16[24,2048]{1,0:T(8,128)(2,1)}, bf16[24,2048]{1,0:T(8,128)(2,1)S(1)}, u32[]{:S(2)}, u32[]{:S(2)}) collective-permute-start(bf16[24,2048]{1,0:T(8,128)(2,1)} %get-tuple-element.59), channel_id=1, source_target_pairs={{0,512},{256,768},{512,0},{768,256},{1,513},{257,769},{513,1},{769... | collective-permute-start | bytes 294920 | tf_op jit(solution)/shard_map/ppermute | solution.py:84
  204.4 8.0 %collective-permute-start.15 = (bf16[24,2048]{1,0:T(8,128)(2,1)S(1)}, bf16[24,2048]{1,0:T(8,128)(2,1)S(1)}, u32[]{:S(2)}, u32[]{:S(2)}) collective-permute-start(bf16[24,2048]{1,0:T(8,128)(2,1)S(1)} %get-tuple-element.60), channel_id=1, source_target_pairs={{0,768},{256,0},{512,256},{768,512},{1,769},{257,1},{513,257},{769... | collective-permute-start | bytes 294920 | tf_op jit(solution)/shard_map/ppermute | solution.py:84
  212.4 6.0 %collective-permute-start.14 = (bf16[24,2048]{1,0:T(8,128)(2,1)S(1)}, bf16[24,2048]{1,0:T(8,128)(2,1)}, u32[]{:S(2)}, u32[]{:S(2)}) collective-permute-start(bf16[24,2048]{1,0:T(8,128)(2,1)S(1)} %get-tuple-element.61), channel_id=1, source_target_pairs={{0,256},{256,512},{512,768},{768,0},{1,257},{257,513},{513,769},{7... | collective-permute-start | bytes 294920 | tf_op jit(solution)/shard_map/ppermute | solution.py:84
  219.9 6.9 %collective-permute-start.12 = (bf16[32,2176]{1,0:T(8,128)(2,1)S(1)}, bf16[32,2176]{1,0:T(8,128)(2,1)S(1)}, u32[]{:S(2)}, u32[]{:S(2)}) collective-permute-start(bf16[32,2176]{1,0:T(8,128)(2,1)S(1)} %fusion.20), channel_id=1, source_target_pairs={{0,16},{16,0},{1,17},{17,1},{2,18},{18,2},{3,19},{19,3},{4,20},{20... | collective-permute-start | bytes 417800 | tf_op jit(solution)/shard_map/ppermute | solution.py:150
  226.8 4.8 %collective-permute-done.15 = bf16[24,2048]{1,0:T(8,128)(2,1)S(1)} collective-permute-done((bf16[24,2048]{1,0:T(8,128)(2,1)S(1)}, bf16[24,2048]{1,0:T(8,128)(2,1)S(1)}, u32[]{:S(2)}, u32[]{:S(2)}) %collective-permute-start.15) | collective-permute-done | bytes 98336 | tf_op jit(solution)/shard_map/ppermute | solution.py:84
  231.7 6.8 %collective-permute-done.14 = bf16[24,2048]{1,0:T(8,128)(2,1)} collective-permute-done((bf16[24,2048]{1,0:T(8,128)(2,1)S(1)}, bf16[24,2048]{1,0:T(8,128)(2,1)}, u32[]{:S(2)}, u32[]{:S(2)}) %collective-permute-start.14) | collective-permute-done | bytes 98336 | tf_op jit(solution)/shard_map/ppermute | solution.py:84
  240.1 17.6 %collective-permute-done.12 = bf16[32,2176]{1,0:T(8,128)(2,1)S(1)} collective-permute-done((bf16[32,2176]{1,0:T(8,128)(2,1)S(1)}, bf16[32,2176]{1,0:T(8,128)(2,1)S(1)}, u32[]{:S(2)}, u32[]{:S(2)}) %collective-permute-start.12) | collective-permute-done | bytes 139296 | tf_op jit(solution)/shard_map/ppermute | solution.py:150
  (107 shorter events, 28.6 us)
Async XLA Ops:
  0.6 25.7 %copy-start = (bf16[32,2048]{1,0:T(8,128)(2,1)S(1)}, bf16[32,2048]{1,0:T(8,128)(2,1)}, u32[]{:S(2)}) copy-start(bf16[32,2048]{1,0:T(8,128)(2,1)} %param.9) | copy-start | bytes 393220
  3.1 21.0 %collective-permute-start = (bf16[32,2176]{1,0:T(8,128)(2,1)S(1)}, bf16[32,2176]{1,0:T(8,128)(2,1)S(1)}, u32[]{:S(2)}, u32[]{:S(2)}) collective-permute-start(bf16[32,2176]{1,0:T(8,128)(2,1)S(1)} %fusion.19), channel_id=1, source_target_pairs={{0,16},{16,0},{1,17},{17,1},{2,18},{18,2},{3,19},{19,3},{4,20},{20... | collective-permute-start | bytes 417800 | tf_op jit(solution)/shard_map/ppermute | solution.py:108
  12.7 13.3 %copy-start.15 = (s32[256]{0:T(256)}, s32[256]{0:T(256)S(1)}, u32[]{:S(2)}) copy-start(s32[256]{0:T(256)S(1)} %fusion.49) | copy-start | bytes 3076
  12.8 13.3 %copy-start.17 = (s32[64]{0:T(128)}, s32[64]{0:T(128)S(1)}, u32[]{:S(2)}) copy-start(s32[64]{0:T(128)S(1)} %and_select_fusion.1) | copy-start | bytes 772
  12.8 13.3 %copy-start.5 = (s32[256]{0:T(256)}, s32[256]{0:T(256)S(1)}, u32[]{:S(2)}) copy-start(s32[256]{0:T(256)S(1)} %get-tuple-element.96) | copy-start | bytes 3076
  27.8 7.9 %copy-start.2 = (bf16[1,24,2048]{2,1,0:T(8,128)(2,1)S(1)}, bf16[1,24,2048]{2,1,0:T(8,128)(2,1)}, u32[]{:S(2)}) copy-start(bf16[1,24,2048]{2,1,0:T(8,128)(2,1)} %param.6) | copy-start | bytes 294916
  27.8 46.7 %copy-start.1 = (bf16[256,768]{1,0:T(8,128)(2,1)S(1)}, bf16[256,768]{1,0:T(8,128)(2,1)}, u32[]{:S(2)}) copy-start(bf16[256,768]{1,0:T(8,128)(2,1)} %param.5) | copy-start | bytes 1179652
  27.8 101.3 %all-to-all-start = ((bf16[16,16,2048]{2,1,0:T(8,128)(2,1)}), bf16[16,16,2048]{2,1,0:T(8,128)(2,1)S(1)}, u32[]{:S(2)}, u32[]{:S(2)}) async-start(bf16[16,16,2048]{2,1,0:T(8,128)(2,1)} %bitcast.22), calls=%async_computation | async-start | bytes 2097152 | tf_op jit(solution)/shard_map/all_to_all | solution.py:23
  35.7 52.6 %collective-permute-start.3 = (bf16[24,2048]{1,0:T(8,128)(2,1)S(1)}, bf16[24,2048]{1,0:T(8,128)(2,1)S(1)}, u32[]{:S(2)}, u32[]{:S(2)}) collective-permute-start(bf16[24,2048]{1,0:T(8,128)(2,1)S(1)} %bitcast.98), channel_id=1, source_target_pairs={{0,256},{256,512},{512,768},{768,0},{1,257},{257,513},{513,769},{7... | collective-permute-start | bytes 294920 | tf_op jit(solution)/shard_map/ppermute | solution.py:78
  51.2 44.8 %collective-permute-start.2 = (bf16[24,2048]{1,0:T(8,128)(2,1)S(1)}, bf16[24,2048]{1,0:T(8,128)(2,1)S(1)}, u32[]{:S(2)}, u32[]{:S(2)}) collective-permute-start(bf16[24,2048]{1,0:T(8,128)(2,1)S(1)} %bitcast.99), channel_id=1, source_target_pairs={{0,512},{256,768},{512,0},{768,256},{1,513},{257,769},{513,1},{769... | collective-permute-start | bytes 294920 | tf_op jit(solution)/shard_map/ppermute | solution.py:78
  66.3 29.6 %collective-permute-start.1 = (bf16[24,2048]{1,0:T(8,128)(2,1)S(1)}, bf16[24,2048]{1,0:T(8,128)(2,1)S(1)}, u32[]{:S(2)}, u32[]{:S(2)}) collective-permute-start(bf16[24,2048]{1,0:T(8,128)(2,1)S(1)} %bitcast.100), channel_id=1, source_target_pairs={{0,768},{256,0},{512,256},{768,512},{1,769},{257,1},{513,257},{769... | collective-permute-start | bytes 294920 | tf_op jit(solution)/shard_map/ppermute | solution.py:78
  98.6 13.6 %collective-permute-start.4 = (bf16[96,2048]{1,0:T(8,128)(2,1)S(1)}, bf16[96,2048]{1,0:T(8,128)(2,1)S(1)}, u32[]{:S(2)}, u32[]{:S(2)}) collective-permute-start(bf16[96,2048]{1,0:T(8,128)(2,1)S(1)} %get-tuple-element.66), channel_id=1, source_target_pairs={{0,192},{64,0},{128,64},{192,128},{1,193},{65,1},{129,65},{193,129... | collective-permute-start | bytes 1179656 | tf_op jit(solution)/shard_map/ppermute | solution.py:78
  103.0 10.1 %collective-permute-start.5 = (bf16[96,2048]{1,0:T(8,128)(2,1)S(1)}, bf16[96,2048]{1,0:T(8,128)(2,1)S(1)}, u32[]{:S(2)}, u32[]{:S(2)}) collective-permute-start(bf16[96,2048]{1,0:T(8,128)(2,1)S(1)} %get-tuple-element.66), channel_id=1, source_target_pairs={{0,128},{64,192},{128,0},{192,64},{1,129},{65,193},{129,1},{193,65... | collective-permute-start | bytes 1179656 | tf_op jit(solution)/shard_map/ppermute | solution.py:78
  105.4 12.2 %collective-permute-start.6 = (bf16[96,2048]{1,0:T(8,128)(2,1)S(1)}, bf16[96,2048]{1,0:T(8,128)(2,1)S(1)}, u32[]{:S(2)}, u32[]{:S(2)}) collective-permute-start(bf16[96,2048]{1,0:T(8,128)(2,1)S(1)} %get-tuple-element.66), channel_id=1, source_target_pairs={{0,64},{64,128},{128,192},{192,0},{1,65},{65,129},{129,193},{193,1... | collective-permute-start | bytes 1179656 | tf_op jit(solution)/shard_map/ppermute | solution.py:78
  118.4 14.0 %collective-permute-start.7 = (bf16[384,2048]{1,0:T(8,128)(2,1)}, bf16[384,2048]{1,0:T(8,128)(2,1)}, u32[]{:S(2)}, u32[]{:S(2)}) collective-permute-start(bf16[384,2048]{1,0:T(8,128)(2,1)} %constant_dynamic-update-slice_fusion.4), channel_id=1, source_target_pairs={{0,32},{32,0},{1,33},{33,1},{2,34},{34,2},{3,35},{35,3},{4,36},{36... | collective-permute-start | bytes 4718600 | tf_op jit(solution)/shard_map/ppermute | solution.py:141
  137.7 80.7 %all-to-all-start.1 = ((bf16[16,16,2048]{2,1,0:T(8,128)(2,1)}), bf16[16,16,2048]{2,1,0:T(8,128)(2,1)S(1)}, u32[]{:S(2)}, u32[]{:S(2)}) async-start(bf16[16,16,2048]{2,1,0:T(8,128)(2,1)} %bitcast.24), calls=%async_computation.1 | async-start | bytes 2097152 | tf_op jit(solution)/shard_map/all_to_all | solution.py:23
  153.5 6.7 %collective-permute-start.8 = (bf16[384,2048]{1,0:T(8,128)(2,1)}, bf16[384,2048]{1,0:T(8,128)(2,1)}, u32[]{:S(2)}, u32[]{:S(2)}) collective-permute-start(bf16[384,2048]{1,0:T(8,128)(2,1)} %convolution_convert_fusion), channel_id=1, source_target_pairs={{0,32},{32,0},{1,33},{33,1},{2,34},{34,2},{3,35},{35,3},{4,36},{36... | collective-permute-start | bytes 4718600 | tf_op jit(solution)/shard_map/ppermute | solution.py:135
  164.8 14.3 %collective-permute-start.9 = (bf16[96,2048]{1,0:T(8,128)(2,1)}, bf16[96,2048]{1,0:T(8,128)(2,1)S(1)}, u32[]{:S(2)}, u32[]{:S(2)}) collective-permute-start(bf16[96,2048]{1,0:T(8,128)(2,1)} %get-tuple-element.56), channel_id=1, source_target_pairs={{0,128},{64,192},{128,0},{192,64},{1,129},{65,193},{129,1},{193,65... | collective-permute-start | bytes 1179656 | tf_op jit(solution)/shard_map/ppermute | solution.py:84
  167.1 18.5 %collective-permute-start.11 = (bf16[96,2048]{1,0:T(8,128)(2,1)}, bf16[96,2048]{1,0:T(8,128)(2,1)}, u32[]{:S(2)}, u32[]{:S(2)}) collective-permute-start(bf16[96,2048]{1,0:T(8,128)(2,1)} %get-tuple-element.57), channel_id=1, source_target_pairs={{0,192},{64,0},{128,64},{192,128},{1,193},{65,1},{129,65},{193,129... | collective-permute-start | bytes 1179656 | tf_op jit(solution)/shard_map/ppermute | solution.py:84
  170.0 18.1 %collective-permute-start.10 = (bf16[96,2048]{1,0:T(8,128)(2,1)}, bf16[96,2048]{1,0:T(8,128)(2,1)}, u32[]{:S(2)}, u32[]{:S(2)}) collective-permute-start(bf16[96,2048]{1,0:T(8,128)(2,1)} %get-tuple-element.58), channel_id=1, source_target_pairs={{0,64},{64,128},{128,192},{192,0},{1,65},{65,129},{129,193},{193,1... | collective-permute-start | bytes 1179656 | tf_op jit(solution)/shard_map/ppermute | solution.py:84
  189.6 29.2 %copy-start.6 = (s32[256]{0:T(256)S(1)}, s32[256]{0:T(256)}, u32[]{:S(2)}) copy-start(s32[256]{0:T(256)} %copy-done.5) | copy-start | bytes 3076
  189.6 29.2 %copy-start.8 = (s32[64]{0:T(128)S(1)}, s32[64]{0:T(128)}, u32[]{:S(2)}) copy-start(s32[64]{0:T(128)} %copy-done.7) | copy-start | bytes 772
  189.6 29.2 %copy-start.10 = (s32[64]{0:T(128)S(1)}, s32[64]{0:T(128)}, u32[]{:S(2)}) copy-start(s32[64]{0:T(128)} %copy-done.9) | copy-start | bytes 772
  189.6 29.2 %copy-start.12 = (s32[64]{0:T(128)S(1)}, s32[64]{0:T(128)}, u32[]{:S(2)}) copy-start(s32[64]{0:T(128)} %copy-done.11) | copy-start | bytes 772
  189.6 29.2 %copy-start.14 = (s32[64]{0:T(128)S(1)}, s32[64]{0:T(128)}, u32[]{:S(2)}) copy-start(s32[64]{0:T(128)} %copy-done.13) | copy-start | bytes 772
  189.6 29.2 %copy-start.16 = (s32[256]{0:T(256)S(1)}, s32[256]{0:T(256)}, u32[]{:S(2)}) copy-start(s32[256]{0:T(256)} %copy-done.15) | copy-start | bytes 3076
  189.6 29.2 %copy-start.18 = (s32[64]{0:T(128)S(1)}, s32[64]{0:T(128)}, u32[]{:S(2)}) copy-start(s32[64]{0:T(128)} %copy-done.17) | copy-start | bytes 772
  189.7 29.6 %copy-start.4 = (f32[256]{0:T(256)S(1)}, f32[256]{0:T(256)}, u32[]{:S(2)}) copy-start(f32[256]{0:T(256)} %copy-done.3) | copy-start | bytes 3076
  190.3 36.5 %collective-permute-start.13 = (bf16[24,2048]{1,0:T(8,128)(2,1)}, bf16[24,2048]{1,0:T(8,128)(2,1)S(1)}, u32[]{:S(2)}, u32[]{:S(2)}) collective-permute-start(bf16[24,2048]{1,0:T(8,128)(2,1)} %get-tuple-element.59), channel_id=1, source_target_pairs={{0,512},{256,768},{512,0},{768,256},{1,513},{257,769},{513,1},{769... | collective-permute-start | bytes 294920 | tf_op jit(solution)/shard_map/ppermute | solution.py:84
  204.4 27.3 %collective-permute-start.15 = (bf16[24,2048]{1,0:T(8,128)(2,1)S(1)}, bf16[24,2048]{1,0:T(8,128)(2,1)S(1)}, u32[]{:S(2)}, u32[]{:S(2)}) collective-permute-start(bf16[24,2048]{1,0:T(8,128)(2,1)S(1)} %get-tuple-element.60), channel_id=1, source_target_pairs={{0,768},{256,0},{512,256},{768,512},{1,769},{257,1},{513,257},{769... | collective-permute-start | bytes 294920 | tf_op jit(solution)/shard_map/ppermute | solution.py:84
  212.4 26.1 %collective-permute-start.14 = (bf16[24,2048]{1,0:T(8,128)(2,1)S(1)}, bf16[24,2048]{1,0:T(8,128)(2,1)}, u32[]{:S(2)}, u32[]{:S(2)}) collective-permute-start(bf16[24,2048]{1,0:T(8,128)(2,1)S(1)} %get-tuple-element.61), channel_id=1, source_target_pairs={{0,256},{256,512},{512,768},{768,0},{1,257},{257,513},{513,769},{7... | collective-permute-start | bytes 294920 | tf_op jit(solution)/shard_map/ppermute | solution.py:84
  219.9 37.7 %collective-permute-start.12 = (bf16[32,2176]{1,0:T(8,128)(2,1)S(1)}, bf16[32,2176]{1,0:T(8,128)(2,1)S(1)}, u32[]{:S(2)}, u32[]{:S(2)}) collective-permute-start(bf16[32,2176]{1,0:T(8,128)(2,1)S(1)} %fusion.20), channel_id=1, source_target_pairs={{0,16},{16,0},{1,17},{17,1},{2,18},{18,2},{3,19},{19,3},{4,20},{20... | collective-permute-start | bytes 417800 | tf_op jit(solution)/shard_map/ppermute | solution.py:150
  (5 other events, 4.1 us)
